TPU v7x, 16 devices: a whole 2x2x2 slice. The times are simulated.
16 devices in a mesh: dp: 2 (over z), cp: 8 (over y, x, core).
Axes of the slice: x: 2, y: 2, z: 2, core: 2. Of those that a mesh axis runs over, the one named last changes fastest.
Arguments:
- x_in: bfloat16 [8, 1024, 3072], P('dp', 'cp'), parts along dimension 0
- dy_in: bfloat16 [8, 1024, 3072], P('dp', 'cp'), parts along dimension 0
- norm_gain: bfloat16 [3072], replicated
- w_q: bfloat16 [3072, 24, 128], replicated
- w_k: bfloat16 [3072, 8, 128], replicated
- w_v: bfloat16 [3072, 8, 128], replicated
- w_o: bfloat16 [24, 128, 3072], replicated
Outputs:
- output 1: bfloat16 [8, 1024, 3072], P('dp', 'cp'), parts along dimension 0
- output 2: bfloat16 [8, 1024, 3072], P('dp', 'cp'), parts along dimension 0
- output 3: float32 [6144], P('dp'), parts along dimension 0
- output 4: float32 [6144, 24, 128], P('dp'), parts along dimension 0
- output 5: float32 [6144, 8, 128], P('dp'), parts along dimension 0
- output 6: float32 [6144, 8, 128], P('dp'), parts along dimension 0
- output 7: float32 [48, 128, 3072], P('dp'), parts along dimension 0
There are 2 independent parts. A program takes and returns all parts, laid end to end along the dimension named above; an argument that names none is the same for every part.
All inputs are finite; a program needn't handle non-finite values.
Results may differ from a plain program's by a relative error of at most 0.00981.
Values are sent between devices in bfloat16 or wider.
A program may use at most 1 GiB of HBM per device.

v0:
```python
import jax
import jax.numpy as jnp
from jax import lax
from jax.sharding import PartitionSpec as P

EPS = 1e-6


def attend_pair(queries, key_blk, val_blk, soft_stats, visible):
    run_max, run_sum, run_acc = soft_stats
    score_scale = queries.shape[-1] ** -0.5
    scores = jnp.einsum('bqkgd,bskd->bkgqs', queries, key_blk, preferred_element_type=jnp.float32) * score_scale
    if visible is not None:
        scores = jnp.where(visible, scores, -jnp.inf)
    new_max = jnp.maximum(run_max, jnp.max(scores, axis=-1))
    correction = jnp.exp(run_max - new_max)
    probs_raw = jnp.exp(scores - new_max[..., None])
    run_sum = run_sum * correction + jnp.sum(probs_raw, axis=-1)
    run_acc = run_acc * correction[..., None] + jnp.einsum('bkgqs,bskd->bkgqd', probs_raw.astype(jnp.bfloat16), val_blk, preferred_element_type=jnp.float32)
    return new_max, run_sum, run_acc


def grad_pair(queries, key_blk, val_blk, d_attn, delta_row, log_norm, visible):
    score_scale = queries.shape[-1] ** -0.5
    scores = jnp.einsum('bqkgd,bskd->bkgqs', queries, key_blk, preferred_element_type=jnp.float32) * score_scale
    probs_norm = jnp.exp(scores - log_norm[..., None])
    if visible is not None:
        probs_norm = jnp.where(visible, probs_norm, 0.0)
    d_val = jnp.einsum('bkgqs,bkgqd->bskd', probs_norm.astype(jnp.bfloat16), d_attn, preferred_element_type=jnp.float32)
    d_probs = jnp.einsum('bkgqd,bskd->bkgqs', d_attn, val_blk, preferred_element_type=jnp.float32)
    d_scores = (probs_norm * (d_probs - delta_row[..., None]) * score_scale).astype(jnp.bfloat16)
    d_query = jnp.einsum('bkgqs,bskd->bqkgd', d_scores, key_blk, preferred_element_type=jnp.float32)
    d_key = jnp.einsum('bkgqs,bqkgd->bskd', d_scores, queries, preferred_element_type=jnp.float32)
    return d_query, d_key, d_val


def solution(mesh):
    n_dev = mesh.shape['cp']
    shift_perm = [(src_dev, (src_dev + 1) % n_dev) for src_dev in range(n_dev)]

    def device_fn(x_in, dy_in, norm_gain, w_q, w_k, w_v, w_o):
        my_idx = lax.axis_index('cp')
        n_batch, seq_len, model_dim = x_in.shape
        n_heads, head_dim = w_q.shape[1], w_q.shape[2]
        kv_heads = w_k.shape[1]
        n_group = n_heads // kv_heads
        w_o4 = w_o.reshape(kv_heads, n_group, head_dim, model_dim)
        gain_f32 = norm_gain.astype(jnp.float32)
        x_f32 = x_in.astype(jnp.float32)
        inv_rms = lax.rsqrt(jnp.mean(x_f32 * x_f32, axis=-1, keepdims=True) + EPS)
        unit_x = x_f32 * inv_rms
        x_norm = (unit_x * gain_f32).astype(jnp.bfloat16)
        queries = jnp.einsum('duo,ojf->dujf', x_norm, w_q, preferred_element_type=jnp.float32).astype(jnp.bfloat16).reshape(n_batch, seq_len, kv_heads, n_group, head_dim)
        keys_own = jnp.einsum('bsm,mkd->bskd', x_norm, w_k, preferred_element_type=jnp.float32).astype(jnp.bfloat16)
        vals_own = jnp.einsum('bsm,mkd->bskd', x_norm, w_v, preferred_element_type=jnp.float32).astype(jnp.bfloat16)
        tok_pos = jnp.arange(seq_len)
        causal = tok_pos[:, None] >= tok_pos[None, :]
        stat_shape = (n_batch, kv_heads, n_group, seq_len)
        soft_stats = (jnp.full(stat_shape, -jnp.inf, jnp.float32),
                      jnp.zeros(stat_shape, jnp.float32),
                      jnp.zeros(stat_shape + (head_dim,), jnp.float32))
        soft_stats = attend_pair(queries, keys_own, vals_own, soft_stats, causal)

        def visit_fwd(key_blk, val_blk, stats_in):
            return attend_pair(queries, key_blk, val_blk, stats_in, None)

        def skip_fwd(key_blk, val_blk, stats_in):
            return stats_in

        def fwd_body(step_idx, loop_state):
            key_blk, val_blk, stats_in = loop_state
            key_blk, val_blk = lax.ppermute((key_blk, val_blk), 'cp', shift_perm)
            stats_in = lax.cond(step_idx <= my_idx, visit_fwd, skip_fwd, key_blk, val_blk, stats_in)
            return key_blk, val_blk, stats_in

        fwd_state = lax.fori_loop(1, n_dev, fwd_body, (keys_own, vals_own, soft_stats))
        run_max, run_sum, run_acc = fwd_state[2]
        attn_out = (run_acc / run_sum[..., None]).astype(jnp.bfloat16)
        log_norm = run_max + jnp.log(run_sum)
        proj_out = jnp.einsum('bkgqd,kgdm->bqm', attn_out, w_o4, preferred_element_type=jnp.float32)
        y_out = (x_f32 + proj_out).astype(jnp.bfloat16)

        d_wo = jnp.einsum('bkgqd,bqm->kgdm', attn_out, dy_in, preferred_element_type=jnp.float32).reshape(n_heads, head_dim, model_dim)
        d_attn = jnp.einsum('bqm,kgdm->bkgqd', dy_in, w_o4, preferred_element_type=jnp.float32).astype(jnp.bfloat16)
        delta_row = jnp.einsum('bkgqd,bkgqd->bkgq', d_attn, attn_out, preferred_element_type=jnp.float32)
        d_query, d_key_acc, d_val_acc = grad_pair(queries, keys_own, vals_own, d_attn, delta_row, log_norm, causal)

        def visit_bwd(key_blk, val_blk, grad_acc):
            d_query_c, d_key_c, d_val_c = grad_pair(queries, key_blk, val_blk, d_attn, delta_row, log_norm, None)
            return (grad_acc[0] + d_key_c, grad_acc[1] + d_val_c, grad_acc[2] + d_query_c)

        def skip_bwd(key_blk, val_blk, grad_acc):
            return grad_acc

        def bwd_body(step_idx, loop_state):
            key_blk, val_blk, d_key_blk, d_val_blk, d_query_acc = loop_state
            key_blk, val_blk, d_key_blk, d_val_blk = lax.ppermute((key_blk, val_blk, d_key_blk, d_val_blk), 'cp', shift_perm)
            d_key_blk, d_val_blk, d_query_acc = lax.cond(step_idx <= my_idx, visit_bwd, skip_bwd, key_blk, val_blk, (d_key_blk, d_val_blk, d_query_acc))
            return key_blk, val_blk, d_key_blk, d_val_blk, d_query_acc

        bwd_state = lax.fori_loop(1, n_dev, bwd_body, (keys_own, vals_own, d_key_acc, d_val_acc, d_query))
        d_key_acc, d_val_acc = lax.ppermute((bwd_state[2], bwd_state[3]), 'cp', shift_perm)
        d_query_b = bwd_state[4].astype(jnp.bfloat16).reshape(n_batch, seq_len, n_heads, head_dim)
        d_key_b = d_key_acc.astype(jnp.bfloat16)
        d_val_b = d_val_acc.astype(jnp.bfloat16)
        d_wq = jnp.einsum('duo,dujf->ojf', x_norm, d_query_b, preferred_element_type=jnp.float32)
        d_wk = jnp.einsum('bsm,bskd->mkd', x_norm, d_key_b, preferred_element_type=jnp.float32)
        d_wv = jnp.einsum('bsm,bskd->mkd', x_norm, d_val_b, preferred_element_type=jnp.float32)
        d_norm = (jnp.einsum('dujf,ojf->duo', d_query_b, w_q, preferred_element_type=jnp.float32)
                  + jnp.einsum('bskd,mkd->bsm', d_key_b, w_k, preferred_element_type=jnp.float32)
                  + jnp.einsum('bskd,mkd->bsm', d_val_b, w_v, preferred_element_type=jnp.float32))
        d_gain = jnp.sum(d_norm * unit_x, axis=(0, 1))
        d_unit = d_norm * gain_f32
        dx_out = (dy_in.astype(jnp.float32) + inv_rms * (d_unit - unit_x * jnp.mean(d_unit * unit_x, axis=-1, keepdims=True))).astype(jnp.bfloat16)
        d_gain, d_wq, d_wk, d_wv, d_wo = lax.psum((d_gain, d_wq, d_wk, d_wv, d_wo), 'cp')
        return y_out, dx_out, d_gain, d_wq, d_wk, d_wv, d_wo

    act_spec = P('dp', 'cp', None)
    mat_spec = P(None, None, None)
    grad_spec = P('dp', None, None)
    return jax.shard_map(device_fn, mesh=mesh,
                         in_specs=(act_spec, act_spec, P(None), mat_spec, mat_spec, mat_spec, mat_spec),
                         out_specs=(act_spec, act_spec, P('dp'), grad_spec, grad_spec, grad_spec, grad_spec),
                         check_vma=False)
```

profile of v0, /device:TPU:0, one launch (start us, length us, event | category | flops | bytes accessed | tf_op | source)
XLA Modules:
  0.0 2384.8 jit_solution(417441424506804649)
XLA Ops:
  7.2 13.9 convert_bitcast_fusion
  24.0 3.5 copy.71
  30.3 7.3 fusion.96
  37.7 3.5 fusion.93
  43.1 13.5 fusion.87
  60.2 4.9 broadcast_add_fusion
  65.0 269.5 %while.42 = (s32[]{:T(128)}, bf16[4,128,8,128]{3,1,2,0:T(8,128)(2,1)}, bf16[4,128,8,128]{3,1,2,0:T(8,128)(2,1)}, f32[4,8,3,128]{3,2,1,0:T(4,128)S(1)}, f32[4,8,3...) while((s32[]{:T(128)}, ...), condition=%wide.region_8.9_spmd, body=%wide.region_3.8_spmd.sunk | while | flops 821059584 | bytes 94110056 | solution.py:76
  68.4 12.8 collective-permute-done.1
  81.1 11.2 collective-permute-done
  97.0 11.0 collective-permute-start.1
  110.4 10.3 collective-permute-done.1
  120.7 11.2 collective-permute-done
  138.0 14.5 collective-permute-start
  152.5 7.8 collective-permute-done.1
  160.3 11.2 collective-permute-done
  176.2 4.0 collective-permute-start.1
  182.6 17.3 collective-permute-done.1
  199.9 11.2 collective-permute-done
  215.8 23.7 collective-permute-done.1
  239.5 11.2 collective-permute-done
  255.3 23.7 collective-permute-done.1
  279.1 11.2 collective-permute-done
  294.9 23.7 collective-permute-done.1
  318.7 11.2 collective-permute-done
  334.6 9.5 multiply_reduce_fusion
  347.3 12.2 multiply_convert_fusion.1
  362.3 3.7 convolution_bitcast_fusion.3
  371.8 6.6 copy.33
  378.4 673.8 %while.43 = (s32[]{:T(128)}, bf16[4,128,8,128]{3,1,2,0:T(8,128)(2,1)}, bf16[4,128,8,128]{3,1,2,0:T(8,128)(2,1)}, f32[4,128,8,128]{3,1,2,0:T(8,128)}, f32[4,128,8...) while((s32[]{:T(128)}, ...), condition=%wide.region_12.13_spmd, body=%wide.region_9.12_spmd.sunk | while | flops 2030043136 | bytes 159531536 | solution.py:101
  378.7 68.4 %collective-permute-done.3 = bf16[4,128,8,128]{3,1,2,0:T(8,128)(2,1)} collective-permute-done((bf16[4,128,8,128]{3,1,2,0:T(8,128)(2,1)}, bf16[4,128,8,128]{3,1,2,0:T(8,128)(2,1)}, u32[]{:S(2)}, u32[]{:S(2)}) %collective-permute-start.3) | collective-permute-done | bytes 1048608 | tf_op jit(solution)/shard_map/while/body/eval_jaxpr/ppermute | solution.py:97
  449.4 8.9 collective-permute-done.2
  466.9 9.3 collective-permute-start.3
  476.2 3.4 collective-permute-start.2
  479.6 65.0 %collective-permute-done.3 = bf16[4,128,8,128]{3,1,2,0:T(8,128)(2,1)} collective-permute-done((bf16[4,128,8,128]{3,1,2,0:T(8,128)(2,1)}, bf16[4,128,8,128]{3,1,2,0:T(8,128)(2,1)}, u32[]{:S(2)}, u32[]{:S(2)}) %collective-permute-start.3) | collective-permute-done | bytes 1048608 | tf_op jit(solution)/shard_map/while/body/eval_jaxpr/ppermute | solution.py:97
  546.9 8.9 collective-permute-done.2
  564.5 12.7 collective-permute-start.3
  580.6 61.6 %collective-permute-done.3 = bf16[4,128,8,128]{3,1,2,0:T(8,128)(2,1)} collective-permute-done((bf16[4,128,8,128]{3,1,2,0:T(8,128)(2,1)}, bf16[4,128,8,128]{3,1,2,0:T(8,128)(2,1)}, u32[]{:S(2)}, u32[]{:S(2)}) %collective-permute-start.3) | collective-permute-done | bytes 1048608 | tf_op jit(solution)/shard_map/while/body/eval_jaxpr/ppermute | solution.py:97
  644.5 8.9 collective-permute-done.2
  662.0 16.1 collective-permute-start.3
  681.5 58.2 %collective-permute-done.3 = bf16[4,128,8,128]{3,1,2,0:T(8,128)(2,1)} collective-permute-done((bf16[4,128,8,128]{3,1,2,0:T(8,128)(2,1)}, bf16[4,128,8,128]{3,1,2,0:T(8,128)(2,1)}, u32[]{:S(2)}, u32[]{:S(2)}) %collective-permute-start.3) | collective-permute-done | bytes 1048608 | tf_op jit(solution)/shard_map/while/body/eval_jaxpr/ppermute | solution.py:97
  742.0 8.9 collective-permute-done.2
  759.6 22.9 collective-permute-start.2
  782.5 54.8 %collective-permute-done.3 = bf16[4,128,8,128]{3,1,2,0:T(8,128)(2,1)} collective-permute-done((bf16[4,128,8,128]{3,1,2,0:T(8,128)(2,1)}, bf16[4,128,8,128]{3,1,2,0:T(8,128)(2,1)}, u32[]{:S(2)}, u32[]{:S(2)}) %collective-permute-start.3) | collective-permute-done | bytes 1048608 | tf_op jit(solution)/shard_map/while/body/eval_jaxpr/ppermute | solution.py:97
  839.6 8.9 collective-permute-done.2
  862.4 72.4 %collective-permute-done.3 = bf16[4,128,8,128]{3,1,2,0:T(8,128)(2,1)} collective-permute-done((bf16[4,128,8,128]{3,1,2,0:T(8,128)(2,1)}, bf16[4,128,8,128]{3,1,2,0:T(8,128)(2,1)}, u32[]{:S(2)}, u32[]{:S(2)}) %collective-permute-start.3) | collective-permute-done | bytes 1048608 | tf_op jit(solution)/shard_map/while/body/eval_jaxpr/ppermute | solution.py:97
  937.1 8.9 collective-permute-done.2
  954.7 77.6 %collective-permute-done.3 = bf16[4,128,8,128]{3,1,2,0:T(8,128)(2,1)} collective-permute-done((bf16[4,128,8,128]{3,1,2,0:T(8,128)(2,1)}, bf16[4,128,8,128]{3,1,2,0:T(8,128)(2,1)}, u32[]{:S(2)}, u32[]{:S(2)}) %collective-permute-start.3) | collective-permute-done | bytes 1048608 | tf_op jit(solution)/shard_map/while/body/eval_jaxpr/ppermute | solution.py:97
  1034.7 8.9 collective-permute-done.2
  1060.4 19.2 convolution_bitcast_fusion
  1079.6 16.6 fusion.70
  1096.2 27.9 %copy.90 = f32[8,3,128,3072,1]{3,2,1,0,4:T(8,128)} copy(f32[8,3,128,3072,1]{3,2,0,1,4:T(8,128)} %fusion.70) | data formatting | bytes 75497472 | tf_op jit(solution)/shard_map/bkgqd,bqm->kgdm/dot_general | solution.py:83
  1124.1 7.9 convolution_bitcast_fusion.1
  1132.0 7.9 convolution_bitcast_fusion.2
  1140.0 16.8 fusion.26
  1156.9 13.8 fusion.44
  1170.7 6.7 fusion.51
  1177.4 14.3 fusion.42
  1191.7 44.5 %psum.35 = f32[3072]{0:T(1024)} all-reduce(f32[3072]{0:T(1024)S(1)} %get-tuple-element.433), channel_id=1, replica_groups=mesh['dp'=2,'cp'=8] {'cp'}, use_global_device_ids=true, to_apply=%region_15.16 | all-reduce | flops 3072 | bytes 24576 | tf_op jit(solution)/shard_map/psum | solution.py:115
  1236.2 6.1 fusion.41
  1242.3 1034.8 %all-reduce.3.cloned.1.call-done = (f32[3072,24,128]{2,0,1:T(8,128)}, f32[3072,8,128]{2,0,1:T(8,128)}, f32[3072,8,128]{2,0,1:T(8,128)}, f32[24,128,3072]{2,1,0:T(8,128)}) async-done(((f32[3072,24,128]{2,0,1:T(8,128)}, f32[3072,8,128]{2,0,1:T(8,128)}, f32[3072,8,128]{2,0,1:T(8,128)}, f32[24,128,3072]{2,1,0:T(8,128)}), (f32[3072,24,128]{2,0,1:T(8,128)}, f32[3072,8,128]{2,0,1:T(8,128)}, ...) | async-done | bytes 100663312 | tf_op jit(solution)/shard_map/psum | solution.py:115
  2277.0 35.9 %copy.45 = f32[3072,24,128]{2,1,0:T(8,128)} copy(f32[3072,24,128]{2,0,1:T(8,128)} %get-tuple-element.473) | data formatting | bytes 75497472
  2313.0 18.2 copy.46
  2331.2 18.5 copy.47
  2349.7 27.9 %copy.191 = f32[24,128,3072]{2,1,0:T(8,128)} copy(f32[24,128,3072]{2,1,0:T(8,128)} %get-tuple-element.697) | data formatting | bytes 75497472
  (180 shorter events, 162.5 us)
Async XLA Ops:
  7.2 2269.9 %all-reduce.3.cloned.1.call-start = ((), (), s32[]{:S(2)}) async-start(), calls=%async_computation | async-start | bytes 201326592 | tf_op jit(solution)/shard_map/psum | solution.py:115
  24.0 6.3 copy-start.24
  27.5 10.2 slice-start.4
  30.2 12.9 copy-start.22
  30.3 12.9 copy-start.20
  30.3 7.4 copy-start.15
  30.3 7.4 slice-start.5
  37.7 22.5 copy-start.18
  41.1 15.5 copy-start.9
  58.1 6.9 copy-start.5
  65.0 16.1 collective-permute-start.1
  65.8 26.6 %collective-permute-start = (bf16[4,128,8,128]{3,1,2,0:T(8,128)(2,1)}, bf16[4,128,8,128]{3,1,2,0:T(8,128)(2,1)}, u32[]{:S(2)}, u32[]{:S(2)}) collective-permute-start(bf16[4,128,8,128]{3,1,2,0:T(8,128)(2,1)} %get-tuple-element.638), channel_id=1, source_target_pairs={{0,1},{1,2},{2,3},{3,4},{4,5},{5,6},{6,7},{7,0},{8,9},{9,10},{10,1... | collective-permute-start | bytes 3145736 | tf_op jit(solution)/shard_map/while/body/eval_jaxpr/ppermute | solution.py:72
  97.0 23.7 collective-permute-start.1
  107.9 24.0 %collective-permute-start = (bf16[4,128,8,128]{3,1,2,0:T(8,128)(2,1)}, bf16[4,128,8,128]{3,1,2,0:T(8,128)(2,1)}, u32[]{:S(2)}, u32[]{:S(2)}) collective-permute-start(bf16[4,128,8,128]{3,1,2,0:T(8,128)(2,1)} %get-tuple-element.638), channel_id=1, source_target_pairs={{0,1},{1,2},{2,3},{3,4},{4,5},{5,6},{6,7},{7,0},{8,9},{9,10},{10,1... | collective-permute-start | bytes 3145736 | tf_op jit(solution)/shard_map/while/body/eval_jaxpr/ppermute | solution.py:72
  136.6 23.7 collective-permute-start.1
  138.0 33.5 %collective-permute-start = (bf16[4,128,8,128]{3,1,2,0:T(8,128)(2,1)}, bf16[4,128,8,128]{3,1,2,0:T(8,128)(2,1)}, u32[]{:S(2)}, u32[]{:S(2)}) collective-permute-start(bf16[4,128,8,128]{3,1,2,0:T(8,128)(2,1)} %get-tuple-element.638), channel_id=1, source_target_pairs={{0,1},{1,2},{2,3},{3,4},{4,5},{5,6},{6,7},{7,0},{8,9},{9,10},{10,1... | collective-permute-start | bytes 3145736 | tf_op jit(solution)/shard_map/while/body/eval_jaxpr/ppermute | solution.py:72
  176.2 23.7 collective-permute-start.1
  180.1 31.0 %collective-permute-start = (bf16[4,128,8,128]{3,1,2,0:T(8,128)(2,1)}, bf16[4,128,8,128]{3,1,2,0:T(8,128)(2,1)}, u32[]{:S(2)}, u32[]{:S(2)}) collective-permute-start(bf16[4,128,8,128]{3,1,2,0:T(8,128)(2,1)} %get-tuple-element.638), channel_id=1, source_target_pairs={{0,1},{1,2},{2,3},{3,4},{4,5},{5,6},{6,7},{7,0},{8,9},{9,10},{10,1... | collective-permute-start | bytes 3145736 | tf_op jit(solution)/shard_map/while/body/eval_jaxpr/ppermute | solution.py:72
  215.7 23.7 collective-permute-start.1
  215.7 35.0 %collective-permute-start = (bf16[4,128,8,128]{3,1,2,0:T(8,128)(2,1)}, bf16[4,128,8,128]{3,1,2,0:T(8,128)(2,1)}, u32[]{:S(2)}, u32[]{:S(2)}) collective-permute-start(bf16[4,128,8,128]{3,1,2,0:T(8,128)(2,1)} %get-tuple-element.638), channel_id=1, source_target_pairs={{0,1},{1,2},{2,3},{3,4},{4,5},{5,6},{6,7},{7,0},{8,9},{9,10},{10,1... | collective-permute-start | bytes 3145736 | tf_op jit(solution)/shard_map/while/body/eval_jaxpr/ppermute | solution.py:72
  255.3 23.7 collective-permute-start.1
  255.3 35.0 %collective-permute-start = (bf16[4,128,8,128]{3,1,2,0:T(8,128)(2,1)}, bf16[4,128,8,128]{3,1,2,0:T(8,128)(2,1)}, u32[]{:S(2)}, u32[]{:S(2)}) collective-permute-start(bf16[4,128,8,128]{3,1,2,0:T(8,128)(2,1)} %get-tuple-element.638), channel_id=1, source_target_pairs={{0,1},{1,2},{2,3},{3,4},{4,5},{5,6},{6,7},{7,0},{8,9},{9,10},{10,1... | collective-permute-start | bytes 3145736 | tf_op jit(solution)/shard_map/while/body/eval_jaxpr/ppermute | solution.py:72
  294.9 23.7 collective-permute-start.1
  294.9 35.0 %collective-permute-start = (bf16[4,128,8,128]{3,1,2,0:T(8,128)(2,1)}, bf16[4,128,8,128]{3,1,2,0:T(8,128)(2,1)}, u32[]{:S(2)}, u32[]{:S(2)}) collective-permute-start(bf16[4,128,8,128]{3,1,2,0:T(8,128)(2,1)} %get-tuple-element.638), channel_id=1, source_target_pairs={{0,1},{1,2},{2,3},{3,4},{4,5},{5,6},{6,7},{7,0},{8,9},{9,10},{10,1... | collective-permute-start | bytes 3145736 | tf_op jit(solution)/shard_map/while/body/eval_jaxpr/ppermute | solution.py:72
  334.5 9.5 copy-start
  334.6 9.5 copy-start.6
  378.4 82.3 %collective-permute-start.5 = (f32[4,128,8,128]{3,1,2,0:T(8,128)}, f32[4,128,8,128]{3,1,2,0:T(8,128)}, u32[]{:S(2)}, u32[]{:S(2)}) collective-permute-start(f32[4,128,8,128]{3,1,2,0:T(8,128)} %get-tuple-element.671), channel_id=1, source_target_pairs={{0,1},{1,2},{2,3},{3,4},{4,5},{5,6},{6,7},{7,0},{8,9},{9,10},{10,1... | collective-permute-start | bytes 6291464 | tf_op jit(solution)/shard_map/while/body/eval_jaxpr/ppermute | solution.py:97
  378.4 82.3 %collective-permute-start.4 = (f32[4,128,8,128]{3,1,2,0:T(8,128)}, f32[4,128,8,128]{3,1,2,0:T(8,128)}, u32[]{:S(2)}, u32[]{:S(2)}) collective-permute-start(f32[4,128,8,128]{3,1,2,0:T(8,128)} %get-tuple-element.670), channel_id=1, source_target_pairs={{0,1},{1,2},{2,3},{3,4},{4,5},{5,6},{6,7},{7,0},{8,9},{9,10},{10,1... | collective-permute-start | bytes 6291464 | tf_op jit(solution)/shard_map/while/body/eval_jaxpr/ppermute | solution.py:97
  378.4 68.7 %collective-permute-start.3 = (bf16[4,128,8,128]{3,1,2,0:T(8,128)(2,1)}, bf16[4,128,8,128]{3,1,2,0:T(8,128)(2,1)}, u32[]{:S(2)}, u32[]{:S(2)}) collective-permute-start(bf16[4,128,8,128]{3,1,2,0:T(8,128)(2,1)} %get-tuple-element.669), channel_id=1, source_target_pairs={{0,1},{1,2},{2,3},{3,4},{4,5},{5,6},{6,7},{7,0},{8,9},{9,10},{10,1... | collective-permute-start | bytes 3145736 | tf_op jit(solution)/shard_map/while/body/eval_jaxpr/ppermute | solution.py:97
  378.4 79.9 %collective-permute-start.2 = (bf16[4,128,8,128]{3,1,2,0:T(8,128)(2,1)}, bf16[4,128,8,128]{3,1,2,0:T(8,128)(2,1)}, u32[]{:S(2)}, u32[]{:S(2)}) collective-permute-start(bf16[4,128,8,128]{3,1,2,0:T(8,128)(2,1)} %get-tuple-element.668), channel_id=1, source_target_pairs={{0,1},{1,2},{2,3},{3,4},{4,5},{5,6},{6,7},{7,0},{8,9},{9,10},{10,1... | collective-permute-start | bytes 3145736 | tf_op jit(solution)/shard_map/while/body/eval_jaxpr/ppermute | solution.py:97
  466.9 91.3 %collective-permute-start.5 = (f32[4,128,8,128]{3,1,2,0:T(8,128)}, f32[4,128,8,128]{3,1,2,0:T(8,128)}, u32[]{:S(2)}, u32[]{:S(2)}) collective-permute-start(f32[4,128,8,128]{3,1,2,0:T(8,128)} %get-tuple-element.671), channel_id=1, source_target_pairs={{0,1},{1,2},{2,3},{3,4},{4,5},{5,6},{6,7},{7,0},{8,9},{9,10},{10,1... | collective-permute-start | bytes 6291464 | tf_op jit(solution)/shard_map/while/body/eval_jaxpr/ppermute | solution.py:97
  466.9 91.3 %collective-permute-start.4 = (f32[4,128,8,128]{3,1,2,0:T(8,128)}, f32[4,128,8,128]{3,1,2,0:T(8,128)}, u32[]{:S(2)}, u32[]{:S(2)}) collective-permute-start(f32[4,128,8,128]{3,1,2,0:T(8,128)} %get-tuple-element.670), channel_id=1, source_target_pairs={{0,1},{1,2},{2,3},{3,4},{4,5},{5,6},{6,7},{7,0},{8,9},{9,10},{10,1... | collective-permute-start | bytes 6291464 | tf_op jit(solution)/shard_map/while/body/eval_jaxpr/ppermute | solution.py:97
  466.9 77.7 %collective-permute-start.3 = (bf16[4,128,8,128]{3,1,2,0:T(8,128)(2,1)}, bf16[4,128,8,128]{3,1,2,0:T(8,128)(2,1)}, u32[]{:S(2)}, u32[]{:S(2)}) collective-permute-start(bf16[4,128,8,128]{3,1,2,0:T(8,128)(2,1)} %get-tuple-element.669), channel_id=1, source_target_pairs={{0,1},{1,2},{2,3},{3,4},{4,5},{5,6},{6,7},{7,0},{8,9},{9,10},{10,1... | collective-permute-start | bytes 3145736 | tf_op jit(solution)/shard_map/while/body/eval_jaxpr/ppermute | solution.py:97
  476.2 79.6 %collective-permute-start.2 = (bf16[4,128,8,128]{3,1,2,0:T(8,128)(2,1)}, bf16[4,128,8,128]{3,1,2,0:T(8,128)(2,1)}, u32[]{:S(2)}, u32[]{:S(2)}) collective-permute-start(bf16[4,128,8,128]{3,1,2,0:T(8,128)(2,1)} %get-tuple-element.668), channel_id=1, source_target_pairs={{0,1},{1,2},{2,3},{3,4},{4,5},{5,6},{6,7},{7,0},{8,9},{9,10},{10,1... | collective-permute-start | bytes 3145736 | tf_op jit(solution)/shard_map/while/body/eval_jaxpr/ppermute | solution.py:97
  564.5 91.3 %collective-permute-start.5 = (f32[4,128,8,128]{3,1,2,0:T(8,128)}, f32[4,128,8,128]{3,1,2,0:T(8,128)}, u32[]{:S(2)}, u32[]{:S(2)}) collective-permute-start(f32[4,128,8,128]{3,1,2,0:T(8,128)} %get-tuple-element.671), channel_id=1, source_target_pairs={{0,1},{1,2},{2,3},{3,4},{4,5},{5,6},{6,7},{7,0},{8,9},{9,10},{10,1... | collective-permute-start | bytes 6291464 | tf_op jit(solution)/shard_map/while/body/eval_jaxpr/ppermute | solution.py:97
  564.5 91.3 %collective-permute-start.4 = (f32[4,128,8,128]{3,1,2,0:T(8,128)}, f32[4,128,8,128]{3,1,2,0:T(8,128)}, u32[]{:S(2)}, u32[]{:S(2)}) collective-permute-start(f32[4,128,8,128]{3,1,2,0:T(8,128)} %get-tuple-element.670), channel_id=1, source_target_pairs={{0,1},{1,2},{2,3},{3,4},{4,5},{5,6},{6,7},{7,0},{8,9},{9,10},{10,1... | collective-permute-start | bytes 6291464 | tf_op jit(solution)/shard_map/while/body/eval_jaxpr/ppermute | solution.py:97
  564.5 77.6 %collective-permute-start.3 = (bf16[4,128,8,128]{3,1,2,0:T(8,128)(2,1)}, bf16[4,128,8,128]{3,1,2,0:T(8,128)(2,1)}, u32[]{:S(2)}, u32[]{:S(2)}) collective-permute-start(bf16[4,128,8,128]{3,1,2,0:T(8,128)(2,1)} %get-tuple-element.669), channel_id=1, source_target_pairs={{0,1},{1,2},{2,3},{3,4},{4,5},{5,6},{6,7},{7,0},{8,9},{9,10},{10,1... | collective-permute-start | bytes 3145736 | tf_op jit(solution)/shard_map/while/body/eval_jaxpr/ppermute | solution.py:97
  577.2 76.2 %collective-permute-start.2 = (bf16[4,128,8,128]{3,1,2,0:T(8,128)(2,1)}, bf16[4,128,8,128]{3,1,2,0:T(8,128)(2,1)}, u32[]{:S(2)}, u32[]{:S(2)}) collective-permute-start(bf16[4,128,8,128]{3,1,2,0:T(8,128)(2,1)} %get-tuple-element.668), channel_id=1, source_target_pairs={{0,1},{1,2},{2,3},{3,4},{4,5},{5,6},{6,7},{7,0},{8,9},{9,10},{10,1... | collective-permute-start | bytes 3145736 | tf_op jit(solution)/shard_map/while/body/eval_jaxpr/ppermute | solution.py:97
  662.0 91.3 %collective-permute-start.5 = (f32[4,128,8,128]{3,1,2,0:T(8,128)}, f32[4,128,8,128]{3,1,2,0:T(8,128)}, u32[]{:S(2)}, u32[]{:S(2)}) collective-permute-start(f32[4,128,8,128]{3,1,2,0:T(8,128)} %get-tuple-element.671), channel_id=1, source_target_pairs={{0,1},{1,2},{2,3},{3,4},{4,5},{5,6},{6,7},{7,0},{8,9},{9,10},{10,1... | collective-permute-start | bytes 6291464 | tf_op jit(solution)/shard_map/while/body/eval_jaxpr/ppermute | solution.py:97
  662.0 91.3 %collective-permute-start.4 = (f32[4,128,8,128]{3,1,2,0:T(8,128)}, f32[4,128,8,128]{3,1,2,0:T(8,128)}, u32[]{:S(2)}, u32[]{:S(2)}) collective-permute-start(f32[4,128,8,128]{3,1,2,0:T(8,128)} %get-tuple-element.670), channel_id=1, source_target_pairs={{0,1},{1,2},{2,3},{3,4},{4,5},{5,6},{6,7},{7,0},{8,9},{9,10},{10,1... | collective-permute-start | bytes 6291464 | tf_op jit(solution)/shard_map/while/body/eval_jaxpr/ppermute | solution.py:97
  662.0 77.7 %collective-permute-start.3 = (bf16[4,128,8,128]{3,1,2,0:T(8,128)(2,1)}, bf16[4,128,8,128]{3,1,2,0:T(8,128)(2,1)}, u32[]{:S(2)}, u32[]{:S(2)}) collective-permute-start(bf16[4,128,8,128]{3,1,2,0:T(8,128)(2,1)} %get-tuple-element.669), channel_id=1, source_target_pairs={{0,1},{1,2},{2,3},{3,4},{4,5},{5,6},{6,7},{7,0},{8,9},{9,10},{10,1... | collective-permute-start | bytes 3145736 | tf_op jit(solution)/shard_map/while/body/eval_jaxpr/ppermute | solution.py:97
  678.1 72.8 %collective-permute-start.2 = (bf16[4,128,8,128]{3,1,2,0:T(8,128)(2,1)}, bf16[4,128,8,128]{3,1,2,0:T(8,128)(2,1)}, u32[]{:S(2)}, u32[]{:S(2)}) collective-permute-start(bf16[4,128,8,128]{3,1,2,0:T(8,128)(2,1)} %get-tuple-element.668), channel_id=1, source_target_pairs={{0,1},{1,2},{2,3},{3,4},{4,5},{5,6},{6,7},{7,0},{8,9},{9,10},{10,1... | collective-permute-start | bytes 3145736 | tf_op jit(solution)/shard_map/while/body/eval_jaxpr/ppermute | solution.py:97
  759.6 91.3 %collective-permute-start.5 = (f32[4,128,8,128]{3,1,2,0:T(8,128)}, f32[4,128,8,128]{3,1,2,0:T(8,128)}, u32[]{:S(2)}, u32[]{:S(2)}) collective-permute-start(f32[4,128,8,128]{3,1,2,0:T(8,128)} %get-tuple-element.671), channel_id=1, source_target_pairs={{0,1},{1,2},{2,3},{3,4},{4,5},{5,6},{6,7},{7,0},{8,9},{9,10},{10,1... | collective-permute-start | bytes 6291464 | tf_op jit(solution)/shard_map/while/body/eval_jaxpr/ppermute | solution.py:97
  759.6 91.3 %collective-permute-start.4 = (f32[4,128,8,128]{3,1,2,0:T(8,128)}, f32[4,128,8,128]{3,1,2,0:T(8,128)}, u32[]{:S(2)}, u32[]{:S(2)}) collective-permute-start(f32[4,128,8,128]{3,1,2,0:T(8,128)} %get-tuple-element.670), channel_id=1, source_target_pairs={{0,1},{1,2},{2,3},{3,4},{4,5},{5,6},{6,7},{7,0},{8,9},{9,10},{10,1... | collective-permute-start | bytes 6291464 | tf_op jit(solution)/shard_map/while/body/eval_jaxpr/ppermute | solution.py:97
  759.6 77.7 %collective-permute-start.3 = (bf16[4,128,8,128]{3,1,2,0:T(8,128)(2,1)}, bf16[4,128,8,128]{3,1,2,0:T(8,128)(2,1)}, u32[]{:S(2)}, u32[]{:S(2)}) collective-permute-start(bf16[4,128,8,128]{3,1,2,0:T(8,128)(2,1)} %get-tuple-element.669), channel_id=1, source_target_pairs={{0,1},{1,2},{2,3},{3,4},{4,5},{5,6},{6,7},{7,0},{8,9},{9,10},{10,1... | collective-permute-start | bytes 3145736 | tf_op jit(solution)/shard_map/while/body/eval_jaxpr/ppermute | solution.py:97
  759.6 88.9 %collective-permute-start.2 = (bf16[4,128,8,128]{3,1,2,0:T(8,128)(2,1)}, bf16[4,128,8,128]{3,1,2,0:T(8,128)(2,1)}, u32[]{:S(2)}, u32[]{:S(2)}) collective-permute-start(bf16[4,128,8,128]{3,1,2,0:T(8,128)(2,1)} %get-tuple-element.668), channel_id=1, source_target_pairs={{0,1},{1,2},{2,3},{3,4},{4,5},{5,6},{6,7},{7,0},{8,9},{9,10},{10,1... | collective-permute-start | bytes 3145736 | tf_op jit(solution)/shard_map/while/body/eval_jaxpr/ppermute | solution.py:97
  857.1 91.3 %collective-permute-start.5 = (f32[4,128,8,128]{3,1,2,0:T(8,128)}, f32[4,128,8,128]{3,1,2,0:T(8,128)}, u32[]{:S(2)}, u32[]{:S(2)}) collective-permute-start(f32[4,128,8,128]{3,1,2,0:T(8,128)} %get-tuple-element.671), channel_id=1, source_target_pairs={{0,1},{1,2},{2,3},{3,4},{4,5},{5,6},{6,7},{7,0},{8,9},{9,10},{10,1... | collective-permute-start | bytes 6291464 | tf_op jit(solution)/shard_map/while/body/eval_jaxpr/ppermute | solution.py:97
  857.1 91.3 %collective-permute-start.4 = (f32[4,128,8,128]{3,1,2,0:T(8,128)}, f32[4,128,8,128]{3,1,2,0:T(8,128)}, u32[]{:S(2)}, u32[]{:S(2)}) collective-permute-start(f32[4,128,8,128]{3,1,2,0:T(8,128)} %get-tuple-element.670), channel_id=1, source_target_pairs={{0,1},{1,2},{2,3},{3,4},{4,5},{5,6},{6,7},{7,0},{8,9},{9,10},{10,1... | collective-permute-start | bytes 6291464 | tf_op jit(solution)/shard_map/while/body/eval_jaxpr/ppermute | solution.py:97
  857.1 77.7 %collective-permute-start.3 = (bf16[4,128,8,128]{3,1,2,0:T(8,128)(2,1)}, bf16[4,128,8,128]{3,1,2,0:T(8,128)(2,1)}, u32[]{:S(2)}, u32[]{:S(2)}) collective-permute-start(bf16[4,128,8,128]{3,1,2,0:T(8,128)(2,1)} %get-tuple-element.669), channel_id=1, source_target_pairs={{0,1},{1,2},{2,3},{3,4},{4,5},{5,6},{6,7},{7,0},{8,9},{9,10},{10,1... | collective-permute-start | bytes 3145736 | tf_op jit(solution)/shard_map/while/body/eval_jaxpr/ppermute | solution.py:97
  859.0 87.0 %collective-permute-start.2 = (bf16[4,128,8,128]{3,1,2,0:T(8,128)(2,1)}, bf16[4,128,8,128]{3,1,2,0:T(8,128)(2,1)}, u32[]{:S(2)}, u32[]{:S(2)}) collective-permute-start(bf16[4,128,8,128]{3,1,2,0:T(8,128)(2,1)} %get-tuple-element.668), channel_id=1, source_target_pairs={{0,1},{1,2},{2,3},{3,4},{4,5},{5,6},{6,7},{7,0},{8,9},{9,10},{10,1... | collective-permute-start | bytes 3145736 | tf_op jit(solution)/shard_map/while/body/eval_jaxpr/ppermute | solution.py:97
  954.7 91.3 %collective-permute-start.5 = (f32[4,128,8,128]{3,1,2,0:T(8,128)}, f32[4,128,8,128]{3,1,2,0:T(8,128)}, u32[]{:S(2)}, u32[]{:S(2)}) collective-permute-start(f32[4,128,8,128]{3,1,2,0:T(8,128)} %get-tuple-element.671), channel_id=1, source_target_pairs={{0,1},{1,2},{2,3},{3,4},{4,5},{5,6},{6,7},{7,0},{8,9},{9,10},{10,1... | collective-permute-start | bytes 6291464 | tf_op jit(solution)/shard_map/while/body/eval_jaxpr/ppermute | solution.py:97
  954.7 91.3 %collective-permute-start.4 = (f32[4,128,8,128]{3,1,2,0:T(8,128)}, f32[4,128,8,128]{3,1,2,0:T(8,128)}, u32[]{:S(2)}, u32[]{:S(2)}) collective-permute-start(f32[4,128,8,128]{3,1,2,0:T(8,128)} %get-tuple-element.670), channel_id=1, source_target_pairs={{0,1},{1,2},{2,3},{3,4},{4,5},{5,6},{6,7},{7,0},{8,9},{9,10},{10,1... | collective-permute-start | bytes 6291464 | tf_op jit(solution)/shard_map/while/body/eval_jaxpr/ppermute | solution.py:97
  954.7 77.7 %collective-permute-start.3 = (bf16[4,128,8,128]{3,1,2,0:T(8,128)(2,1)}, bf16[4,128,8,128]{3,1,2,0:T(8,128)(2,1)}, u32[]{:S(2)}, u32[]{:S(2)}) collective-permute-start(bf16[4,128,8,128]{3,1,2,0:T(8,128)(2,1)} %get-tuple-element.669), channel_id=1, source_target_pairs={{0,1},{1,2},{2,3},{3,4},{4,5},{5,6},{6,7},{7,0},{8,9},{9,10},{10,1... | collective-permute-start | bytes 3145736 | tf_op jit(solution)/shard_map/while/body/eval_jaxpr/ppermute | solution.py:97
  954.7 88.9 %collective-permute-start.2 = (bf16[4,128,8,128]{3,1,2,0:T(8,128)(2,1)}, bf16[4,128,8,128]{3,1,2,0:T(8,128)(2,1)}, u32[]{:S(2)}, u32[]{:S(2)}) collective-permute-start(bf16[4,128,8,128]{3,1,2,0:T(8,128)(2,1)} %get-tuple-element.668), channel_id=1, source_target_pairs={{0,1},{1,2},{2,3},{3,4},{4,5},{5,6},{6,7},{7,0},{8,9},{9,10},{10,1... | collective-permute-start | bytes 3145736 | tf_op jit(solution)/shard_map/while/body/eval_jaxpr/ppermute | solution.py:97
  1055.1 69.0 %collective-permute-start.7 = (bf16[4,128,8,128]{3,1,2,0:T(8,128)(2,1)}, bf16[4,128,8,128]{3,1,2,0:T(8,128)(2,1)}, u32[]{:S(2)}, u32[]{:S(2)}) collective-permute-start(bf16[4,128,8,128]{3,1,2,0:T(8,128)(2,1)} %convert.12), channel_id=1, source_target_pairs={{0,1},{1,2},{2,3},{3,4},{4,5},{5,6},{6,7},{7,0},{8,9},{9,10},{10,1... | collective-permute-start | bytes 3145736 | tf_op jit(solution)/shard_map/ppermute | solution.py:102
  1058.0 74.0 %collective-permute-start.6 = (bf16[4,128,8,128]{3,1,2,0:T(8,128)(2,1)}, bf16[4,128,8,128]{3,1,2,0:T(8,128)(2,1)}, u32[]{:S(2)}, u32[]{:S(2)}) collective-permute-start(bf16[4,128,8,128]{3,1,2,0:T(8,128)(2,1)} %convert.11), channel_id=1, source_target_pairs={{0,1},{1,2},{2,3},{3,4},{4,5},{5,6},{6,7},{7,0},{8,9},{9,10},{10,1... | collective-permute-start | bytes 3145736 | tf_op jit(solution)/shard_map/ppermute | solution.py:102
  1060.3 19.3 copy-start.7
  1060.4 19.2 copy-start.11
  1140.0 16.8 copy-start.8
  1140.0 16.8 copy-start.17
  1156.8 13.8 copy-start.25
  1177.4 58.8 %copy-start.12 = (bf16[4,128,3072]{2,1,0:T(8,128)(2,1)S(1)}, bf16[4,128,3072]{2,1,0:T(8,128)(2,1)}, u32[]{:S(2)}) copy-start(bf16[4,128,3072]{2,1,0:T(8,128)(2,1)} %param.16) | copy-start | bytes 9437188
  2277.0 35.9 %copy-start.14 = (f32[3072,8,128]{2,0,1:T(8,128)S(1)}, f32[3072,8,128]{2,0,1:T(8,128)}, u32[]{:S(2)}) copy-start(f32[3072,8,128]{2,0,1:T(8,128)} %get-tuple-element.474) | copy-start | bytes 37748740
  2313.0 18.2 copy-start.13
  (6 other events, 27.6 us)
Sparse Core Ops, SparseCore 0:
  1140.1 1136.8 all-reduce.2
where the time goes:
time: 2400 us; the launch traced here: 2380 us
  waiting for transfers between devices  1750 us (73%)
  local copies, waits for them, and re-layouts  258 us (11%)
  matrix products  170 us (7%)
  starting transfers between devices  116 us (5%)
  blocking collectives  44.5 us (2%)
  other arithmetic  28.4 us (1%)
    psum x1, waiting for transfers between devices, device_fn(): lax.psum((d_gain, d_wq, d_wk, d_wv, d_wo), 'cp')  1030 us
    ppermute x28, waiting for transfers between devices, bwd_body(): lax.ppermute((key_blk, val_blk, d_key_blk, d_val_blk), 'cp', shift_perm)  520 us
    ppermute x14, waiting for transfers between devices, fwd_body(): key_blk, val_blk = lax.ppermute((key_blk, val_blk), 'cp', shift_perm)  198 us
    while x42, local copies, waits for them, and re-layouts  109 us
    unnamed x57, local copies, waits for them, and re-layouts  106 us
    ppermute x28, starting transfers between devices, bwd_body(): lax.ppermute((key_blk, val_blk, d_key_blk, d_val_blk), 'cp', shift_perm)  76.8 us
  transfers between devices with their start and end apart: 45, of which 29 were waited for; matrix products, arithmetic and copies ran while one was open for 7% of the time, Pallas kernels for 0%

commit v1 on v0

v1 whole, which is shorter than its diff:
```python
import functools
import math

import jax
import jax.numpy as jnp
from jax import lax
from jax.experimental import pallas as pl
from jax.experimental.pallas import tpu as pltpu
from jax.sharding import PartitionSpec as P

EPS = 1e-6
HD = 128
LOG2E = math.log2(math.e)
NEG = -1e30
BIG = pltpu.CompilerParams(vmem_limit_bytes=60 * 1024 * 1024)


def dot(a, b, ca, cb):
    return lax.dot_general(a, b, (((ca,), (cb,)), ((), ())), preferred_element_type=jnp.float32)


def cost(flops, nbytes):
    return pl.CostEstimate(flops=int(flops), bytes_accessed=int(nbytes), transcendentals=0)


def relayout_kernel(core_ref, wq_ref, wk_ref, wv_ref, out_ref, half_ref, tmp):
    rows = wq_ref.shape[0]
    first = core_ref[0] == 0
    col, base = 0, 0
    for ref in (wq_ref, wk_ref, wv_ref):
        width = ref.shape[1] * HD
        start = col
        for g in range(ref.shape[1] // 8):
            tmp[...] = ref[:, 8 * g:8 * g + 8, :].astype(jnp.float32).reshape(rows * 8, HD)
            for h in range(8):
                out_ref[:, col:col + HD] = tmp[pl.ds(h, rows, stride=8), :].astype(jnp.bfloat16)
                col += HD
        half = width // 2
        half_ref[:, base:base + half] = jnp.where(first, out_ref[:, start:start + half], out_ref[:, start + half:start + width])
        base += half


def relayout(w_q, w_k, w_v, core):
    dm = w_q.shape[0]
    cols = (w_q.shape[1] + w_k.shape[1] + w_v.shape[1]) * HD
    rows = 256
    return pl.pallas_call(
        relayout_kernel,
        grid_spec=pltpu.PrefetchScalarGridSpec(
            num_scalar_prefetch=1, grid=(dm // rows,),
            in_specs=[pl.BlockSpec((rows, w.shape[1], HD), lambda i, c: (i, 0, 0)) for w in (w_q, w_k, w_v)],
            out_specs=[pl.BlockSpec((rows, cols), lambda i, c: (i, 0)), pl.BlockSpec((rows, cols // 2), lambda i, c: (i, 0))],
            scratch_shapes=[pltpu.VMEM((rows * 8, HD), jnp.float32)]),
        out_shape=[jax.ShapeDtypeStruct((dm, cols), jnp.bfloat16), jax.ShapeDtypeStruct((dm, cols // 2), jnp.bfloat16)],
        cost_estimate=cost(1e10, 4 * dm * cols), name='relayout')(core, w_q, w_k, w_v)


def near_kernel(cb, tbl_ref, a_ref, b_ref, w_ref, o_ref):
    m = pl.program_id(1)
    a = jnp.where(m == 0, a_ref[...], b_ref[...])
    o_ref[...] = dot(a, w_ref[...], 1, cb).astype(jnp.bfloat16)


def far_kernel(cb, tbl_ref, a_ref, w_ref, old_ref, o_ref):
    o_ref[...] = dot(a_ref[...], w_ref[...], 1, cb).astype(jnp.bfloat16)


def proj_specs(w, width, cb, row):
    bn = width // 2
    if cb == 0:
        return bn, pl.BlockSpec((w.shape[0], bn), lambda n, m, t: (0, n))
    return bn, pl.BlockSpec((bn, w.shape[1]), lambda n, m, t: (2 * t[row] + n, 0))


def proj_near(a, b, w, tbl, tok, width, cb, name):
    bm, dm = a.shape
    bn, w_spec = proj_specs(w, width, cb, 2)
    line = pl.BlockSpec((bm, dm), lambda n, m, t: (0, 0))
    return pl.pallas_call(
        functools.partial(near_kernel, cb),
        grid_spec=pltpu.PrefetchScalarGridSpec(
            num_scalar_prefetch=1, grid=(2, 2), in_specs=[line, line, w_spec],
            out_specs=pl.BlockSpec((bm, bn), lambda n, m, t: (t[m], n))),
        out_shape=jax.ShapeDtypeStruct((tok, width), jnp.bfloat16),
        compiler_params=BIG, cost_estimate=cost(4 * bm * dm * width, 2 * dm * width), name=name)(tbl, a, b, w)


def proj_far(a, w, old, tbl, bm, cb, name):
    tok, dm = a.shape
    width = old.shape[1]
    rest = tok // bm - 2
    bn, w_spec = proj_specs(w, width, cb, rest)
    return pl.pallas_call(
        functools.partial(far_kernel, cb),
        grid_spec=pltpu.PrefetchScalarGridSpec(
            num_scalar_prefetch=1, grid=(2, rest),
            in_specs=[pl.BlockSpec((bm, dm), lambda n, m, t: (t[m], 0)), w_spec, pl.BlockSpec(memory_space=pl.ANY)],
            out_specs=pl.BlockSpec((bm, bn), lambda n, m, t: (t[m], n))),
        out_shape=jax.ShapeDtypeStruct(old.shape, jnp.bfloat16), input_output_aliases={3: 0},
        compiler_params=BIG, cost_estimate=cost(2 * rest * bm * dm * width, 2 * tok * dm), name=name)(tbl, a, w, old)


def stack(ref, rb, nblk, rows, group):
    parts = [ref[rb * nblk:(rb + 1) * nblk, 0, :, g * HD:(g + 1) * HD].reshape(rows, HD) for g in range(group)]
    return jnp.concatenate(parts, axis=0)


def fwd_kernel(rows, q_ref, k_ref, v_ref, o_ref, l_ref):
    n, _, blk, width = q_ref.shape
    group, seq, nblk = width // HD, n * blk, rows // blk
    c2 = HD ** -0.5 * LOG2E
    k = k_ref[...].reshape(seq, HD)
    v = v_ref[...].reshape(seq, HD)
    tall = group * rows
    row = lax.broadcasted_iota(jnp.int32, (tall, rows), 0) % rows
    col = lax.broadcasted_iota(jnp.int32, (tall, rows), 1)
    visible = row >= col

    def score(rb):
        return dot(stack(q_ref, rb, nblk, rows, group), k[:(rb + 1) * rows], 1, 1)

    s_next = score(0)
    for rb in range(seq // rows):
        r0 = rb * rows
        s = s_next
        if rb + 1 < seq // rows:
            s_next = score(rb + 1)
        s_d = jnp.where(visible, s[:, r0:], NEG)
        m = jnp.max(s_d, axis=1, keepdims=True)
        if rb:
            m = jnp.maximum(m, jnp.max(s[:, :r0], axis=1, keepdims=True))
        m = m * c2
        p_d = jnp.exp2(s_d * c2 - m)
        l = jnp.sum(p_d, axis=1, keepdims=True)
        p = p_d.astype(jnp.bfloat16)
        if rb:
            p_o = jnp.exp2(s[:, :r0] * c2 - m)
            l = l + jnp.sum(p_o, axis=1, keepdims=True)
            p = jnp.concatenate([p_o.astype(jnp.bfloat16), p], axis=1)
        acc = dot(p, v[:r0 + rows], 1, 0)
        o = (acc / l).astype(jnp.bfloat16)
        log2n = jnp.broadcast_to(m + jnp.log2(l), (tall, 128))
        for g in range(group):
            for j in range(nblk):
                o_ref[rb * nblk + j, 0, :, g * HD:(g + 1) * HD] = o[g * rows + j * blk:g * rows + (j + 1) * blk]
            l_ref[0, g, :, r0:r0 + rows] = log2n[g * rows:(g + 1) * rows].T[0:1]


def attn_fwd(qkv, kvh, group):
    n, nb, s, _ = qkv.shape
    width = group * HD
    first = kvh * group
    return pl.pallas_call(
        functools.partial(fwd_kernel, 128), grid=(nb, kvh),
        in_specs=[pl.BlockSpec((n, 1, s, width), lambda b, h: (0, b, 0, h)),
                  pl.BlockSpec((n, 1, s, HD), lambda b, h: (0, b, 0, first + h)),
                  pl.BlockSpec((n, 1, s, HD), lambda b, h: (0, b, 0, first + kvh + h))],
        out_specs=[pl.BlockSpec((n, 1, s, width), lambda b, h: (0, b, 0, h)),
                   pl.BlockSpec((1, group, 1, n * s), lambda b, h: (b, h, 0, 0))],
        out_shape=[jax.ShapeDtypeStruct((n, nb, s, kvh * width), jnp.bfloat16),
                   jax.ShapeDtypeStruct((nb, kvh * group, 1, n * s), jnp.float32)],
        compiler_params=BIG, cost_estimate=cost(nb * kvh * group * 4 * (n * s) ** 2 * HD, 10 ** 7),
        name='attn_fwd')(qkv, qkv, qkv)


def bwd_kernel(rows, q_ref, k_ref, v_ref, o_ref, do_ref, l_ref, dq_ref, dk_ref, dv_ref, dq_acc):
    n, _, blk, width = q_ref.shape
    group, seq, nblk = width // HD, n * blk, rows // blk
    scale = HD ** -0.5
    c2 = scale * LOG2E
    k = k_ref[...].reshape(seq, HD)
    v = v_ref[...].reshape(seq, HD)
    row = lax.broadcasted_iota(jnp.int32, (rows, rows), 0)
    col = lax.broadcasted_iota(jnp.int32, (rows, rows), 1)
    visible = row <= col
    qs, dos, deltas = [], [], []
    for g in range(group):
        cols = slice(g * HD, (g + 1) * HD)
        qs.append(q_ref[:, 0, :, cols].reshape(seq, HD))
        d_o = do_ref[:, 0, :, cols].reshape(seq, HD)
        o = o_ref[:, 0, :, cols].reshape(seq, HD)
        dos.append(d_o)
        dcol = jnp.sum(d_o.astype(jnp.float32) * o.astype(jnp.float32), axis=1, keepdims=True)
        deltas.append(jnp.broadcast_to(dcol, (seq, 128)).T[0:1])
    units = [(kb, g) for kb in range(seq // rows) for g in range(group)]

    def score(unit):
        k0, g = unit[0] * rows, unit[1]
        return dot(k[k0:k0 + rows], qs[g][k0:], 1, 1), dot(v[k0:k0 + rows], dos[g][k0:], 1, 1)

    following = score(units[0])
    for i, (kb, g) in enumerate(units):
        k0 = kb * rows
        s, dp = following
        if i + 1 < len(units):
            following = score(units[i + 1])
        p = jnp.exp2(s * c2 - l_ref[0, g][:, k0:])
        p_d = jnp.where(visible, p[:, :rows], 0.0)
        p = p_d if k0 + rows == seq else jnp.concatenate([p_d, p[:, rows:]], axis=1)
        ds = (p * (dp - deltas[g][:, k0:]) * scale).astype(jnp.bfloat16)
        dv_c = dot(p.astype(jnp.bfloat16), dos[g][k0:], 1, 0)
        dk_c = dot(ds, qs[g][k0:], 1, 0)
        dq_c = dot(ds, k[k0:k0 + rows], 0, 0)
        if kb == 0:
            dq_acc[g] = dq_c
        else:
            dq_acc[g, k0:] += dq_c
        dv_t, dk_t = (dv_c, dk_c) if g == 0 else (dv_t + dv_c, dk_t + dk_c)
        if g == group - 1:
            dk_ref[kb * nblk:(kb + 1) * nblk, 0] = dk_t.astype(jnp.bfloat16).reshape(nblk, blk, HD)
            dv_ref[kb * nblk:(kb + 1) * nblk, 0] = dv_t.astype(jnp.bfloat16).reshape(nblk, blk, HD)
    for g in range(group):
        dq_ref[:, 0, :, g * HD:(g + 1) * HD] = dq_acc[g].astype(jnp.bfloat16).reshape(n, blk, HD)


def attn_bwd(qkv, o, do, log2n, kvh, group, h0, count):
    n, nb, s, _ = qkv.shape
    width = group * HD
    first = kvh * group
    q_in = pl.BlockSpec((n, 1, s, width), lambda b, h: (0, b, 0, h0 + h))
    q_out = pl.BlockSpec((n, 1, s, width), lambda b, h: (0, b, 0, h))
    k_out = pl.BlockSpec((n, 1, s, HD), lambda b, h: (0, b, 0, h))
    return pl.pallas_call(
        functools.partial(bwd_kernel, 256), grid=(nb, count),
        in_specs=[q_in,
                  pl.BlockSpec((n, 1, s, HD), lambda b, h: (0, b, 0, first + h0 + h)),
                  pl.BlockSpec((n, 1, s, HD), lambda b, h: (0, b, 0, first + kvh + h0 + h)),
                  q_in, q_in,
                  pl.BlockSpec((1, group, 1, n * s), lambda b, h: (b, h0 + h, 0, 0))],
        out_specs=[q_out, k_out, k_out],
        out_shape=[jax.ShapeDtypeStruct((n, nb, s, count * width), jnp.bfloat16),
                   jax.ShapeDtypeStruct((n, nb, s, count * HD), jnp.bfloat16),
                   jax.ShapeDtypeStruct((n, nb, s, count * HD), jnp.bfloat16)],
        scratch_shapes=[pltpu.VMEM((group, n * s, HD), jnp.float32)],
        compiler_params=BIG, cost_estimate=cost(nb * count * group * 10 * (n * s) ** 2 * HD, 10 ** 7),
        name='attn_bwd')(qkv, qkv, qkv, o, do, log2n)


def grad_wo_kernel(chip_ref, a_ref, b_ref, out_ref):
    out_ref[...] = dot(a_ref[...], b_ref[...], 0, 0)


def grad_wo(o, dy, chip, n_chips):
    tok, half = o.shape
    dm = dy.shape[1]
    bm, bn = half // n_chips, 1024
    return pl.pallas_call(
        grad_wo_kernel,
        grid_spec=pltpu.PrefetchScalarGridSpec(
            num_scalar_prefetch=1, grid=(dm // bn,),
            in_specs=[pl.BlockSpec((tok, bm), lambda n, c: (0, c[0])), pl.BlockSpec((tok, bn), lambda n, c: (0, n))],
            out_specs=pl.BlockSpec((bm, bn), lambda n, c: (0, n))),
        out_shape=jax.ShapeDtypeStruct((bm, dm), jnp.float32),
        compiler_params=BIG, cost_estimate=cost(2 * tok * bm * dm, 2 * tok * dm), name='grad_wo')(chip, o, dy)


def grad_wx_kernel(plan, n_src, n_out, core_ref, a_ref, *refs):
    srcs, fulls = refs[:2 * n_src], refs[2 * n_src:2 * n_src + n_out]
    sends, (buf, sem) = refs[2 * n_src + n_out:2 * n_src + 2 * n_out], refs[2 * n_src + 2 * n_out:]
    core = core_ref[0]
    n, nn = pl.program_id(1), pl.num_programs(1)
    step = pl.program_id(0) * nn + n

    def fetch(idx, slot):
        for pos, pieces in enumerate(plan):
            off = 0
            for half, which, lo, hi in pieces:
                for is_mine in (True, False):
                    src = srcs[2 * which + (0 if is_mine else 1)]

                    @pl.when(jnp.logical_and(idx == pos, (core == half) == is_mine))
                    def _(src=src, off=off, lo=lo, w=hi - lo):
                        pltpu.make_async_copy(src.at[:, pl.ds(lo, w)], buf.at[slot, :, pl.ds(off, w)], sem.at[slot]).start()
                off += hi - lo

    @pl.when(step == 0)
    def _():
        fetch(n, 0)

    @pl.when(step + 1 < pl.num_programs(0) * nn)
    def _():
        fetch(lax.rem(n + 1, nn), lax.rem(step + 1, 2))

    slot = lax.rem(step, 2)
    pltpu.make_async_copy(buf.at[slot], buf.at[slot], sem.at[slot]).wait()
    acc = dot(a_ref[...], buf[slot], 0, 0)
    rows = acc.shape[0]

    def store(refs):
        for ref in refs:
            flat = ref.reshape(rows * 8, HD)
            for h in range(8):
                flat[pl.ds(h, rows, stride=8), :] = acc[:, h * HD:(h + 1) * HD]

    if n_out == 1:
        store((fulls[0], sends[0]))
    else:
        for pos in range(n_out):
            @pl.when(n == pos)
            def _(pos=pos):
                store((fulls[pos], sends[pos]))


def grad_wx(x, srcs, plan, heads, core, name):
    tok, dm = x.shape
    bm = 768
    nm = dm // 2 // bm
    flat = [a for pair in srcs for a in pair]
    if len(heads) == 1:
        col = lambda n: n
    else:
        col = lambda n: 0
    return pl.pallas_call(
        functools.partial(grad_wx_kernel, plan, len(srcs), len(heads)),
        grid_spec=pltpu.PrefetchScalarGridSpec(
            num_scalar_prefetch=1, grid=(nm, len(plan)),
            in_specs=[pl.BlockSpec((tok, bm), lambda m, n, c: (0, c[0] * nm + m))]
            + [pl.BlockSpec(memory_space=pl.ANY)] * len(flat),
            out_specs=[pl.BlockSpec((bm, 8, HD), lambda m, n, c: (c[0] * nm + m, col(n), 0)) for _ in heads]
            + [pl.BlockSpec((bm, 8, HD), lambda m, n, c: (m, col(n), 0)) for _ in heads],
            scratch_shapes=[pltpu.VMEM((2, tok, 8 * HD), jnp.bfloat16), pltpu.SemaphoreType.DMA((2,))]),
        out_shape=[jax.ShapeDtypeStruct((dm, h, HD), jnp.float32) for h in heads]
        + [jax.ShapeDtypeStruct((dm // 2, h, HD), jnp.float32) for h in heads],
        compiler_params=BIG, cost_estimate=cost(tok * dm * 8 * HD * len(plan), 2 * tok * dm), name=name)(core, x, *flat)


def merge_kernel(core_ref, *refs):
    n = len(refs) // 3
    for i in range(n):
        refs[2 * n + i][...] = refs[n + i][...]


def merge(fulls, recvs, core):
    steps = 12
    n = len(fulls)

    def spec(a, mine):
        block = (a.shape[0] // steps,) + a.shape[1:]
        zeros = (0,) * (len(block) - 1)
        if mine:
            return pl.BlockSpec(block, lambda i, c: (i,) + zeros)
        return pl.BlockSpec(block, lambda i, c: ((1 - c[0]) * steps + i,) + zeros)

    return pl.pallas_call(
        merge_kernel,
        grid_spec=pltpu.PrefetchScalarGridSpec(
            num_scalar_prefetch=1, grid=(steps,),
            in_specs=[pl.BlockSpec(memory_space=pl.ANY)] * n + [spec(r, True) for r in recvs],
            out_specs=[spec(r, False) for r in recvs]),
        out_shape=[jax.ShapeDtypeStruct(f.shape, f.dtype) for f in fulls],
        input_output_aliases={1 + i: i for i in range(n)},
        cost_estimate=cost(1e10, 10 ** 8), name='merge')(core, *fulls, *recvs)


def y_kernel(idx_ref, loc_ref, rem_ref, w_ref, x_ref, y_ref, acc):
    k = pl.program_id(0)
    per = pl.num_programs(0) // 2
    nb, s, dm = x_ref.shape
    tok = nb * s
    mine = k // per == idx_ref[0]
    part = dot(jnp.where(mine, loc_ref[...].reshape(tok, -1), rem_ref[...].reshape(tok, -1)), w_ref[...], 1, 0)

    @pl.when(k == 0)
    def _():
        acc[...] = part

    @pl.when(k > 0)
    def _():
        acc[...] += part

    @pl.when(k == 2 * per - 1)
    def _():
        for b in range(nb):
            y_ref[b] = (x_ref[b].astype(jnp.float32) + acc[b * s:(b + 1) * s]).astype(jnp.bfloat16)


def out_proj(idx, o, o_rem, wo, x):
    nb, s, dm = x.shape
    wide = 768
    per = o.shape[3] // wide
    whole = pl.BlockSpec((nb, s, dm), lambda k, i: (0, 0, 0))
    return pl.pallas_call(
        y_kernel,
        grid_spec=pltpu.PrefetchScalarGridSpec(
            num_scalar_prefetch=1, grid=(2 * per,),
            in_specs=[pl.BlockSpec((1, nb, s, wide), lambda k, i: (i[1], 0, 0, lax.rem(k, per))),
                      pl.BlockSpec((nb, s, wide), lambda k, i: (0, 0, lax.rem(k, per))),
                      pl.BlockSpec((wide, dm), lambda k, i: (k, 0)), whole],
            out_specs=whole, scratch_shapes=[pltpu.VMEM((nb * s, dm), jnp.float32)]),
        out_shape=jax.ShapeDtypeStruct(x.shape, jnp.bfloat16),
        compiler_params=BIG, cost_estimate=cost(2 * nb * s * dm * dm, 2 * dm * dm), name='out_proj')(idx, o, o_rem, wo, x)


def dx_kernel(plan, n_src, idx_ref, *refs):
    srcs = refs[:2 * n_src]
    w_ref, x_ref, dy_ref, g_ref, dx_ref, dg_ref, acc = refs[2 * n_src:]
    k = pl.program_id(0)
    nb, s, dm = x_ref.shape
    for pos, pieces in enumerate(plan):
        @pl.when(k == pos)
        def _(pos=pos, pieces=pieces):
            cols = []
            for half, which, lo, hi in pieces:
                loc, rem = srcs[2 * which], srcs[2 * which + 1]
                cols.append(jnp.where(idx_ref[0] == half, loc[0, :, :, lo:hi].reshape(nb * s, hi - lo),
                                      rem[0, :, :, lo:hi].reshape(nb * s, hi - lo)))
            part = dot(jnp.concatenate(cols, axis=1), w_ref[...], 1, 1)
            if pos == 0:
                acc[...] = part
            else:
                acc[...] += part

    @pl.when(k == len(plan) - 1)
    def _():
        gain = g_ref[...].astype(jnp.float32)
        total = jnp.zeros((1, dm), jnp.float32)
        for b in range(nb):
            x32 = x_ref[b].astype(jnp.float32)
            inv = lax.rsqrt(jnp.mean(x32 * x32, axis=-1, keepdims=True) + EPS)
            unit = x32 * inv
            d_norm = acc[b * s:(b + 1) * s]
            total = total + jnp.sum(d_norm * unit, axis=0, keepdims=True)
            e = d_norm * gain
            d_x = inv * (e - unit * jnp.mean(e * unit, axis=-1, keepdims=True))
            dx_ref[b] = (dy_ref[b].astype(jnp.float32) + d_x).astype(jnp.bfloat16)
        dg_ref[...] = total


def cut(order, srcs, wide):
    plan, room = [], 0
    for half, which in order:
        lo, end = 0, srcs[which][0].shape[3]
        while lo < end:
            if room == 0:
                plan.append([])
                room = wide
            hi = min(end, lo + room)
            plan[-1].append((half, which, lo, hi))
            room -= hi - lo
            lo = hi
    return plan


def grad_x(idx, srcs, plan, wide, wcat, x, dy, gain):
    nb, s, dm = x.shape
    flat = [a for pair in srcs for a in pair]
    whole = pl.BlockSpec((nb, s, dm), lambda k, i: (0, 0, 0))
    line = pl.BlockSpec((1, dm), lambda k, i: (0, 0))
    return pl.pallas_call(
        functools.partial(dx_kernel, plan, len(srcs)),
        grid_spec=pltpu.PrefetchScalarGridSpec(
            num_scalar_prefetch=1, grid=(len(plan),),
            in_specs=[pl.BlockSpec((1, nb, s, a.shape[3]), lambda k, i: (i[1], 0, 0, 0)) for a in flat]
            + [pl.BlockSpec((dm, wide), lambda k, i: (0, k)), whole, whole, line],
            out_specs=[whole, line], scratch_shapes=[pltpu.VMEM((nb * s, dm), jnp.float32)]),
        out_shape=[jax.ShapeDtypeStruct(x.shape, jnp.bfloat16), jax.ShapeDtypeStruct((1, dm), jnp.float32)],
        compiler_params=BIG, cost_estimate=cost(2 * nb * s * dm * wide * len(plan), 2 * dm * dm),
        name='grad_x')(idx, *flat, wcat, x, dy, gain)


def solution(mesh):
    n_dev = mesh.shape['cp']
    n_chips = n_dev // 2
    pair = [(d, d ^ 1) for d in range(n_dev)]
    by_core = [[2 * p + c for c in range(2) for p in range(n_chips)]]

    def device_fn(x_in, dy_in, norm_gain, w_q, w_k, w_v, w_o):
        me = lax.axis_index('cp')
        core = me % 2
        nb, s, dm = x_in.shape
        n_heads, kv_heads = w_q.shape[1], w_k.shape[1]
        group = n_heads // kv_heads
        kvh = kv_heads // 2
        qd = n_heads * HD
        tok = n_dev * nb * s
        core_arr = core[None].astype(jnp.int32)
        chip_arr = (me // 2)[None].astype(jnp.int32)
        idx = jnp.stack([core, me]).astype(jnp.int32)

        def swap(a):
            return lax.ppermute(a, 'cp', pair)

        x32 = x_in.astype(jnp.float32)
        inv = lax.rsqrt(jnp.mean(x32 * x32, axis=-1, keepdims=True) + EPS)
        xn = (x32 * inv * norm_gain.astype(jnp.float32)).astype(jnp.bfloat16)
        own = nb * s
        xn = xn.reshape(own, dm)
        dy = dy_in.reshape(own, dm)
        xg = lax.all_gather(xn, 'cp', tiled=True)
        dyg = lax.all_gather(dy, 'cp', tiled=True)
        wcat, wh = relayout(w_q, w_k, w_v, core_arr)
        wo = w_o.reshape(qd, dm)
        near = jnp.stack([me, me ^ 1, core]).astype(jnp.int32)
        chip = me // 2
        far = [2 * lax.rem(chip + 1 + j // 2, n_chips) + j % 2 for j in range(n_dev - 2)]
        far = jnp.stack(far + [core]).astype(jnp.int32)
        qkv = proj_near(xn, swap(xn), wh, near, tok, wh.shape[1], 0, 'near_qkv')
        do = proj_near(dy, swap(dy), wo, near, tok, qd // 2, 1, 'near_do')
        qkv = proj_far(xg, wh, qkv, far, own, 0, 'far_qkv').reshape(n_dev, nb, s, -1)
        o, log2n = attn_fwd(qkv, kvh, group)
        dyg, o = lax.optimization_barrier((dyg, o))
        d_wo = lax.all_gather(grad_wo(o.reshape(tok, -1), dyg, chip_arr, n_chips), 'cp', axis_index_groups=by_core, tiled=True)
        do = proj_far(dyg, wo, do, far, own, 1, 'far_do').reshape(n_dev, nb, s, -1)
        o_rem = swap(lax.dynamic_index_in_dim(o, me ^ 1, 0, keepdims=False))
        half = kvh // 2
        first = attn_bwd(qkv, o, do, log2n, kvh, group, 0, half)
        first_rem = [swap(a) for a in first]
        second = attn_bwd(qkv, o, do, log2n, kvh, group, half, half)
        second_rem = [swap(a) for a in second]
        o_late, _ = lax.optimization_barrier((o, second[0]))
        y_out = out_proj(idx, o_late, o_rem, wo, x_in)
        rems, xg, y_out = lax.optimization_barrier((first_rem + second_rem, xg, y_out))
        pairs = list(zip(list(first) + list(second), rems))
        flat = [(a.reshape(tok, -1), b.reshape(tok, -1)) for a, b in pairs]
        wide = kv_heads * HD
        by_q = [(h, j) for h in range(2) for j in (0, 3)]
        by_k = [(h, j) for h in range(2) for j in (1, 4)]
        by_v = [(h, j) for h in range(2) for j in (2, 5)]
        wq_full, wq_send = grad_wx(xg, flat, cut(by_q, pairs, wide), (n_heads,), core_arr, 'grad_wq')
        wq_send, xg = lax.optimization_barrier((wq_send, xg))
        wq_recv = swap(wq_send)
        wk_full, wv_full, wk_send, wv_send = grad_wx(
            xg, flat, cut(by_k, pairs, wide) + cut(by_v, pairs, wide), (kv_heads, kv_heads), core_arr, 'grad_wkv')
        wk_send, wv_send, x_late = lax.optimization_barrier((wk_send, wv_send, x_in))
        wk_recv, wv_recv = swap(wk_send), swap(wv_send)
        dx_out, d_gain = grad_x(idx, pairs, cut(by_q + by_k + by_v, pairs, wide), wide, wcat, x_late, dy_in, norm_gain[None])
        d_gain = d_gain[0]
        for bit in (1, 2, 4):
            d_gain = d_gain + lax.ppermute(d_gain, 'cp', [(d, d ^ bit) for d in range(n_dev)])
        wq_recv, wk_recv, wv_recv, dx_out = lax.optimization_barrier((wq_recv, wk_recv, wv_recv, dx_out))
        d_wq, d_wk, d_wv = merge((wq_full, wk_full, wv_full), (wq_recv, wk_recv, wv_recv), core_arr)
        d_wo = d_wo.reshape(n_heads, HD, dm)
        return y_out, dx_out, d_gain, d_wq, d_wk, d_wv, d_wo

    act_spec = P('dp', 'cp', None)
    mat_spec = P(None, None, None)
    grad_spec = P('dp', None, None)
    return jax.shard_map(device_fn, mesh=mesh,
                         in_specs=(act_spec, act_spec, P(None), mat_spec, mat_spec, mat_spec, mat_spec),
                         out_specs=(act_spec, act_spec, P('dp'), grad_spec, grad_spec, grad_spec, grad_spec),
                         check_vma=False)
```

time: 2400 us -> 688 us (0.29)
  waiting for transfers between devices: 1750 us -> 110 us
  Pallas kernels: 0 us -> 502 us
  local copies, waits for them, and re-layouts: 258 us -> 35.5 us
  matrix products: 170 us -> 0 us
  starting transfers between devices: 116 us -> 5.65 us
  blocking collectives: 44.5 us -> 0 us
    psum x1 -> x0, waiting for transfers between devices: 1030 us -> none  [device_fn(): lax.psum((d_gain, d_wq, d_wk, d_wv, d_wo), 'cp')]
    ppermute x44 -> x15, waiting for transfers between devices: 718 us -> 27.9 us  [the longest x12 21 us: swap(): return lax.ppermute(a, 'cp', pair)]
    pallas_call x0 -> x14, Pallas kernels: none -> 502 us  [the longest x2 98.7 us: attn_bwd(): pl.pallas_call(functools.partial(bwd_kernel, 256), grid=(nb, count), in_s...]
    dot_general x18 -> x0, matrix products: 170 us -> none  [the longest x1 19.2 us: device_fn(): jnp.einsum('duo,dujf->ojf', x_norm, d_query_b, preferred_element_type=jnp...]
    while x45 -> x0, local copies, waits for them, and re-layouts: 121 us -> none
    ppermute x44 -> x15, starting transfers between devices: 116 us -> 5.53 us  [the longest x12 3.85 us: swap(): return lax.ppermute(a, 'cp', pair)]
    all_gather x0 -> x3, waiting for transfers between devices: none -> 81.3 us  [the longest x1 64.1 us: device_fn(): xg = lax.all_gather(xn, 'cp', tiled=True)]
    unnamed x57 -> x15, local copies, waits for them, and re-layouts: 106 us -> 32.8 us
  transfers between devices with their start and end apart: 45 -> 18, of which waited for: 29 -> 7; matrix products, arithmetic and copies ran while one was open for 7% -> 1% of each run, Pallas kernels for 0% -> 72%
where the time goes in v1:
time: 688 us; the launch traced here: 678 us
  Pallas kernels  502 us (73%)
  waiting for transfers between devices  110 us (16%)
  local copies, waits for them, and re-layouts  35.5 us (5%)
  between operations  14.2 us (2%)
  other arithmetic  10.6 us (2%)
    pallas_call x2, Pallas kernels, attn_bwd(): pl.pallas_call(functools.partial(bwd_kernel, 256), grid=(nb, count), in_s...  98.7 us
    pallas_call x2, Pallas kernels, grad_wx(): pl.pallas_call(functools.partial(grad_wx_kernel, plan, len(srcs), len(hea...  97.1 us
    pallas_call x2, Pallas kernels, proj_far(): pl.pallas_call(functools.partial(far_kernel, cb), grid_spec=pltpu.Prefetc...  95.2 us
    all_gather x1, waiting for transfers between devices, device_fn(): xg = lax.all_gather(xn, 'cp', tiled=True)  64.1 us
    pallas_call x1, Pallas kernels, attn_fwd(): pl.pallas_call(functools.partial(fwd_kernel, 128), grid=(nb, kvh), in_spe...  48.8 us
    pallas_call x2, Pallas kernels, proj_near(): pl.pallas_call(functools.partial(near_kernel, cb), grid_spec=pltpu.Prefet...  40.2 us
    unnamed x15, local copies, waits for them, and re-layouts  32.8 us
    pallas_call x1, Pallas kernels, relayout(): pl.pallas_call(relayout_kernel, grid_spec=pltpu.PrefetchScalarGridSpec(nu...  32.7 us
  transfers between devices with their start and end apart: 18, of which 7 were waited for; matrix products, arithmetic and copies ran while one was open for 1% of the time, Pallas kernels for 72%

profile of v1, /device:TPU:0, one launch (start us, length us, event | category | flops | bytes accessed | tf_op | source)
XLA Modules:
  0.0 677.7 jit_solution(14251369088707108303)
XLA Ops:
  7.2 0.0 all-gather.4.cloned.1.call-start
  7.2 0.7 convert_element_type.10
  7.9 2.6 fusion
  10.5 4.8 fusion.2
  15.3 0.0 all-gather.4.cloned.1.call-update
  15.3 0.0 all-gather.6.cloned.1.call-start
  15.3 0.7 all-gather.6.cloned.1.call-update
  16.0 0.0 all-gather.8.cloned.1.call-start
  16.1 1.1 copy-done.1
  17.1 0.7 collective-permute-start
  17.9 0.6 stack.46.tbl_ref
  18.5 0.6 pad_add_fusion.tbl_ref
  19.1 32.7 %relayout.1 = (bf16[3072,5120]{1,0:T(8,128)(2,1)}, bf16[3072,2560]{1,0:T(8,128)(2,1)}) custom-call(s32[1]{0:T(128)} %bitcast.6.core_ref, bf16[3072,24,128]{2,1,0:T(8,128)(2,1)} %wq_ref.1, bf16[3072,8,128]{2,1,0:T(8,128)(2,1)} %wk_ref.1, bf16[3072,8,128]{2,1,0:T(8,128)(2,1)} %wv_ref.1), custom_call_target="tpu_custom_call" | custom-call | flops 10000000000 | bytes 62914560 | tf_op jit(solution)/shard_map/relayout/pallas_call | solution.py:47
  51.9 0.0 collective-permute-done.b_ref
  51.9 23.7 %near_qkv.1.old_ref = bf16[4096,2560]{1,0:T(8,128)(2,1)} custom-call(s32[3]{0:T(128)} %pad_add_fusion.tbl_ref, bf16[512,3072]{1,0:T(8,128)(2,1)} %bitcast.43, bf16[512,3072]{1,0:T(8,128)(2,1)} %collective-permute-done.b_ref, bf16[3072,2560]{1,0:T(8,128)(2,1)} %get-tuple-element.48.w_ref), custom_call_target="tpu_custom_call" | custom-call | flops 16106127360 | bytes 15728640 | tf_op jit(solution)/shard_map/near_qkv/pallas_call | solution.py:79
  75.6 64.1 %all-gather.4.cloned.1.call-done.a_ref = bf16[4096,3072]{1,0:T(8,128)(2,1)} async-done(((bf16[512,3072]{1,0:T(8,128)(2,1)}), bf16[4096,3072]{1,0:T(8,128)(2,1)}) %all-gather.4.cloned.1.call-update) | async-done | bytes 25165840 | tf_op jit(solution)/shard_map/all_gather | solution.py:489
  139.7 57.3 %far_qkv.1 = bf16[4096,2560]{1,0:T(8,128)(2,1)} custom-call(s32[7]{0:T(128)} %stack.46.tbl_ref, bf16[4096,3072]{1,0:T(8,128)(2,1)} %all-gather.4.cloned.1.call-done.a_ref, bf16[3072,2560]{1,0:T(8,128)(2,1)} %get-tuple-element.48.w_ref, bf16[4096,2560]{1,0:T(8,128)(2,1)} %near_qkv.1.old_ref), custom_call_target="tpu_custom_call", output_to_operand_aliasing={{}: (3, {})} | custom-call | flops 48318382080 | bytes 25165824 | tf_op jit(solution)/shard_map/far_qkv/pallas_call | solution.py:93
  197.1 48.8 %attn_fwd.1 = (bf16[8,4,128,1536]{3,2,1,0:T(8,128)(2,1)}, f32[4,12,1,1024]{3,2,1,0:T(1,128)}) custom-call(bf16[8,4,128,2560]{3,2,1,0:T(8,128)(2,1)} %bitcast.61, bf16[8,4,128,2560]{3,2,1,0:T(8,128)(2,1)} %bitcast.62, bf16[8,4,128,2560]{3,2,1,0:T(8,128)(2,1)} %bitcast.63), custom_call_target="tpu_custom_call" | custom-call | flops 25769803776 | bytes 10000000 | tf_op jit(solution)/shard_map/attn_fwd/pallas_call | solution.py:153
  245.9 17.1 %all-gather.6.cloned.1.call-done.a_ref.b_ref = bf16[4096,3072]{1,0:T(8,128)(2,1)} async-done(((bf16[512,3072]{1,0:T(8,128)(2,1)}), bf16[4096,3072]{1,0:T(8,128)(2,1)}) %all-gather.6.cloned.1.call-update) | async-done | bytes 25165840 | tf_op jit(solution)/shard_map/all_gather | solution.py:490
  263.1 16.8 %grad_wo.1 = f32[384,3072]{1,0:T(8,128)} custom-call(s32[1]{0:T(128)} %bitcast.28.chip_ref, bf16[4096,1536]{1,0:T(8,128)(2,1)} %bitcast.35, bf16[4096,3072]{1,0:T(8,128)(2,1)} %all-gather.6.cloned.1.call-done.a_ref.b_ref), custom_call_target="tpu_custom_call" | custom-call | flops 9663676416 | bytes 25165824 | tf_op jit(solution)/shard_map/grad_wo/pallas_call | solution.py:247
  279.9 0.0 all-gather.8.cloned.1.call-update
  279.9 0.3 collective-permute-start.1
  280.2 5.4 collective-permute-done.1.b_ref
  285.6 1.7 copy-done.2
  287.3 16.4 %near_do.1.old_ref = bf16[4096,1536]{1,0:T(8,128)(2,1)} custom-call(s32[3]{0:T(128)} %pad_add_fusion.tbl_ref, bf16[512,3072]{1,0:T(8,128)(2,1)} %bitcast.38, bf16[512,3072]{1,0:T(8,128)(2,1)} %copy-done.2, bf16[3072,3072]{1,0:T(8,128)(2,1)} %bitcast.32), custom_call_target="tpu_custom_call" | custom-call | flops 9663676416 | bytes 9437184 | tf_op jit(solution)/shard_map/near_do/pallas_call | solution.py:79
  303.7 37.8 %far_do.1 = bf16[4096,1536]{1,0:T(8,128)(2,1)} custom-call(s32[7]{0:T(128)} %stack.46.tbl_ref, bf16[4096,3072]{1,0:T(8,128)(2,1)} %all-gather.6.cloned.1.call-done.a_ref.b_ref, bf16[3072,3072]{1,0:T(8,128)(2,1)} %bitcast.33, bf16[4096,1536]{1,0:T(8,128)(2,1)} %near_do.1.old_ref), custom_call_target="tpu_custom_call", output_to_operand_aliasing={{}: (3, {})} | custom-call | flops 28991029248 | bytes 25165824 | tf_op jit(solution)/shard_map/far_do/pallas_call | solution.py:93
  341.5 49.1 %attn_bwd.2 = (bf16[8,4,128,768]{3,2,1,0:T(8,128)(2,1)}, bf16[8,4,128,256]{3,2,1,0:T(8,128)(2,1)}, bf16[8,4,128,256]{3,2,1,0:T(8,128)(2,1)}) custom-call(bf16[8,4,128,2560]{3,2,1,0:T(8,128)(2,1)} %bitcast.64, bf16[8,4,128,2560]{3,2,1,0:T(8,128)(2,1)} %bitcast.65, bf16[8,4,128,2560]{3,2,1,0:T(8,128)(2,1)} %bitcast.66, ...), custom_call_target="tpu_custom_call" | custom-call | flops 32212254720 | bytes 10000000 | tf_op jit(solution)/shard_map/attn_bwd/pallas_call | solution.py:223
  390.6 0.3 collective-permute-start.2
  390.9 49.5 %attn_bwd.3 = (bf16[8,4,128,768]{3,2,1,0:T(8,128)(2,1)}, bf16[8,4,128,256]{3,2,1,0:T(8,128)(2,1)}, bf16[8,4,128,256]{3,2,1,0:T(8,128)(2,1)}) custom-call(bf16[8,4,128,2560]{3,2,1,0:T(8,128)(2,1)} %bitcast.67, bf16[8,4,128,2560]{3,2,1,0:T(8,128)(2,1)} %bitcast.68, bf16[8,4,128,2560]{3,2,1,0:T(8,128)(2,1)} %bitcast.69, ...), custom_call_target="tpu_custom_call" | custom-call | flops 32212254720 | bytes 10000000 | tf_op jit(solution)/shard_map/attn_bwd/pallas_call | solution.py:223
  440.5 0.3 collective-permute-start.5
  440.7 0.2 collective-permute-start.3
  441.0 1.5 dynamic-slice_bitcast_fusion
  442.5 0.3 collective-permute-start.8
  442.8 0.2 collective-permute-start.4
  443.0 15.5 %collective-permute-done.8.rem_ref = bf16[4,128,1536]{2,1,0:T(8,128)(2,1)S(1)} collective-permute-done((bf16[4,128,1536]{2,1,0:T(8,128)(2,1)S(1)}, bf16[4,128,1536]{2,1,0:T(8,128)(2,1)S(1)}, u32[]{:S(2)}, u32[]{:S(2)}) %collective-permute-start.8) | collective-permute-done | bytes 1572896 | tf_op jit(solution)/shard_map/ppermute | solution.py:481
  458.6 0.4 collective-permute-start.6
  459.0 0.8 copy-done.5
  459.7 0.4 collective-permute-start.7
  460.1 0.6 pad_add_fusion.1.idx_ref
  460.7 19.6 %out_proj.1 = bf16[4,128,3072]{2,1,0:T(8,128)(2,1)} custom-call(s32[2]{0:T(128)} %pad_add_fusion.1.idx_ref, bf16[8,4,128,1536]{3,2,1,0:T(8,128)(2,1)} %get-tuple-element.59.o_ref.loc_ref, bf16[4,128,1536]{2,1,0:T(8,128)(2,1)} %copy-done.5, bf16[3072,3072]{1,0:T(8,128)(2,1)} %bitcast.34, bf16[4,128,3072]{2,1,0:T(8,128)(2,1)} %refs_13_), custom_call_target="tpu_custom_call" | custom-call | flops 9663676416 | bytes 18874368 | tf_op jit(solution)/shard_map/out_proj/pallas_call | solution.py:382
  480.3 0.0 collective-permute-done.6.refs_9_
  480.3 0.0 collective-permute-done.7.refs_11_
  480.4 0.0 collective-permute-done.2.refs_1_
  480.4 1.4 copy-done.4
  481.7 53.3 %grad_wq.1 = (f32[3072,24,128]{2,1,0:T(8,128)}, f32[1536,24,128]{2,1,0:T(8,128)}) custom-call(s32[1]{0:T(128)} %bitcast.6.core_ref, bf16[4096,3072]{1,0:T(8,128)(2,1)} %all-gather.4.cloned.1.call-done.a_ref, bf16[4096,768]{1,0:T(8,128)(2,1)} %bitcast.45, bf16[4096,768]{1,0:T(8,128)(2,1)} %bitcast.16.refs_1_, bf16[4096,256]{1,0:T(8,128)(2,1)} %bitcast.49, ...), custom_call_target="tpu_custom_call" | custom-call | flops 38654705664 | bytes 25165824 | tf_op jit(solution)/shard_map/grad_wq/pallas_call | solution.py:313
  535.1 0.0 copy-start.6
  535.1 0.2 collective-permute-start.9
  535.3 43.8 %grad_wkv.1 = (f32[3072,8,128]{2,1,0:T(8,128)}, f32[3072,8,128]{2,1,0:T(8,128)}, f32[1536,8,128]{2,1,0:T(8,128)}, f32[1536,8,128]{2,1,0:T(8,128)}) custom-call(s32[1]{0:T(128)} %bitcast.6.core_ref, bf16[4096,3072]{1,0:T(8,128)(2,1)} %all-gather.4.cloned.1.call-done.a_ref, bf16[4096,768]{1,0:T(8,128)(2,1)} %bitcast.46, bf16[4096,768]{1,0:T(8,128)(2,1)} %bitcast.16.refs_1_, ...), custom_call_target="tpu_custom_call" | custom-call | flops 25769803776 | bytes 25165824 | tf_op jit(solution)/shard_map/grad_wkv/pallas_call | solution.py:313
  579.1 0.4 collective-permute-start.10
  579.5 0.1 collective-permute-start.11
  579.6 0.6 broadcast_in_dim.4.refs_15_
  580.2 29.0 %grad_x.1 = (bf16[4,128,3072]{2,1,0:T(8,128)(2,1)}, f32[1,3072]{1,0:T(1,128)}) custom-call(s32[2]{0:T(128)} %pad_add_fusion.1.idx_ref, bf16[8,4,128,768]{3,2,1,0:T(8,128)(2,1)} %get-tuple-element.53.refs_0_, bf16[8,4,128,768]{3,2,1,0:T(8,128)(2,1)} %collective-permute-done.2.refs_1_, bf16[8,4,128,256]{3,2,1,0:T(8,128)(2,1)} %get-tuple-element.54.refs_2_, ...), custom_call_target="tpu_custom_call" | custom-call | flops 16106127360 | bytes 18874368 | tf_op jit(solution)/shard_map/grad_x/pallas_call | solution.py:449
  609.2 0.2 collective-permute-start.12
  609.4 1.0 collective-permute-done.12
  610.4 0.7 add.68
  611.1 1.4 collective-permute-start.13
  612.5 2.3 collective-permute-done.13
  614.8 0.1 collective-permute-start.14
  614.9 3.6 collective-permute-done.14
  618.5 0.6 add.70
  619.1 0.0 collective-permute-done.10.refs_4_
  619.1 0.0 collective-permute-done.11.refs_5_
  619.1 23.8 %merge.1 = (f32[3072,24,128]{2,1,0:T(8,128)}, f32[3072,8,128]{2,1,0:T(8,128)}, f32[3072,8,128]{2,1,0:T(8,128)}) custom-call(s32[1]{0:T(128)} %bitcast.6.core_ref, f32[3072,24,128]{2,1,0:T(8,128)} %get-tuple-element.80.refs_0_, f32[3072,8,128]{2,1,0:T(8,128)} %get-tuple-element.81.refs_1_, ...), custom_call_target="tpu_custom_call", output_to_operand_aliasing={{0}: (1, {}), {1}: (2, {}), {2}: (3, {})} | custom-call | flops 10000000000 | bytes 100000000 | tf_op jit(solution)/shard_map/merge/pallas_call | solution.py:344
  642.9 27.9 %copy.25 = f32[24,128,3072]{2,1,0:T(8,128)} copy(f32[24,128,3072]{2,1,0:T(8,128)} %bitcast.36) | data formatting | bytes 75497472
  (16 shorter events, 0.0 us)
Async XLA Ops:
  7.2 132.6 %all-gather.4.cloned.1.call-start = ((), (), s32[]{:S(2)}) async-start(), calls=%async_computation | async-start | bytes 28311552 | tf_op jit(solution)/shard_map/all_gather | solution.py:489
  15.3 1.9 copy-start.1
  15.3 247.8 %all-gather.6.cloned.1.call-start = ((), (), s32[]{:S(2)}) async-start(), calls=%async_computation.1 | async-start | bytes 28311552 | tf_op jit(solution)/shard_map/all_gather | solution.py:490
  16.0 626.9 %all-gather.8.cloned.1.call-start = ((), (), s32[]{:S(2)}) async-start(), calls=%async_computation.2 | async-start | bytes 42467328 | tf_op jit(solution)/shard_map/all_gather | solution.py:502
  17.1 34.7 %collective-permute-start = (bf16[512,3072]{1,0:T(8,128)(2,1)S(1)}, bf16[512,3072]{1,0:T(8,128)(2,1)}, u32[]{:S(2)}, u32[]{:S(2)}) collective-permute-start(bf16[512,3072]{1,0:T(8,128)(2,1)S(1)} %bitcast.44), channel_id=1, source_target_pairs={{0,1},{1,0},{2,3},{3,2},{4,5},{5,4},{6,7},{7,6},{8,9},{9,8},{10,11... | collective-permute-start | bytes 9437192 | tf_op jit(solution)/shard_map/ppermute | solution.py:481
  263.1 16.8 %copy-start = (bf16[4,128,3072]{2,1,0:T(8,128)(2,1)S(1)}, bf16[4,128,3072]{2,1,0:T(8,128)(2,1)}, u32[]{:S(2)}) copy-start(bf16[4,128,3072]{2,1,0:T(8,128)(2,1)} %refs_14_.1) | copy-start | bytes 9437188
  279.9 5.7 collective-permute-start.1
  285.6 1.7 copy-start.2
  390.6 50.1 %copy-start.3 = (bf16[8,4,128,256]{3,2,1,0:T(8,128)(2,1)S(1)}, bf16[8,4,128,256]{3,2,1,0:T(8,128)(2,1)}, u32[]{:S(2)}) copy-start(bf16[8,4,128,256]{3,2,1,0:T(8,128)(2,1)} %get-tuple-element.54.refs_2_) | copy-start | bytes 6291460
  390.6 89.7 %collective-permute-start.2 = (bf16[8,4,128,768]{3,2,1,0:T(8,128)(2,1)}, bf16[8,4,128,768]{3,2,1,0:T(8,128)(2,1)}, u32[]{:S(2)}, u32[]{:S(2)}) collective-permute-start(bf16[8,4,128,768]{3,2,1,0:T(8,128)(2,1)} %get-tuple-element.53.refs_0_), channel_id=1, source_target_pairs={{0,1},{1,0},{2,3},{3,2},{4,5},{5,4},{6,7},{7,6},{8,9},{9,8},{10,11... | collective-permute-start | bytes 18874376 | tf_op jit(solution)/shard_map/ppermute | solution.py:481
  440.5 39.9 %collective-permute-start.5 = (bf16[8,4,128,768]{3,2,1,0:T(8,128)(2,1)}, bf16[8,4,128,768]{3,2,1,0:T(8,128)(2,1)}, u32[]{:S(2)}, u32[]{:S(2)}) collective-permute-start(bf16[8,4,128,768]{3,2,1,0:T(8,128)(2,1)} %get-tuple-element.56.refs_6_), channel_id=1, source_target_pairs={{0,1},{1,0},{2,3},{3,2},{4,5},{5,4},{6,7},{7,6},{8,9},{9,8},{10,11... | collective-permute-start | bytes 18874376 | tf_op jit(solution)/shard_map/ppermute | solution.py:481
  440.7 18.2 %collective-permute-start.3 = (bf16[8,4,128,256]{3,2,1,0:T(8,128)(2,1)S(1)}, bf16[8,4,128,256]{3,2,1,0:T(8,128)(2,1)}, u32[]{:S(2)}, u32[]{:S(2)}) collective-permute-start(bf16[8,4,128,256]{3,2,1,0:T(8,128)(2,1)S(1)} %copy-done.3), channel_id=1, source_target_pairs={{0,1},{1,0},{2,3},{3,2},{4,5},{5,4},{6,7},{7,6},{8,9},{9,8},{10,11... | collective-permute-start | bytes 6291464 | tf_op jit(solution)/shard_map/ppermute | solution.py:481
  442.5 16.1 %collective-permute-start.8 = (bf16[4,128,1536]{2,1,0:T(8,128)(2,1)S(1)}, bf16[4,128,1536]{2,1,0:T(8,128)(2,1)S(1)}, u32[]{:S(2)}, u32[]{:S(2)}) collective-permute-start(bf16[4,128,1536]{2,1,0:T(8,128)(2,1)S(1)} %dynamic-slice_bitcast_fusion), channel_id=1, source_target_pairs={{0,1},{1,0},{2,3},{3,2},{4,5},{5,4},{6,7},{7,6},{8,9},{9,8},{10,11... | collective-permute-start | bytes 4718600 | tf_op jit(solution)/shard_map/ppermute | solution.py:481
  442.8 37.5 %collective-permute-start.4 = (bf16[8,4,128,256]{3,2,1,0:T(8,128)(2,1)}, bf16[8,4,128,256]{3,2,1,0:T(8,128)(2,1)}, u32[]{:S(2)}, u32[]{:S(2)}) collective-permute-start(bf16[8,4,128,256]{3,2,1,0:T(8,128)(2,1)} %get-tuple-element.55.refs_4_), channel_id=1, source_target_pairs={{0,1},{1,0},{2,3},{3,2},{4,5},{5,4},{6,7},{7,6},{8,9},{9,8},{10,11... | collective-permute-start | bytes 6291464 | tf_op jit(solution)/shard_map/ppermute | solution.py:481
  458.6 1.1 copy-start.5
  458.6 21.8 %collective-permute-start.6 = (bf16[8,4,128,256]{3,2,1,0:T(8,128)(2,1)}, bf16[8,4,128,256]{3,2,1,0:T(8,128)(2,1)}, u32[]{:S(2)}, u32[]{:S(2)}) collective-permute-start(bf16[8,4,128,256]{3,2,1,0:T(8,128)(2,1)} %get-tuple-element.57.refs_8_), channel_id=1, source_target_pairs={{0,1},{1,0},{2,3},{3,2},{4,5},{5,4},{6,7},{7,6},{8,9},{9,8},{10,11... | collective-permute-start | bytes 6291464 | tf_op jit(solution)/shard_map/ppermute | solution.py:481
  459.7 20.6 %collective-permute-start.7 = (bf16[8,4,128,256]{3,2,1,0:T(8,128)(2,1)}, bf16[8,4,128,256]{3,2,1,0:T(8,128)(2,1)S(1)}, u32[]{:S(2)}, u32[]{:S(2)}) collective-permute-start(bf16[8,4,128,256]{3,2,1,0:T(8,128)(2,1)} %get-tuple-element.58.refs_10_), channel_id=1, source_target_pairs={{0,1},{1,0},{2,3},{3,2},{4,5},{5,4},{6,7},{7,6},{8,9},{9,8},{10,11... | collective-permute-start | bytes 6291464 | tf_op jit(solution)/shard_map/ppermute | solution.py:481
  480.4 1.4 copy-start.4
  535.1 44.6 %copy-start.6 = (bf16[3072]{0:T(1024)(128)(2,1)S(1)}, bf16[3072]{0:T(1024)(128)(2,1)}, u32[]{:S(2)}) copy-start(bf16[3072]{0:T(1024)(128)(2,1)} %param.9) | copy-start | bytes 18436
  535.1 84.0 %collective-permute-start.9 = (f32[1536,24,128]{2,1,0:T(8,128)}, f32[1536,24,128]{2,1,0:T(8,128)}, u32[]{:S(2)}, u32[]{:S(2)}) collective-permute-start(f32[1536,24,128]{2,1,0:T(8,128)} %get-tuple-element.69), channel_id=1, source_target_pairs={{0,1},{1,0},{2,3},{3,2},{4,5},{5,4},{6,7},{7,6},{8,9},{9,8},{10,11... | collective-permute-start | bytes 56623112 | tf_op jit(solution)/shard_map/ppermute | solution.py:481
  579.1 40.0 %collective-permute-start.10 = (f32[1536,8,128]{2,1,0:T(8,128)}, f32[1536,8,128]{2,1,0:T(8,128)}, u32[]{:S(2)}, u32[]{:S(2)}) collective-permute-start(f32[1536,8,128]{2,1,0:T(8,128)} %get-tuple-element.73), channel_id=1, source_target_pairs={{0,1},{1,0},{2,3},{3,2},{4,5},{5,4},{6,7},{7,6},{8,9},{9,8},{10,11... | collective-permute-start | bytes 18874376 | tf_op jit(solution)/shard_map/ppermute | solution.py:481
  579.5 39.6 %collective-permute-start.11 = (f32[1536,8,128]{2,1,0:T(8,128)}, f32[1536,8,128]{2,1,0:T(8,128)}, u32[]{:S(2)}, u32[]{:S(2)}) collective-permute-start(f32[1536,8,128]{2,1,0:T(8,128)} %get-tuple-element.74), channel_id=1, source_target_pairs={{0,1},{1,0},{2,3},{3,2},{4,5},{5,4},{6,7},{7,6},{8,9},{9,8},{10,11... | collective-permute-start | bytes 18874376 | tf_op jit(solution)/shard_map/ppermute | solution.py:481
  609.2 1.2 collective-permute-start.12
  611.1 3.7 collective-permute-start.13
  614.8 3.7 collective-permute-start.14
Sparse Core Ops, SparseCore 0:
  15.4 124.2 all-gather.3
  141.6 121.4 all-gather.5
  280.0 178.3 all-gather.7

commit v2 on v1

--- a/solution.py
+++ b/solution.py
@@ -163,7 +163,7 @@
         name='attn_fwd')(qkv, qkv, qkv)
 
 
-def bwd_kernel(rows, q_ref, k_ref, v_ref, o_ref, do_ref, l_ref, dq_ref, dk_ref, dv_ref, dq_acc):
+def bwd_kernel(rows, q_ref, k_ref, v_ref, o_ref, do_ref, l_ref, d_ref, dq_acc):
     n, _, blk, width = q_ref.shape
     group, seq, nblk = width // HD, n * blk, rows // blk
     scale = HD ** -0.5
@@ -207,10 +207,11 @@
             dq_acc[g, k0:] += dq_c
         dv_t, dk_t = (dv_c, dk_c) if g == 0 else (dv_t + dv_c, dk_t + dk_c)
         if g == group - 1:
-            dk_ref[kb * nblk:(kb + 1) * nblk, 0] = dk_t.astype(jnp.bfloat16).reshape(nblk, blk, HD)
-            dv_ref[kb * nblk:(kb + 1) * nblk, 0] = dv_t.astype(jnp.bfloat16).reshape(nblk, blk, HD)
+            for j, total in enumerate((dk_t, dv_t)):
+                cols = slice(width + j * HD, width + (j + 1) * HD)
+                d_ref[kb * nblk:(kb + 1) * nblk, 0, :, cols] = total.astype(jnp.bfloat16).reshape(nblk, blk, HD)
     for g in range(group):
-        dq_ref[:, 0, :, g * HD:(g + 1) * HD] = dq_acc[g].astype(jnp.bfloat16).reshape(n, blk, HD)
+        d_ref[:, 0, :, g * HD:(g + 1) * HD] = dq_acc[g].astype(jnp.bfloat16).reshape(n, blk, HD)
 
 
 def attn_bwd(qkv, o, do, log2n, kvh, group, h0, count):
@@ -218,8 +219,7 @@
     width = group * HD
     first = kvh * group
     q_in = pl.BlockSpec((n, 1, s, width), lambda b, h: (0, b, 0, h0 + h))
-    q_out = pl.BlockSpec((n, 1, s, width), lambda b, h: (0, b, 0, h))
-    k_out = pl.BlockSpec((n, 1, s, HD), lambda b, h: (0, b, 0, h))
+    out = width + 2 * HD
     return pl.pallas_call(
         functools.partial(bwd_kernel, 256), grid=(nb, count),
         in_specs=[q_in,
@@ -227,10 +227,8 @@
                   pl.BlockSpec((n, 1, s, HD), lambda b, h: (0, b, 0, first + kvh + h0 + h)),
                   q_in, q_in,
                   pl.BlockSpec((1, group, 1, n * s), lambda b, h: (b, h0 + h, 0, 0))],
-        out_specs=[q_out, k_out, k_out],
-        out_shape=[jax.ShapeDtypeStruct((n, nb, s, count * width), jnp.bfloat16),
-                   jax.ShapeDtypeStruct((n, nb, s, count * HD), jnp.bfloat16),
-                   jax.ShapeDtypeStruct((n, nb, s, count * HD), jnp.bfloat16)],
+        out_specs=pl.BlockSpec((n, 1, s, out), lambda b, h: (0, b, 0, h)),
+        out_shape=jax.ShapeDtypeStruct((n, nb, s, count * out), jnp.bfloat16),
         scratch_shapes=[pltpu.VMEM((group, n * s, HD), jnp.float32)],
         compiler_params=BIG, cost_estimate=cost(nb * count * group * 10 * (n * s) ** 2 * HD, 10 ** 7),
         name='attn_bwd')(qkv, qkv, qkv, o, do, log2n)
@@ -325,12 +323,12 @@
 
 
 def merge_kernel(core_ref, *refs):
-    n = len(refs) // 3
-    for i in range(n):
-        refs[2 * n + i][...] = refs[n + i][...]
-
-
-def merge(fulls, recvs, core):
+    n = (len(refs) - 2) // 3
+    for i in range(n + 1):
+        refs[2 * n + 1 + i][...] = refs[n + i][...]
+
+
+def merge(fulls, recvs, gathered, core):
     steps = 12
     n = len(fulls)
 
@@ -345,11 +343,11 @@
         merge_kernel,
         grid_spec=pltpu.PrefetchScalarGridSpec(
             num_scalar_prefetch=1, grid=(steps,),
-            in_specs=[pl.BlockSpec(memory_space=pl.ANY)] * n + [spec(r, True) for r in recvs],
-            out_specs=[spec(r, False) for r in recvs]),
-        out_shape=[jax.ShapeDtypeStruct(f.shape, f.dtype) for f in fulls],
+            in_specs=[pl.BlockSpec(memory_space=pl.ANY)] * n + [spec(r, True) for r in recvs] + [spec(gathered, True)],
+            out_specs=[spec(r, False) for r in recvs] + [spec(gathered, True)]),
+        out_shape=[jax.ShapeDtypeStruct(f.shape, f.dtype) for f in fulls] + [jax.ShapeDtypeStruct(gathered.shape, gathered.dtype)],
         input_output_aliases={1 + i: i for i in range(n)},
-        cost_estimate=cost(1e10, 10 ** 8), name='merge')(core, *fulls, *recvs)
+        compiler_params=BIG, cost_estimate=cost(1e10, 10 ** 8), name='merge')(core, *fulls, *recvs, gathered)
 
 
 def y_kernel(idx_ref, loc_ref, rem_ref, w_ref, x_ref, y_ref, acc):
@@ -426,10 +424,9 @@
         dg_ref[...] = total
 
 
-def cut(order, srcs, wide):
+def cut(spans, wide):
     plan, room = [], 0
-    for half, which in order:
-        lo, end = 0, srcs[which][0].shape[3]
+    for half, which, lo, end in spans:
         while lo < end:
             if room == 0:
                 plan.append([])
@@ -496,39 +493,50 @@
         far = jnp.stack(far + [core]).astype(jnp.int32)
         qkv = proj_near(xn, swap(xn), wh, near, tok, wh.shape[1], 0, 'near_qkv')
         do = proj_near(dy, swap(dy), wo, near, tok, qd // 2, 1, 'near_do')
+        qkv, do, xg = lax.optimization_barrier((qkv, do, xg))
         qkv = proj_far(xg, wh, qkv, far, own, 0, 'far_qkv').reshape(n_dev, nb, s, -1)
         o, log2n = attn_fwd(qkv, kvh, group)
-        dyg, o = lax.optimization_barrier((dyg, o))
+        o_rem = swap(lax.dynamic_index_in_dim(o, me ^ 1, 0, keepdims=False))
+        y_out = out_proj(idx, o, o_rem, wo, x_in)
+        dyg, o, y_out = lax.optimization_barrier((dyg, o, y_out))
         d_wo = lax.all_gather(grad_wo(o.reshape(tok, -1), dyg, chip_arr, n_chips), 'cp', axis_index_groups=by_core, tiled=True)
         do = proj_far(dyg, wo, do, far, own, 1, 'far_do').reshape(n_dev, nb, s, -1)
-        o_rem = swap(lax.dynamic_index_in_dim(o, me ^ 1, 0, keepdims=False))
-        half = kvh // 2
-        first = attn_bwd(qkv, o, do, log2n, kvh, group, 0, half)
-        first_rem = [swap(a) for a in first]
-        second = attn_bwd(qkv, o, do, log2n, kvh, group, half, half)
-        second_rem = [swap(a) for a in second]
-        o_late, _ = lax.optimization_barrier((o, second[0]))
-        y_out = out_proj(idx, o_late, o_rem, wo, x_in)
-        rems, xg, y_out = lax.optimization_barrier((first_rem + second_rem, xg, y_out))
-        pairs = list(zip(list(first) + list(second), rems))
+        most = kvh - 1
+        first = attn_bwd(qkv, o, do, log2n, kvh, group, 0, most)
+        first_rem = swap(first)
+        second = attn_bwd(qkv, o, do, log2n, kvh, group, most, kvh - most)
+        second_rem = swap(second)
+        first_rem, second_rem, xg = lax.optimization_barrier((first_rem, second_rem, xg))
+        pairs = [(first, first_rem), (second, second_rem)]
         flat = [(a.reshape(tok, -1), b.reshape(tok, -1)) for a, b in pairs]
         wide = kv_heads * HD
-        by_q = [(h, j) for h in range(2) for j in (0, 3)]
-        by_k = [(h, j) for h in range(2) for j in (1, 4)]
-        by_v = [(h, j) for h in range(2) for j in (2, 5)]
-        wq_full, wq_send = grad_wx(xg, flat, cut(by_q, pairs, wide), (n_heads,), core_arr, 'grad_wq')
+
+        def columns(lo, hi):
+            spans = []
+            for h in range(2):
+                for j in range(kvh):
+                    base = (j % most) * (group + 2) * HD
+                    spans.append((h, j // most, base + lo * HD, base + hi * HD))
+            return spans
+
+        by_q, by_k, by_v = columns(0, group), columns(group, group + 1), columns(group + 1, group + 2)
+        wq_full, wq_send = grad_wx(xg, flat, cut(by_q, wide), (n_heads,), core_arr, 'grad_wq')
         wq_send, xg = lax.optimization_barrier((wq_send, xg))
         wq_recv = swap(wq_send)
         wk_full, wv_full, wk_send, wv_send = grad_wx(
-            xg, flat, cut(by_k, pairs, wide) + cut(by_v, pairs, wide), (kv_heads, kv_heads), core_arr, 'grad_wkv')
+            xg, flat, cut(by_k + by_v, wide), (kv_heads, kv_heads), core_arr, 'grad_wkv')
         wk_send, wv_send, x_late = lax.optimization_barrier((wk_send, wv_send, x_in))
         wk_recv, wv_recv = swap(wk_send), swap(wv_send)
-        dx_out, d_gain = grad_x(idx, pairs, cut(by_q + by_k + by_v, pairs, wide), wide, wcat, x_late, dy_in, norm_gain[None])
+        dx_out, d_gain = grad_x(idx, pairs, cut(by_q + by_k + by_v, wide), wide, wcat, x_late, dy_in, norm_gain[None])
         d_gain = d_gain[0]
-        for bit in (1, 2, 4):
-            d_gain = d_gain + lax.ppermute(d_gain, 'cp', [(d, d ^ bit) for d in range(n_dev)])
-        wq_recv, wk_recv, wv_recv, dx_out = lax.optimization_barrier((wq_recv, wk_recv, wv_recv, dx_out))
-        d_wq, d_wk, d_wv = merge((wq_full, wk_full, wv_full), (wq_recv, wk_recv, wv_recv), core_arr)
+
+        def add_from(bit, a):
+            return a + lax.ppermute(a, 'cp', [(d, d ^ bit) for d in range(n_dev)])
+
+        d_gain = add_from(2, add_from(1, d_gain))
+        wq_recv, wk_recv, wv_recv, d_wo, dx_out = lax.optimization_barrier((wq_recv, wk_recv, wv_recv, d_wo, dx_out))
+        d_wq, d_wk, d_wv, d_wo = merge((wq_full, wk_full, wv_full), (wq_recv, wk_recv, wv_recv), d_wo, core_arr)
+        d_gain = add_from(4, d_gain)
         d_wo = d_wo.reshape(n_heads, HD, dm)
         return y_out, dx_out, d_gain, d_wq, d_wk, d_wv, d_wo
 

time: 688 us -> 625 us (0.908); the launches traced: 678 us -> 622 us
  waiting for transfers between devices: 110 us -> 66.7 us
  local copies, waits for them, and re-layouts: 35.5 us -> 3.91 us
  Pallas kernels: 502 us -> 522 us
    unnamed x15 -> x6, local copies, waits for them, and re-layouts: 32.8 us -> 1.15 us
    pallas_call x1, Pallas kernels: 23.8 us -> 44.1 us  [merge(): pl.pallas_call(merge_kernel, grid_spec=pltpu.PrefetchScalarGridSpec(num_s...]
    all_gather x1, waiting for transfers between devices: 17.1 us -> 0.01 us  [device_fn(): dyg = lax.all_gather(dy, 'cp', tiled=True)]
    all_gather x1, waiting for transfers between devices: 64.1 us -> 48.5 us  [device_fn(): xg = lax.all_gather(xn, 'cp', tiled=True)]
    ppermute x12 -> x8, waiting for transfers between devices: 21 us -> 10.9 us  [swap(): return lax.ppermute(a, 'cp', pair)]
  transfers between devices with their start and end apart: 18 -> 14, of which waited for: 7 -> 6; matrix products, arithmetic and copies ran while one was open for 1% -> 1% of each run, Pallas kernels for 72% -> 74%
where the time goes in v2:
time: 625 us; the launch traced here: 622 us
  Pallas kernels  522 us (84%)
  waiting for transfers between devices  66.7 us (11%)
  between operations  14 us (2%)
  other arithmetic  10.7 us (2%)
    pallas_call x2, Pallas kernels, attn_bwd(): pl.pallas_call(functools.partial(bwd_kernel, 256), grid=(nb, count), in_s...  98.2 us
    pallas_call x2, Pallas kernels, grad_wx(): pl.pallas_call(functools.partial(grad_wx_kernel, plan, len(srcs), len(hea...  97.4 us
    pallas_call x2, Pallas kernels, proj_far(): pl.pallas_call(functools.partial(far_kernel, cb), grid_spec=pltpu.Prefetc...  95.2 us
    pallas_call x1, Pallas kernels, attn_fwd(): pl.pallas_call(functools.partial(fwd_kernel, 128), grid=(nb, kvh), in_spe...  49 us
    all_gather x1, waiting for transfers between devices, device_fn(): xg = lax.all_gather(xn, 'cp', tiled=True)  48.5 us
    pallas_call x1, Pallas kernels, merge(): pl.pallas_call(merge_kernel, grid_spec=pltpu.PrefetchScalarGridSpec(num_s...  44.1 us
    pallas_call x2, Pallas kernels, proj_near(): pl.pallas_call(functools.partial(near_kernel, cb), grid_spec=pltpu.Prefet...  40.2 us
    pallas_call x1, Pallas kernels, relayout(): pl.pallas_call(relayout_kernel, grid_spec=pltpu.PrefetchScalarGridSpec(nu...  32.9 us
  transfers between devices with their start and end apart: 14, of which 6 were waited for; matrix products, arithmetic and copies ran while one was open for 1% of the time, Pallas kernels for 74%

profile of v2, /device:TPU:0, one launch (start us, length us, event | category | flops | bytes accessed | tf_op | source)
XLA Modules:
  0.0 621.7 jit_solution(4573094804126111692)
XLA Ops:
  7.2 0.0 all-gather.6.cloned.1.call-start
  7.2 2.6 fusion
  9.8 0.7 convert_element_type.10
  10.5 0.0 copy-start
  10.5 4.9 fusion.2
  15.4 0.0 all-gather.6.cloned.1.call-update
  15.4 0.0 all-gather.4.cloned.1.call-start
  15.5 0.7 all-gather.4.cloned.1.call-update
  16.2 0.0 all-gather.8.cloned.1.call-start
  16.2 0.0 copy-done
  16.2 0.8 collective-permute-start.1
  17.0 0.1 collective-permute-start
  17.1 0.6 stack.46.tbl_ref
  17.7 0.6 pad_add_fusion.tbl_ref
  18.3 32.9 %relayout.1 = (bf16[3072,5120]{1,0:T(8,128)(2,1)}, bf16[3072,2560]{1,0:T(8,128)(2,1)}) custom-call(s32[1]{0:T(128)} %bitcast.7.core_ref, bf16[3072,24,128]{2,1,0:T(8,128)(2,1)} %wq_ref.1, bf16[3072,8,128]{2,1,0:T(8,128)(2,1)} %wk_ref.1, bf16[3072,8,128]{2,1,0:T(8,128)(2,1)} %wv_ref.1), custom_call_target="tpu_custom_call" | custom-call | flops 10000000000 | bytes 62914560 | tf_op jit(solution)/shard_map/relayout/pallas_call | solution.py:47
  51.2 0.0 collective-permute-done.1.b_ref
  51.2 16.4 %near_do.1.old_ref = bf16[4096,1536]{1,0:T(8,128)(2,1)} custom-call(s32[3]{0:T(128)} %pad_add_fusion.tbl_ref, bf16[512,3072]{1,0:T(8,128)(2,1)} %bitcast.40, bf16[512,3072]{1,0:T(8,128)(2,1)} %collective-permute-done.1.b_ref, bf16[3072,3072]{1,0:T(8,128)(2,1)} %bitcast.34), custom_call_target="tpu_custom_call" | custom-call | flops 9663676416 | bytes 9437184 | tf_op jit(solution)/shard_map/near_do/pallas_call | solution.py:79
  67.7 0.0 collective-permute-done.b_ref
  67.7 23.7 %near_qkv.1.old_ref = bf16[4096,2560]{1,0:T(8,128)(2,1)} custom-call(s32[3]{0:T(128)} %pad_add_fusion.tbl_ref, bf16[512,3072]{1,0:T(8,128)(2,1)} %bitcast.48, bf16[512,3072]{1,0:T(8,128)(2,1)} %collective-permute-done.b_ref, bf16[3072,2560]{1,0:T(8,128)(2,1)} %get-tuple-element.42.w_ref), custom_call_target="tpu_custom_call" | custom-call | flops 16106127360 | bytes 15728640 | tf_op jit(solution)/shard_map/near_qkv/pallas_call | solution.py:79
  91.4 48.5 %all-gather.6.cloned.1.call-done.a_ref = bf16[4096,3072]{1,0:T(8,128)(2,1)} async-done(((bf16[512,3072]{1,0:T(8,128)(2,1)}), bf16[4096,3072]{1,0:T(8,128)(2,1)}) %all-gather.6.cloned.1.call-update) | async-done | bytes 25165840 | tf_op jit(solution)/shard_map/all_gather | solution.py:486
  139.9 57.3 %far_qkv.1 = bf16[4096,2560]{1,0:T(8,128)(2,1)} custom-call(s32[7]{0:T(128)} %stack.46.tbl_ref, bf16[4096,3072]{1,0:T(8,128)(2,1)} %all-gather.6.cloned.1.call-done.a_ref, bf16[3072,2560]{1,0:T(8,128)(2,1)} %get-tuple-element.42.w_ref, bf16[4096,2560]{1,0:T(8,128)(2,1)} %near_qkv.1.old_ref), custom_call_target="tpu_custom_call", output_to_operand_aliasing={{}: (3, {})} | custom-call | flops 48318382080 | bytes 25165824 | tf_op jit(solution)/shard_map/far_qkv/pallas_call | solution.py:93
  197.2 49.0 %attn_fwd.1 = (bf16[8,4,128,1536]{3,2,1,0:T(8,128)(2,1)}, f32[4,12,1,1024]{3,2,1,0:T(1,128)}) custom-call(bf16[8,4,128,2560]{3,2,1,0:T(8,128)(2,1)} %bitcast.24, bf16[8,4,128,2560]{3,2,1,0:T(8,128)(2,1)} %bitcast.25, bf16[8,4,128,2560]{3,2,1,0:T(8,128)(2,1)} %bitcast.26), custom_call_target="tpu_custom_call" | custom-call | flops 25769803776 | bytes 10000000 | tf_op jit(solution)/shard_map/attn_fwd/pallas_call | solution.py:153
  246.3 1.5 dynamic-slice_bitcast_fusion
  247.8 0.3 collective-permute-start.2
  248.1 0.6 pad_add_fusion.1.idx_ref
  248.7 2.5 collective-permute-done.2.rem_ref
  251.2 0.0 copy-start.1
  251.2 1.1 copy-done.1
  252.4 19.6 %out_proj.1 = bf16[4,128,3072]{2,1,0:T(8,128)(2,1)} custom-call(s32[2]{0:T(128)} %pad_add_fusion.1.idx_ref, bf16[8,4,128,1536]{3,2,1,0:T(8,128)(2,1)} %get-tuple-element.47.loc_ref.o_ref, bf16[4,128,1536]{2,1,0:T(8,128)(2,1)} %copy-done.1, bf16[3072,3072]{1,0:T(8,128)(2,1)} %bitcast.35, bf16[4,128,3072]{2,1,0:T(8,128)(2,1)} %refs_5_), custom_call_target="tpu_custom_call" | custom-call | flops 9663676416 | bytes 18874368 | tf_op jit(solution)/shard_map/out_proj/pallas_call | solution.py:380
  272.0 0.0 all-gather.4.cloned.1.call-done.a_ref.b_ref
  272.0 16.4 %grad_wo.1 = f32[384,3072]{1,0:T(8,128)} custom-call(s32[1]{0:T(128)} %bitcast.19.chip_ref, bf16[4096,1536]{1,0:T(8,128)(2,1)} %bitcast.33, bf16[4096,3072]{1,0:T(8,128)(2,1)} %all-gather.4.cloned.1.call-done.a_ref.b_ref), custom_call_target="tpu_custom_call" | custom-call | flops 9663676416 | bytes 25165824 | tf_op jit(solution)/shard_map/grad_wo/pallas_call | solution.py:245
  288.3 0.0 all-gather.8.cloned.1.call-update
  288.4 37.8 %far_do.1 = bf16[4096,1536]{1,0:T(8,128)(2,1)} custom-call(s32[7]{0:T(128)} %stack.46.tbl_ref, bf16[4096,3072]{1,0:T(8,128)(2,1)} %all-gather.4.cloned.1.call-done.a_ref.b_ref, bf16[3072,3072]{1,0:T(8,128)(2,1)} %bitcast.36, bf16[4096,1536]{1,0:T(8,128)(2,1)} %near_do.1.old_ref), custom_call_target="tpu_custom_call", output_to_operand_aliasing={{}: (3, {})} | custom-call | flops 28991029248 | bytes 25165824 | tf_op jit(solution)/shard_map/far_do/pallas_call | solution.py:93
  326.2 72.5 %attn_bwd.2.refs_0_ = bf16[8,4,128,1920]{3,2,1,0:T(8,128)(2,1)} custom-call(bf16[8,4,128,2560]{3,2,1,0:T(8,128)(2,1)} %bitcast.27, bf16[8,4,128,2560]{3,2,1,0:T(8,128)(2,1)} %bitcast.28, bf16[8,4,128,2560]{3,2,1,0:T(8,128)(2,1)} %bitcast.29, bf16[8,4,128,1536]{3,2,1,0:T(8,128)(2,1)} %get-tuple-element.47.loc_ref.o_ref, bf16[8,4,128,1536]{3,2,1,0:T(8,128)(2,1)} %bitcast.37, ...), custom_call_target="tpu_custom_call" | custom-call | flops 48318382080 | bytes 10000000 | tf_op jit(solution)/shard_map/attn_bwd/pallas_call | solution.py:223
  398.7 0.3 collective-permute-start.3
  398.9 25.8 %attn_bwd.3.refs_2_ = bf16[8,4,128,640]{3,2,1,0:T(8,128)(2,1)} custom-call(bf16[8,4,128,2560]{3,2,1,0:T(8,128)(2,1)} %bitcast.30, bf16[8,4,128,2560]{3,2,1,0:T(8,128)(2,1)} %bitcast.31, bf16[8,4,128,2560]{3,2,1,0:T(8,128)(2,1)} %bitcast.32, bf16[8,4,128,1536]{3,2,1,0:T(8,128)(2,1)} %get-tuple-element.47.loc_ref.o_ref, bf16[8,4,128,1536]{3,2,1,0:T(8,128)(2,1)} %bitcast.38, ...), custom_call_target="tpu_custom_call" | custom-call | flops 16106127360 | bytes 10000000 | tf_op jit(solution)/shard_map/attn_bwd/pallas_call | solution.py:223
  424.7 0.3 collective-permute-start.4
  424.9 8.4 %collective-permute-done.4.refs_3_ = bf16[8,4,128,640]{3,2,1,0:T(8,128)(2,1)} collective-permute-done((bf16[8,4,128,640]{3,2,1,0:T(8,128)(2,1)}, bf16[8,4,128,640]{3,2,1,0:T(8,128)(2,1)}, u32[]{:S(2)}, u32[]{:S(2)}) %collective-permute-start.4) | collective-permute-done | bytes 5242912 | tf_op jit(solution)/shard_map/ppermute | solution.py:478
  433.3 0.0 collective-permute-done.3.refs_1_
  433.3 53.5 %grad_wq.1 = (f32[3072,24,128]{2,1,0:T(8,128)}, f32[1536,24,128]{2,1,0:T(8,128)}) custom-call(s32[1]{0:T(128)} %bitcast.7.core_ref, bf16[4096,3072]{1,0:T(8,128)(2,1)} %all-gather.6.cloned.1.call-done.a_ref, bf16[4096,1920]{1,0:T(8,128)(2,1)} %bitcast.44, bf16[4096,1920]{1,0:T(8,128)(2,1)} %bitcast.16.refs_1_, bf16[4096,640]{1,0:T(8,128)(2,1)} %bitcast.42, ...), custom_call_target="tpu_custom_call" | custom-call | flops 38654705664 | bytes 25165824 | tf_op jit(solution)/shard_map/grad_wq/pallas_call | solution.py:311
  486.9 0.0 copy-start.2
  486.9 0.3 collective-permute-start.5
  487.2 43.8 %grad_wkv.1 = (f32[3072,8,128]{2,1,0:T(8,128)}, f32[3072,8,128]{2,1,0:T(8,128)}, f32[1536,8,128]{2,1,0:T(8,128)}, f32[1536,8,128]{2,1,0:T(8,128)}) custom-call(s32[1]{0:T(128)} %bitcast.7.core_ref, bf16[4096,3072]{1,0:T(8,128)(2,1)} %all-gather.6.cloned.1.call-done.a_ref, bf16[4096,1920]{1,0:T(8,128)(2,1)} %bitcast.45, bf16[4096,1920]{1,0:T(8,128)(2,1)} %bitcast.16.refs_1_, ...), custom_call_target="tpu_custom_call" | custom-call | flops 25769803776 | bytes 25165824 | tf_op jit(solution)/shard_map/grad_wkv/pallas_call | solution.py:311
  531.0 0.3 collective-permute-start.6
  531.3 0.3 collective-permute-start.7
  531.6 0.0 copy-done.2
  531.6 0.6 broadcast_in_dim.10.refs_7_
  532.2 28.7 %grad_x.1 = (bf16[4,128,3072]{2,1,0:T(8,128)(2,1)}, f32[1,3072]{1,0:T(1,128)}) custom-call(s32[2]{0:T(128)} %pad_add_fusion.1.idx_ref, bf16[8,4,128,1920]{3,2,1,0:T(8,128)(2,1)} %attn_bwd.2.refs_0_, bf16[8,4,128,1920]{3,2,1,0:T(8,128)(2,1)} %collective-permute-done.3.refs_1_, bf16[8,4,128,640]{3,2,1,0:T(8,128)(2,1)} %attn_bwd.3.refs_2_, ...), custom_call_target="tpu_custom_call" | custom-call | flops 16106127360 | bytes 18874368 | tf_op jit(solution)/shard_map/grad_x/pallas_call | solution.py:446
  560.9 0.1 collective-permute-start.8
  561.0 1.0 collective-permute-done.8
  562.1 0.7 add.68
  562.8 1.5 collective-permute-start.9
  564.3 2.2 collective-permute-done.9
  566.5 0.4 collective-permute-start.10
  566.8 3.3 collective-permute-done.10
  570.2 0.6 add.70
  570.8 0.0 collective-permute-done.6.refs_4_
  570.8 0.0 collective-permute-done.7.refs_5_
  570.8 0.0 collective-permute-done.5.refs_3_
  570.8 0.0 all-gather.8.cloned.1.call-done.refs_6_
  570.8 44.1 %merge.1 = (f32[3072,24,128]{2,1,0:T(8,128)}, f32[3072,8,128]{2,1,0:T(8,128)}, f32[3072,8,128]{2,1,0:T(8,128)}, f32[3072,3072]{1,0:T(8,128)}) custom-call(s32[1]{0:T(128)} %bitcast.7.core_ref, f32[3072,24,128]{2,1,0:T(8,128)} %get-tuple-element.66.refs_0_, ...), custom_call_target="tpu_custom_call", output_to_operand_aliasing={{0}: (1, {}), {1}: (2, {}), {2}: (3, {})} | custom-call | flops 10000000000 | bytes 100000000 | tf_op jit(solution)/shard_map/merge/pallas_call | solution.py:342
  (2 shorter events, 0.0 us)
Async XLA Ops:
  7.2 132.7 %all-gather.6.cloned.1.call-start = ((), (), s32[]{:S(2)}) async-start(), calls=%async_computation.1 | async-start | bytes 28311552 | tf_op jit(solution)/shard_map/all_gather | solution.py:486
  10.5 5.7 copy-start
  15.4 256.6 %all-gather.4.cloned.1.call-start = ((), (), s32[]{:S(2)}) async-start(), calls=%async_computation | async-start | bytes 28311552 | tf_op jit(solution)/shard_map/all_gather | solution.py:487
  16.2 554.6 %all-gather.8.cloned.1.call-start = ((), (), s32[]{:S(2)}) async-start(), calls=%async_computation.2 | async-start | bytes 42467328 | tf_op jit(solution)/shard_map/all_gather | solution.py:502
  16.2 35.0 %collective-permute-start.1 = (bf16[512,3072]{1,0:T(8,128)(2,1)S(1)}, bf16[512,3072]{1,0:T(8,128)(2,1)}, u32[]{:S(2)}, u32[]{:S(2)}) collective-permute-start(bf16[512,3072]{1,0:T(8,128)(2,1)S(1)} %bitcast.41), channel_id=1, source_target_pairs={{0,1},{1,0},{2,3},{3,2},{4,5},{5,4},{6,7},{7,6},{8,9},{9,8},{10,11... | collective-permute-start | bytes 9437192 | tf_op jit(solution)/shard_map/ppermute | solution.py:478
  17.0 50.6 %collective-permute-start = (bf16[512,3072]{1,0:T(8,128)(2,1)}, bf16[512,3072]{1,0:T(8,128)(2,1)}, u32[]{:S(2)}, u32[]{:S(2)}) collective-permute-start(bf16[512,3072]{1,0:T(8,128)(2,1)} %bitcast.47), channel_id=1, source_target_pairs={{0,1},{1,0},{2,3},{3,2},{4,5},{5,4},{6,7},{7,6},{8,9},{9,8},{10,11... | collective-permute-start | bytes 9437192 | tf_op jit(solution)/shard_map/ppermute | solution.py:478
  247.8 3.4 collective-permute-start.2
  251.2 1.1 copy-start.1
  398.7 34.6 %collective-permute-start.3 = (bf16[8,4,128,1920]{3,2,1,0:T(8,128)(2,1)}, bf16[8,4,128,1920]{3,2,1,0:T(8,128)(2,1)}, u32[]{:S(2)}, u32[]{:S(2)}) collective-permute-start(bf16[8,4,128,1920]{3,2,1,0:T(8,128)(2,1)} %attn_bwd.2.refs_0_), channel_id=1, source_target_pairs={{0,1},{1,0},{2,3},{3,2},{4,5},{5,4},{6,7},{7,6},{8,9},{9,8},{10,11... | collective-permute-start | bytes 47185928 | tf_op jit(solution)/shard_map/ppermute | solution.py:478
  424.7 8.6 %collective-permute-start.4 = (bf16[8,4,128,640]{3,2,1,0:T(8,128)(2,1)}, bf16[8,4,128,640]{3,2,1,0:T(8,128)(2,1)}, u32[]{:S(2)}, u32[]{:S(2)}) collective-permute-start(bf16[8,4,128,640]{3,2,1,0:T(8,128)(2,1)} %attn_bwd.3.refs_2_), channel_id=1, source_target_pairs={{0,1},{1,0},{2,3},{3,2},{4,5},{5,4},{6,7},{7,6},{8,9},{9,8},{10,11... | collective-permute-start | bytes 15728648 | tf_op jit(solution)/shard_map/ppermute | solution.py:478
  486.9 44.7 %copy-start.2 = (bf16[3072]{0:T(1024)(128)(2,1)S(1)}, bf16[3072]{0:T(1024)(128)(2,1)}, u32[]{:S(2)}) copy-start(bf16[3072]{0:T(1024)(128)(2,1)} %param.9) | copy-start | bytes 18436
  486.9 83.9 %collective-permute-start.5 = (f32[1536,24,128]{2,1,0:T(8,128)}, f32[1536,24,128]{2,1,0:T(8,128)}, u32[]{:S(2)}, u32[]{:S(2)}) collective-permute-start(f32[1536,24,128]{2,1,0:T(8,128)} %get-tuple-element.55), channel_id=1, source_target_pairs={{0,1},{1,0},{2,3},{3,2},{4,5},{5,4},{6,7},{7,6},{8,9},{9,8},{10,11... | collective-permute-start | bytes 56623112 | tf_op jit(solution)/shard_map/ppermute | solution.py:478
  531.0 39.8 %collective-permute-start.6 = (f32[1536,8,128]{2,1,0:T(8,128)}, f32[1536,8,128]{2,1,0:T(8,128)}, u32[]{:S(2)}, u32[]{:S(2)}) collective-permute-start(f32[1536,8,128]{2,1,0:T(8,128)} %get-tuple-element.59), channel_id=1, source_target_pairs={{0,1},{1,0},{2,3},{3,2},{4,5},{5,4},{6,7},{7,6},{8,9},{9,8},{10,11... | collective-permute-start | bytes 18874376 | tf_op jit(solution)/shard_map/ppermute | solution.py:478
  531.3 39.5 %collective-permute-start.7 = (f32[1536,8,128]{2,1,0:T(8,128)}, f32[1536,8,128]{2,1,0:T(8,128)}, u32[]{:S(2)}, u32[]{:S(2)}) collective-permute-start(f32[1536,8,128]{2,1,0:T(8,128)} %get-tuple-element.60), channel_id=1, source_target_pairs={{0,1},{1,0},{2,3},{3,2},{4,5},{5,4},{6,7},{7,6},{8,9},{9,8},{10,11... | collective-permute-start | bytes 18874376 | tf_op jit(solution)/shard_map/ppermute | solution.py:478
  560.9 1.2 collective-permute-start.8
  562.8 3.7 collective-permute-start.9
  566.5 3.7 collective-permute-start.10
Sparse Core Ops, SparseCore 0:
  15.5 124.2 all-gather.5
  141.7 121.4 all-gather.3
  288.5 175.8 all-gather.7

commit v3 on v2

--- a/solution.py
+++ b/solution.py
@@ -7,6 +7,7 @@
 from jax.experimental import pallas as pl
 from jax.experimental.pallas import tpu as pltpu
 from jax.sharding import PartitionSpec as P
+
 
 EPS = 1e-6
 HD = 128
@@ -55,49 +56,63 @@
         cost_estimate=cost(1e10, 4 * dm * cols), name='relayout')(core, w_q, w_k, w_v)
 
 
-def near_kernel(cb, tbl_ref, a_ref, b_ref, w_ref, o_ref):
-    m = pl.program_id(1)
-    a = jnp.where(m == 0, a_ref[...], b_ref[...])
+def proj_kernel(cb, counts, tbl_ref, *refs):
+    n_in = sum(counts)
+    w_ref, (o_ref, x_ref, buf, sem) = refs[n_in], refs[-4:]
+    m, nm = pl.program_id(1), pl.num_programs(1)
+    step = pl.program_id(0) * nm + m
+
+    def fetch(idx, slot):
+        at = 0
+        for j, count in enumerate(counts):
+            @pl.when(idx == j)
+            def _(parts=refs[at:at + count]):
+                row = 0
+                for part in parts:
+                    rows = part.shape[0]
+                    pltpu.make_async_copy(part, buf.at[slot, pl.ds(row, rows)], sem.at[slot]).start()
+                    row += rows
+
+            at += count
+
+    @pl.when(step == 0)
+    def _():
+        fetch(m, 0)
+
+    @pl.when(step + 1 < pl.num_programs(0) * nm)
+    def _():
+        fetch(lax.rem(m + 1, nm), lax.rem(step + 1, 2))
+
+    slot = lax.rem(step, 2)
+    pltpu.make_async_copy(buf.at[slot], buf.at[slot], sem.at[slot]).wait()
+    a = buf[slot]
     o_ref[...] = dot(a, w_ref[...], 1, cb).astype(jnp.bfloat16)
-
-
-def far_kernel(cb, tbl_ref, a_ref, w_ref, old_ref, o_ref):
-    o_ref[...] = dot(a_ref[...], w_ref[...], 1, cb).astype(jnp.bfloat16)
-
-
-def proj_specs(w, width, cb, row):
+    x_ref[...] = a
+
+
+def proj(pieces, w, blocks, core, tok, width, cb, old):
+    dm = pieces[0][0].shape[1]
+    bm = sum(p.shape[0] for p in pieces[0])
     bn = width // 2
+    nm = len(pieces)
+    tbl = jnp.stack(blocks + [core]).astype(jnp.int32)
+    flat = [p for piece in pieces for p in piece]
     if cb == 0:
-        return bn, pl.BlockSpec((w.shape[0], bn), lambda n, m, t: (0, n))
-    return bn, pl.BlockSpec((bn, w.shape[1]), lambda n, m, t: (2 * t[row] + n, 0))
-
-
-def proj_near(a, b, w, tbl, tok, width, cb, name):
-    bm, dm = a.shape
-    bn, w_spec = proj_specs(w, width, cb, 2)
-    line = pl.BlockSpec((bm, dm), lambda n, m, t: (0, 0))
-    return pl.pallas_call(
-        functools.partial(near_kernel, cb),
-        grid_spec=pltpu.PrefetchScalarGridSpec(
-            num_scalar_prefetch=1, grid=(2, 2), in_specs=[line, line, w_spec],
-            out_specs=pl.BlockSpec((bm, bn), lambda n, m, t: (t[m], n))),
-        out_shape=jax.ShapeDtypeStruct((tok, width), jnp.bfloat16),
-        compiler_params=BIG, cost_estimate=cost(4 * bm * dm * width, 2 * dm * width), name=name)(tbl, a, b, w)
-
-
-def proj_far(a, w, old, tbl, bm, cb, name):
-    tok, dm = a.shape
-    width = old.shape[1]
-    rest = tok // bm - 2
-    bn, w_spec = proj_specs(w, width, cb, rest)
-    return pl.pallas_call(
-        functools.partial(far_kernel, cb),
-        grid_spec=pltpu.PrefetchScalarGridSpec(
-            num_scalar_prefetch=1, grid=(2, rest),
-            in_specs=[pl.BlockSpec((bm, dm), lambda n, m, t: (t[m], 0)), w_spec, pl.BlockSpec(memory_space=pl.ANY)],
-            out_specs=pl.BlockSpec((bm, bn), lambda n, m, t: (t[m], n))),
-        out_shape=jax.ShapeDtypeStruct(old.shape, jnp.bfloat16), input_output_aliases={3: 0},
-        compiler_params=BIG, cost_estimate=cost(2 * rest * bm * dm * width, 2 * tok * dm), name=name)(tbl, a, w, old)
+        w_spec = pl.BlockSpec((dm, bn), lambda n, m, t: (0, n))
+    else:
+        w_spec = pl.BlockSpec((bn, dm), lambda n, m, t: (2 * t[nm] + n, 0))
+    any_spec = pl.BlockSpec(memory_space=pl.ANY)
+    first = 2 + len(flat)
+    return pl.pallas_call(
+        functools.partial(proj_kernel, cb, [len(p) for p in pieces]),
+        grid_spec=pltpu.PrefetchScalarGridSpec(
+            num_scalar_prefetch=1, grid=(2, nm),
+            in_specs=[any_spec] * len(flat) + [w_spec] + [any_spec] * len(old),
+            out_specs=[pl.BlockSpec((bm, bn), lambda n, m, t: (t[m], n)), pl.BlockSpec((bm, dm), lambda n, m, t: (t[m], 0))],
+            scratch_shapes=[pltpu.VMEM((2, bm, dm), jnp.bfloat16), pltpu.SemaphoreType.DMA((2,))]),
+        out_shape=[jax.ShapeDtypeStruct((tok, width), jnp.bfloat16), jax.ShapeDtypeStruct((tok, dm), jnp.bfloat16)],
+        input_output_aliases={first + i: i for i in range(len(old))},
+        compiler_params=BIG, cost_estimate=cost(2 * nm * bm * dm * width, 2 * dm * width))(tbl, *flat, w, *old)
 
 
 def stack(ref, rb, nblk, rows, group):
@@ -105,7 +120,8 @@
     return jnp.concatenate(parts, axis=0)
 
 
-def fwd_kernel(rows, q_ref, k_ref, v_ref, o_ref, l_ref):
+def fwd_kernel(rows, q_ref, k_ref, v_ref, *refs):
+    o_ref, l_ref = refs[-2:]
     n, _, blk, width = q_ref.shape
     group, seq, nblk = width // HD, n * blk, rows // blk
     c2 = HD ** -0.5 * LOG2E
@@ -146,21 +162,23 @@
             l_ref[0, g, :, r0:r0 + rows] = log2n[g * rows:(g + 1) * rows].T[0:1]
 
 
-def attn_fwd(qkv, kvh, group):
+def attn_fwd(qkv, kvh, group, b0, count, old):
     n, nb, s, _ = qkv.shape
     width = group * HD
     first = kvh * group
     return pl.pallas_call(
-        functools.partial(fwd_kernel, 128), grid=(nb, kvh),
-        in_specs=[pl.BlockSpec((n, 1, s, width), lambda b, h: (0, b, 0, h)),
-                  pl.BlockSpec((n, 1, s, HD), lambda b, h: (0, b, 0, first + h)),
-                  pl.BlockSpec((n, 1, s, HD), lambda b, h: (0, b, 0, first + kvh + h))],
-        out_specs=[pl.BlockSpec((n, 1, s, width), lambda b, h: (0, b, 0, h)),
-                   pl.BlockSpec((1, group, 1, n * s), lambda b, h: (b, h, 0, 0))],
+        functools.partial(fwd_kernel, 128), grid=(count, kvh),
+        in_specs=[pl.BlockSpec((n, 1, s, width), lambda b, h: (0, b0 + b, 0, h)),
+                  pl.BlockSpec((n, 1, s, HD), lambda b, h: (0, b0 + b, 0, first + h)),
+                  pl.BlockSpec((n, 1, s, HD), lambda b, h: (0, b0 + b, 0, first + kvh + h))]
+        + [pl.BlockSpec(memory_space=pl.ANY)] * len(old),
+        out_specs=[pl.BlockSpec((n, 1, s, width), lambda b, h: (0, b0 + b, 0, h)),
+                   pl.BlockSpec((1, group, 1, n * s), lambda b, h: (b0 + b, h, 0, 0))],
         out_shape=[jax.ShapeDtypeStruct((n, nb, s, kvh * width), jnp.bfloat16),
                    jax.ShapeDtypeStruct((nb, kvh * group, 1, n * s), jnp.float32)],
-        compiler_params=BIG, cost_estimate=cost(nb * kvh * group * 4 * (n * s) ** 2 * HD, 10 ** 7),
-        name='attn_fwd')(qkv, qkv, qkv)
+        input_output_aliases={3 + i: i for i in range(len(old))},
+        compiler_params=BIG, cost_estimate=cost(count * kvh * group * 4 * (n * s) ** 2 * HD, 10 ** 7),
+        name='attn_fwd')(qkv, qkv, qkv, *old)
 
 
 def bwd_kernel(rows, q_ref, k_ref, v_ref, o_ref, do_ref, l_ref, d_ref, dq_acc):
@@ -299,7 +317,7 @@
                 store((fulls[pos], sends[pos]))
 
 
-def grad_wx(x, srcs, plan, heads, core, name):
+def grad_wx(x, srcs, plan, heads, core):
     tok, dm = x.shape
     bm = 768
     nm = dm // 2 // bm
@@ -319,7 +337,7 @@
             scratch_shapes=[pltpu.VMEM((2, tok, 8 * HD), jnp.bfloat16), pltpu.SemaphoreType.DMA((2,))]),
         out_shape=[jax.ShapeDtypeStruct((dm, h, HD), jnp.float32) for h in heads]
         + [jax.ShapeDtypeStruct((dm // 2, h, HD), jnp.float32) for h in heads],
-        compiler_params=BIG, cost_estimate=cost(tok * dm * 8 * HD * len(plan), 2 * tok * dm), name=name)(core, x, *flat)
+        compiler_params=BIG, cost_estimate=cost(tok * dm * 8 * HD * len(plan), 2 * tok * dm))(core, x, *flat)
 
 
 def merge_kernel(core_ref, *refs):
@@ -353,7 +371,7 @@
 def y_kernel(idx_ref, loc_ref, rem_ref, w_ref, x_ref, y_ref, acc):
     k = pl.program_id(0)
     per = pl.num_programs(0) // 2
-    nb, s, dm = x_ref.shape
+    nb, s, _ = x_ref.shape
     tok = nb * s
     mine = k // per == idx_ref[0]
     part = dot(jnp.where(mine, loc_ref[...].reshape(tok, -1), rem_ref[...].reshape(tok, -1)), w_ref[...], 1, 0)
@@ -461,7 +479,7 @@
     pair = [(d, d ^ 1) for d in range(n_dev)]
     by_core = [[2 * p + c for c in range(2) for p in range(n_chips)]]
 
-    def device_fn(x_in, dy_in, norm_gain, w_q, w_k, w_v, w_o):
+    def compute(x_in, dy_in, norm_gain, w_q, w_k, w_v, w_o):
         me = lax.axis_index('cp')
         core = me % 2
         nb, s, dm = x_in.shape
@@ -483,24 +501,47 @@
         own = nb * s
         xn = xn.reshape(own, dm)
         dy = dy_in.reshape(own, dm)
-        xg = lax.all_gather(xn, 'cp', tiled=True)
-        dyg = lax.all_gather(dy, 'cp', tiled=True)
+        wo = w_o.reshape(qd, dm)
+        fence = lax.optimization_barrier
+        cut_row = own // 2
+
+        def hop(a, bit):
+            return lax.ppermute(a, 'cp', [(d, d ^ bit) for d in range(n_dev)])
+
+        def block(bit):
+            return me ^ bit
+
+        xn_x, xn_y, xn_c = hop(xn, 2), hop(xn, 4), swap(xn)
         wcat, wh = relayout(w_q, w_k, w_v, core_arr)
-        wo = w_o.reshape(qd, dm)
-        near = jnp.stack([me, me ^ 1, core]).astype(jnp.int32)
-        chip = me // 2
-        far = [2 * lax.rem(chip + 1 + j // 2, n_chips) + j % 2 for j in range(n_dev - 2)]
-        far = jnp.stack(far + [core]).astype(jnp.int32)
-        qkv = proj_near(xn, swap(xn), wh, near, tok, wh.shape[1], 0, 'near_qkv')
-        do = proj_near(dy, swap(dy), wo, near, tok, qd // 2, 1, 'near_do')
-        qkv, do, xg = lax.optimization_barrier((qkv, do, xg))
-        qkv = proj_far(xg, wh, qkv, far, own, 0, 'far_qkv').reshape(n_dev, nb, s, -1)
-        o, log2n = attn_fwd(qkv, kvh, group)
+        dy_c = swap(dy)
+        wide_qkv = wh.shape[1]
+        seen = proj([(xn,), (xn_c,)], wh, [block(0), block(1)], core, tok, wide_qkv, 0, [])
+        xn_x, xn_y, seen = fence((xn_x, xn_y, seen))
+        xn_d = hop(xn_x[:cut_row], 4), hop(xn_y[cut_row:], 2)
+        xn_xc, xn_yc = swap(xn_x), swap(xn_y)
+        done = proj([(dy,), (dy_c,)], wo, [block(0), block(1)], core, tok, qd // 2, 1, [])
+        xn_xc, xn_yc, done, seen, dy = fence((xn_xc, xn_yc, done, seen, dy))
+        dy_x, dy_y = hop(dy, 2), hop(dy, 4)
+        beside = [block(2), block(3), block(4), block(5)]
+        across = [block(6), block(7)]
+        seen = proj([(xn_x,), (xn_xc,), (xn_y,), (xn_yc,)], wh, beside, core, tok, wide_qkv, 0, seen)
+        xn_d, seen = fence((xn_d, seen))
+        xn_dc = swap(xn_d[0]), swap(xn_d[1])
+        qkv, xg = proj([xn_d, xn_dc], wh, across, core, tok, wide_qkv, 0, seen)
+        qkv = qkv.reshape(n_dev, nb, s, -1)
+        fwd = attn_fwd(qkv, kvh, group, 0, nb // 2, [])
+        dy_x, dy_y, fwd = fence((dy_x, dy_y, fwd))
+        dy_d = hop(dy_x[:cut_row], 4), hop(dy_y[cut_row:], 2)
+        dy_xc, dy_yc = swap(dy_x), swap(dy_y)
+        o, log2n = attn_fwd(qkv, kvh, group, nb // 2, nb - nb // 2, fwd)
         o_rem = swap(lax.dynamic_index_in_dim(o, me ^ 1, 0, keepdims=False))
         y_out = out_proj(idx, o, o_rem, wo, x_in)
-        dyg, o, y_out = lax.optimization_barrier((dyg, o, y_out))
+        dy_d, dy_xc, dy_yc, done, y_out = fence((dy_d, dy_xc, dy_yc, done, y_out))
+        dy_dc = swap(dy_d[0]), swap(dy_d[1])
+        done = proj([(dy_x,), (dy_xc,), (dy_y,), (dy_yc,)], wo, beside, core, tok, qd // 2, 1, done)
+        do, dyg = proj([dy_d, dy_dc], wo, across, core, tok, qd // 2, 1, done)
+        do = do.reshape(n_dev, nb, s, -1)
         d_wo = lax.all_gather(grad_wo(o.reshape(tok, -1), dyg, chip_arr, n_chips), 'cp', axis_index_groups=by_core, tiled=True)
-        do = proj_far(dyg, wo, do, far, own, 1, 'far_do').reshape(n_dev, nb, s, -1)
         most = kvh - 1
         first = attn_bwd(qkv, o, do, log2n, kvh, group, 0, most)
         first_rem = swap(first)
@@ -520,11 +561,11 @@
             return spans
 
         by_q, by_k, by_v = columns(0, group), columns(group, group + 1), columns(group + 1, group + 2)
-        wq_full, wq_send = grad_wx(xg, flat, cut(by_q, wide), (n_heads,), core_arr, 'grad_wq')
+        wq_full, wq_send = grad_wx(xg, flat, cut(by_q, wide), (n_heads,), core_arr)
         wq_send, xg = lax.optimization_barrier((wq_send, xg))
         wq_recv = swap(wq_send)
         wk_full, wv_full, wk_send, wv_send = grad_wx(
-            xg, flat, cut(by_k + by_v, wide), (kv_heads, kv_heads), core_arr, 'grad_wkv')
+            xg, flat, cut(by_k + by_v, wide), (kv_heads, kv_heads), core_arr)
         wk_send, wv_send, x_late = lax.optimization_barrier((wk_send, wv_send, x_in))
         wk_recv, wv_recv = swap(wk_send), swap(wv_send)
         dx_out, d_gain = grad_x(idx, pairs, cut(by_q + by_k + by_v, wide), wide, wcat, x_late, dy_in, norm_gain[None])
@@ -543,7 +584,7 @@
     act_spec = P('dp', 'cp', None)
     mat_spec = P(None, None, None)
     grad_spec = P('dp', None, None)
-    return jax.shard_map(device_fn, mesh=mesh,
+    return jax.shard_map(compute, mesh=mesh,
                          in_specs=(act_spec, act_spec, P(None), mat_spec, mat_spec, mat_spec, mat_spec),
                          out_specs=(act_spec, act_spec, P('dp'), grad_spec, grad_spec, grad_spec, grad_spec),
                          check_vma=False)

time: 625 us -> 691 us (1.11); the launches traced: 622 us -> 680 us
  Pallas kernels: 522 us -> 560 us
  starting transfers between devices: 4.59 us -> 16.9 us
  local copies, waits for them, and re-layouts: 3.91 us -> 13.9 us
    all_gather x3 -> x1, waiting for transfers between devices: 48.5 us -> 0.02 us  [compute(): lax.all_gather(grad_wo(o.reshape(tok, -1), dyg, chip_arr, n_chips), 'cp',...]
    ppermute x0 -> x8, waiting for transfers between devices: none -> 38.5 us  [hop(): return lax.ppermute(a, 'cp', [(d, d ^ bit) for d in range(n_dev)])]
    pallas_call x5 -> x8, Pallas kernels: 184 us -> 221 us  [the longest x6 170 us: proj(): pl.pallas_call(functools.partial(proj_kernel, cb, [len(p) for p in pieces...]
    ppermute x8 -> x16, waiting for transfers between devices: 10.9 us -> 20.2 us  [swap(): return lax.ppermute(a, 'cp', pair)]
    ppermute x0 -> x8, starting transfers between devices: none -> 8.92 us  [hop(): return lax.ppermute(a, 'cp', [(d, d ^ bit) for d in range(n_dev)])]
    slice x0 -> x4, local copies, waits for them, and re-layouts: none -> 8.32 us  [the longest x2 5.3 us: compute(): xn_d = (hop(xn_x[:cut_row], 4), hop(xn_y[cut_row:], 2))]
  transfers between devices with their start and end apart: 14 -> 28, of which waited for: 6 -> 12; matrix products, arithmetic and copies ran while one was open for 1% -> 2% of each run, Pallas kernels for 74% -> 70%
where the time goes in v3:
time: 691 us; the launch traced here: 680 us
  Pallas kernels  560 us (81%)
  waiting for transfers between devices  64 us (9%)
  starting transfers between devices  16.9 us (2%)
  between operations  14.6 us (2%)
  local copies, waits for them, and re-layouts  13.9 us (2%)
  other arithmetic  11.3 us (2%)
    pallas_call x6, Pallas kernels, proj(): pl.pallas_call(functools.partial(proj_kernel, cb, [len(p) for p in pieces...  170 us
    pallas_call x2, Pallas kernels, attn_bwd(): pl.pallas_call(functools.partial(bwd_kernel, 256), grid=(nb, count), in_s...  99.1 us
    pallas_call x2, Pallas kernels, grad_wx(): pl.pallas_call(functools.partial(grad_wx_kernel, plan, len(srcs), len(hea...  97.9 us
    pallas_call x2, Pallas kernels, attn_fwd(): pl.pallas_call(functools.partial(fwd_kernel, 128), grid=(count, kvh), in_...  51 us
    pallas_call x1, Pallas kernels, merge(): pl.pallas_call(merge_kernel, grid_spec=pltpu.PrefetchScalarGridSpec(num_s...  44.1 us
    ppermute x8, waiting for transfers between devices, hop(): return lax.ppermute(a, 'cp', [(d, d ^ bit) for d in range(n_dev)])  38.5 us
    pallas_call x1, Pallas kernels, relayout(): pl.pallas_call(relayout_kernel, grid_spec=pltpu.PrefetchScalarGridSpec(nu...  32.7 us
    pallas_call x1, Pallas kernels, grad_x(): pl.pallas_call(functools.partial(dx_kernel, plan, len(srcs)), grid_spec=p...  28.9 us
  transfers between devices with their start and end apart: 28, of which 12 were waited for; matrix products, arithmetic and copies ran while one was open for 2% of the time, Pallas kernels for 70%

profile of v3, /device:TPU:0, one launch (start us, length us, event | category | flops | bytes accessed | tf_op | source)
XLA Modules:
  0.0 680.3 jit_solution(4006218304423362382)
XLA Ops:
  7.2 2.7 fusion
  10.0 0.7 convert_element_type.10
  10.7 4.7 fusion.2
  15.4 0.7 collective-permute-start.2
  16.1 2.5 collective-permute-start.1
  18.6 1.5 collective-permute-start
  20.1 0.6 add_add_fusion.tbl_ref
  20.7 32.7 %relayout.1 = (bf16[3072,5120]{1,0:T(8,128)(2,1)}, bf16[3072,2560]{1,0:T(8,128)(2,1)}) custom-call(s32[1]{0:T(128)} %bitcast.3.core_ref, bf16[3072,24,128]{2,1,0:T(8,128)(2,1)} %wq_ref.1, bf16[3072,8,128]{2,1,0:T(8,128)(2,1)} %wk_ref.1, bf16[3072,8,128]{2,1,0:T(8,128)(2,1)} %wv_ref.1), custom_call_target="tpu_custom_call" | custom-call | flops 10000000000 | bytes 62914560 | tf_op jit(solution)/shard_map/relayout/pallas_call | solution.py:48
  53.5 26.7 %shard_map.126 = (bf16[4096,2560]{1,0:T(8,128)(2,1)}, bf16[4096,3072]{1,0:T(8,128)(2,1)}) custom-call(s32[3]{0:T(128)} %add_add_fusion.tbl_ref, bf16[512,3072]{1,0:T(8,128)(2,1)} %bitcast.refs_0_, bf16[512,3072]{1,0:T(8,128)(2,1)} %collective-permute-done.2.refs_1_, bf16[3072,2560]{1,0:T(8,128)(2,1)} %get-tuple-element.76.refs_2_.refs_4_), custom_call_target="tpu_custom_call" | custom-call | flops 16106127360 | bytes 15728640 | tf_op jit(solution)/shard_map/pallas_call | solution.py:106
  80.2 7.6 %collective-permute-done.1.refs_2_ = bf16[512,3072]{1,0:T(8,128)(2,1)} collective-permute-done((bf16[512,3072]{1,0:T(8,128)(2,1)}, bf16[512,3072]{1,0:T(8,128)(2,1)}, u32[]{:S(2)}, u32[]{:S(2)}) %collective-permute-start.1) | collective-permute-done | bytes 3145760 | tf_op jit(solution)/shard_map/ppermute | solution.py:509
  87.7 1.5 collective-permute-done.refs_0_
  89.2 0.5 collective-permute-start.4
  89.7 0.7 stack.68.tbl_ref
  90.4 2.7 slice.12
  93.0 2.7 slice.13
  95.7 1.5 collective-permute-start.9
  97.2 0.5 collective-permute-start.8
  97.7 20.3 %shard_map.127 = (bf16[4096,1536]{1,0:T(8,128)(2,1)}, bf16[4096,3072]{1,0:T(8,128)(2,1)}) custom-call(s32[3]{0:T(128)} %add_add_fusion.tbl_ref, bf16[512,3072]{1,0:T(8,128)(2,1)} %bitcast.47, bf16[512,3072]{1,0:T(8,128)(2,1)} %collective-permute-done.5.refs_1_, bf16[3072,3072]{1,0:T(8,128)(2,1)} %bitcast.37), custom_call_target="tpu_custom_call" | custom-call | flops 9663676416 | bytes 9437184 | tf_op jit(solution)/shard_map/pallas_call | solution.py:106
  118.0 44.1 %shard_map.128 = (bf16[4096,2560]{1,0:T(8,128)(2,1)}, bf16[4096,3072]{1,0:T(8,128)(2,1)}) custom-call(s32[5]{0:T(128)} %stack.68.tbl_ref, bf16[512,3072]{1,0:T(8,128)(2,1)} %collective-permute-done.refs_0_, bf16[512,3072]{1,0:T(8,128)(2,1)} %collective-permute-done.3.refs_1_, ...), custom_call_target="tpu_custom_call", output_to_operand_aliasing={{0}: (6, {}), {1}: (7, {})} | custom-call | flops 32212254720 | bytes 15728640 | tf_op jit(solution)/shard_map/pallas_call | solution.py:106
  162.1 0.5 collective-permute-start.11
  162.6 1.5 collective-permute-start.7
  164.2 0.5 collective-permute-start.6
  164.7 0.6 add_add_fusion.1.tbl_ref
  165.3 0.5 collective-permute-done.10.refs_2_
  165.9 2.2 collective-permute-done.11.refs_3_
  168.1 26.8 %shard_map.129 = (bf16[4096,2560]{1,0:T(8,128)(2,1)}, bf16[4096,3072]{1,0:T(8,128)(2,1)}) custom-call(s32[3]{0:T(128)} %add_add_fusion.1.tbl_ref, bf16[256,3072]{1,0:T(8,128)(2,1)} %collective-permute-done.8.refs_0_, bf16[256,3072]{1,0:T(8,128)(2,1)} %collective-permute-done.9.refs_1_, ...), custom_call_target="tpu_custom_call", output_to_operand_aliasing={{0}: (6, {}), {1}: (7, {})} | custom-call | flops 16106127360 | bytes 15728640 | tf_op jit(solution)/shard_map/pallas_call | solution.py:106
  194.9 25.5 %attn_fwd.2 = (bf16[8,4,128,1536]{3,2,1,0:T(8,128)(2,1)}, f32[4,12,1,1024]{3,2,1,0:T(1,128)}) custom-call(bf16[8,4,128,2560]{3,2,1,0:T(8,128)(2,1)} %bitcast.24, bf16[8,4,128,2560]{3,2,1,0:T(8,128)(2,1)} %bitcast.25, bf16[8,4,128,2560]{3,2,1,0:T(8,128)(2,1)} %bitcast.26), custom_call_target="tpu_custom_call" | custom-call | flops 12884901888 | bytes 10000000 | tf_op jit(solution)/shard_map/attn_fwd/pallas_call | solution.py:169
  220.5 12.3 %collective-permute-done.7.refs_2_ = bf16[512,3072]{1,0:T(8,128)(2,1)} collective-permute-done((bf16[512,3072]{1,0:T(8,128)(2,1)S(1)}, bf16[512,3072]{1,0:T(8,128)(2,1)}, u32[]{:S(2)}, u32[]{:S(2)}) %collective-permute-start.7) | collective-permute-done | bytes 3145760 | tf_op jit(solution)/shard_map/ppermute | solution.py:509
  232.8 1.3 collective-permute-done.6.refs_0_
  234.1 0.5 collective-permute-start.15
  234.6 25.5 %attn_fwd.3 = (bf16[8,4,128,1536]{3,2,1,0:T(8,128)(2,1)}, f32[4,12,1,1024]{3,2,1,0:T(1,128)}) custom-call(bf16[8,4,128,2560]{3,2,1,0:T(8,128)(2,1)} %bitcast.27, bf16[8,4,128,2560]{3,2,1,0:T(8,128)(2,1)} %bitcast.28, bf16[8,4,128,2560]{3,2,1,0:T(8,128)(2,1)} %bitcast.29, ...), custom_call_target="tpu_custom_call", output_to_operand_aliasing={{0}: (3, {}), {1}: (4, {})} | custom-call | flops 12884901888 | bytes 10000000 | tf_op jit(solution)/shard_map/attn_fwd/pallas_call | solution.py:169
  260.1 2.7 dynamic-slice_bitcast_fusion
  262.7 1.5 slice.14
  264.2 1.5 slice.15
  265.8 0.6 collective-permute-start.13
  266.3 0.3 collective-permute-start.12
  266.6 0.6 pad_add_fusion.idx_ref
  267.2 19.8 %out_proj.1 = bf16[4,128,3072]{2,1,0:T(8,128)(2,1)} custom-call(s32[2]{0:T(128)} %pad_add_fusion.idx_ref, bf16[8,4,128,1536]{3,2,1,0:T(8,128)(2,1)} %get-tuple-element.105.loc_ref.o_ref, bf16[4,128,1536]{2,1,0:T(8,128)(2,1)} %collective-permute-done.16.rem_ref, bf16[3072,3072]{1,0:T(8,128)(2,1)} %bitcast.38, bf16[4,128,3072]{2,1,0:T(8,128)(2,1)} %refs_5_), custom_call_target="tpu_custom_call" | custom-call | flops 9663676416 | bytes 18874368 | tf_op jit(solution)/shard_map/out_proj/pallas_call | solution.py:398
  287.0 15.7 %collective-permute-done.13.refs_1_ = bf16[256,3072]{1,0:T(8,128)(2,1)} collective-permute-done((bf16[256,3072]{1,0:T(8,128)(2,1)S(1)}, bf16[256,3072]{1,0:T(8,128)(2,1)}, u32[]{:S(2)}, u32[]{:S(2)}) %collective-permute-start.13) | collective-permute-done | bytes 1572896 | tf_op jit(solution)/shard_map/ppermute | solution.py:509
  302.7 0.3 collective-permute-done.12.refs_0_
  303.0 0.5 collective-permute-start.18
  303.5 31.4 %shard_map.130 = (bf16[4096,1536]{1,0:T(8,128)(2,1)}, bf16[4096,3072]{1,0:T(8,128)(2,1)}) custom-call(s32[5]{0:T(128)} %stack.68.tbl_ref, bf16[512,3072]{1,0:T(8,128)(2,1)} %collective-permute-done.6.refs_0_, bf16[512,3072]{1,0:T(8,128)(2,1)} %collective-permute-done.14.refs_1_, ...), custom_call_target="tpu_custom_call", output_to_operand_aliasing={{0}: (6, {}), {1}: (7, {})} | custom-call | flops 19327352832 | bytes 9437184 | tf_op jit(solution)/shard_map/pallas_call | solution.py:106
  335.0 1.1 copy-done.2
  336.1 0.5 copy-done.3
  336.6 20.2 %shard_map.131 = (bf16[4096,1536]{1,0:T(8,128)(2,1)}, bf16[4096,3072]{1,0:T(8,128)(2,1)}) custom-call(s32[3]{0:T(128)} %add_add_fusion.1.tbl_ref, bf16[256,3072]{1,0:T(8,128)(2,1)} %collective-permute-done.12.refs_0_, bf16[256,3072]{1,0:T(8,128)(2,1)} %collective-permute-done.13.refs_1_, ...), custom_call_target="tpu_custom_call", output_to_operand_aliasing={{0}: (6, {}), {1}: (7, {})} | custom-call | flops 9663676416 | bytes 9437184 | tf_op jit(solution)/shard_map/pallas_call | solution.py:106
  356.9 16.4 %grad_wo.1 = f32[384,3072]{1,0:T(8,128)} custom-call(s32[1]{0:T(128)} %bitcast.19.chip_ref, bf16[4096,1536]{1,0:T(8,128)(2,1)} %bitcast.36, bf16[4096,3072]{1,0:T(8,128)(2,1)} %get-tuple-element.128.b_ref), custom_call_target="tpu_custom_call" | custom-call | flops 9663676416 | bytes 25165824 | tf_op jit(solution)/shard_map/grad_wo/pallas_call | solution.py:263
  373.3 72.5 %attn_bwd.2.refs_0_ = bf16[8,4,128,1920]{3,2,1,0:T(8,128)(2,1)} custom-call(bf16[8,4,128,2560]{3,2,1,0:T(8,128)(2,1)} %bitcast.30, bf16[8,4,128,2560]{3,2,1,0:T(8,128)(2,1)} %bitcast.31, bf16[8,4,128,2560]{3,2,1,0:T(8,128)(2,1)} %bitcast.32, bf16[8,4,128,1536]{3,2,1,0:T(8,128)(2,1)} %get-tuple-element.105.loc_ref.o_ref, bf16[8,4,128,1536]{3,2,1,0:T(8,128)(2,1)} %bitcast.41, ...), custom_call_target="tpu_custom_call" | custom-call | flops 48318382080 | bytes 10000000 | tf_op jit(solution)/shard_map/attn_bwd/pallas_call | solution.py:241
  445.8 26.7 %attn_bwd.3.refs_2_ = bf16[8,4,128,640]{3,2,1,0:T(8,128)(2,1)} custom-call(bf16[8,4,128,2560]{3,2,1,0:T(8,128)(2,1)} %bitcast.33, bf16[8,4,128,2560]{3,2,1,0:T(8,128)(2,1)} %bitcast.34, bf16[8,4,128,2560]{3,2,1,0:T(8,128)(2,1)} %bitcast.35, bf16[8,4,128,1536]{3,2,1,0:T(8,128)(2,1)} %get-tuple-element.105.loc_ref.o_ref, bf16[8,4,128,1536]{3,2,1,0:T(8,128)(2,1)} %bitcast.42, ...), custom_call_target="tpu_custom_call" | custom-call | flops 16106127360 | bytes 10000000 | tf_op jit(solution)/shard_map/attn_bwd/pallas_call | solution.py:241
  472.5 0.5 collective-permute-start.20
  473.0 17.3 %collective-permute-done.20.refs_3_ = bf16[8,4,128,640]{3,2,1,0:T(8,128)(2,1)} collective-permute-done((bf16[8,4,128,640]{3,2,1,0:T(8,128)(2,1)}, bf16[8,4,128,640]{3,2,1,0:T(8,128)(2,1)}, u32[]{:S(2)}, u32[]{:S(2)}) %collective-permute-start.20) | collective-permute-done | bytes 5242912 | tf_op jit(solution)/shard_map/ppermute | solution.py:496
  490.3 53.6 %shard_map.132 = (f32[3072,24,128]{2,1,0:T(8,128)}, f32[1536,24,128]{2,1,0:T(8,128)}) custom-call(s32[1]{0:T(128)} %bitcast.3.core_ref, bf16[4096,3072]{1,0:T(8,128)(2,1)} %get-tuple-element.123.a_ref, bf16[4096,1920]{1,0:T(8,128)(2,1)} %bitcast.45, bf16[4096,1920]{1,0:T(8,128)(2,1)} %bitcast.16.refs_1_, bf16[4096,640]{1,0:T(8,128)(2,1)} %bitcast.43, ...), custom_call_target="tpu_custom_call" | custom-call | flops 38654705664 | bytes 25165824 | tf_op jit(solution)/shard_map/pallas_call | solution.py:329
  543.9 0.6 collective-permute-start.21
  544.5 44.3 %shard_map.133 = (f32[3072,8,128]{2,1,0:T(8,128)}, f32[3072,8,128]{2,1,0:T(8,128)}, f32[1536,8,128]{2,1,0:T(8,128)}, f32[1536,8,128]{2,1,0:T(8,128)}) custom-call(s32[1]{0:T(128)} %bitcast.3.core_ref, bf16[4096,3072]{1,0:T(8,128)(2,1)} %get-tuple-element.123.a_ref, bf16[4096,1920]{1,0:T(8,128)(2,1)} %bitcast.46, bf16[4096,1920]{1,0:T(8,128)(2,1)} %bitcast.16.refs_1_, ...), custom_call_target="tpu_custom_call" | custom-call | flops 25769803776 | bytes 25165824 | tf_op jit(solution)/shard_map/pallas_call | solution.py:329
  589.0 0.4 collective-permute-start.23
  589.4 0.6 broadcast_in_dim.10.refs_7_
  590.0 28.9 %grad_x.1 = (bf16[4,128,3072]{2,1,0:T(8,128)(2,1)}, f32[1,3072]{1,0:T(1,128)}) custom-call(s32[2]{0:T(128)} %pad_add_fusion.idx_ref, bf16[8,4,128,1920]{3,2,1,0:T(8,128)(2,1)} %attn_bwd.2.refs_0_, bf16[8,4,128,1920]{3,2,1,0:T(8,128)(2,1)} %collective-permute-done.19.refs_1_, bf16[8,4,128,640]{3,2,1,0:T(8,128)(2,1)} %attn_bwd.3.refs_2_, ...), custom_call_target="tpu_custom_call" | custom-call | flops 16106127360 | bytes 18874368 | tf_op jit(solution)/shard_map/grad_x/pallas_call | solution.py:464
  618.8 1.4 collective-permute-done.24
  620.2 0.7 add.33
  620.9 1.7 collective-permute-start.25
  622.6 2.0 collective-permute-done.25
  624.6 1.8 collective-permute-start.26
  626.4 1.9 collective-permute-done.26
  628.3 0.6 add.35
  629.0 44.1 %merge.1 = (f32[3072,24,128]{2,1,0:T(8,128)}, f32[3072,8,128]{2,1,0:T(8,128)}, f32[3072,8,128]{2,1,0:T(8,128)}, f32[3072,3072]{1,0:T(8,128)}) custom-call(s32[1]{0:T(128)} %bitcast.3.core_ref, f32[3072,24,128]{2,1,0:T(8,128)} %get-tuple-element.134.refs_0_, ...), custom_call_target="tpu_custom_call", output_to_operand_aliasing={{0}: (1, {}), {1}: (2, {}), {2}: (3, {})} | custom-call | flops 10000000000 | bytes 100000000 | tf_op jit(solution)/shard_map/merge/pallas_call | solution.py:360
  (37 shorter events, 0.4 us)
Async XLA Ops:
  7.2 13.0 %copy-start = (bf16[4,128,3072]{2,1,0:T(8,128)(2,1)S(1)}, bf16[4,128,3072]{2,1,0:T(8,128)(2,1)}, u32[]{:S(2)}) copy-start(bf16[4,128,3072]{2,1,0:T(8,128)(2,1)} %refs_6_.1) | copy-start | bytes 9437188
  7.2 621.8 %all-gather.2.cloned.1.call-start = ((), (), s32[]{:S(2)}) async-start(), calls=%async_computation | async-start | bytes 42467328 | tf_op jit(solution)/shard_map/all_gather | solution.py:544
  15.4 38.0 %collective-permute-start.2 = (bf16[512,3072]{1,0:T(8,128)(2,1)}, bf16[512,3072]{1,0:T(8,128)(2,1)}, u32[]{:S(2)}, u32[]{:S(2)}) collective-permute-start(bf16[512,3072]{1,0:T(8,128)(2,1)} %bitcast.refs_0_), channel_id=1, source_target_pairs={{0,1},{1,0},{2,3},{3,2},{4,5},{5,4},{6,7},{7,6},{8,9},{9,8},{10,11... | collective-permute-start | bytes 9437192 | tf_op jit(solution)/shard_map/ppermute | solution.py:496
  16.1 71.6 %collective-permute-start.1 = (bf16[512,3072]{1,0:T(8,128)(2,1)}, bf16[512,3072]{1,0:T(8,128)(2,1)}, u32[]{:S(2)}, u32[]{:S(2)}) collective-permute-start(bf16[512,3072]{1,0:T(8,128)(2,1)} %bitcast.refs_0_), channel_id=1, source_target_pairs={{0,4},{1,5},{2,6},{3,7},{4,0},{5,1},{6,2},{7,3},{8,12},{9,13},{10,... | collective-permute-start | bytes 9437192 | tf_op jit(solution)/shard_map/ppermute | solution.py:509
  18.6 70.5 %collective-permute-start = (bf16[512,3072]{1,0:T(8,128)(2,1)}, bf16[512,3072]{1,0:T(8,128)(2,1)}, u32[]{:S(2)}, u32[]{:S(2)}) collective-permute-start(bf16[512,3072]{1,0:T(8,128)(2,1)} %bitcast.refs_0_), channel_id=1, source_target_pairs={{0,2},{1,3},{2,0},{3,1},{4,6},{5,7},{6,4},{7,5},{8,10},{9,11},{10,... | collective-permute-start | bytes 9437192 | tf_op jit(solution)/shard_map/ppermute | solution.py:509
  20.1 77.6 %collective-permute-start.5 = (bf16[512,3072]{1,0:T(8,128)(2,1)S(1)}, bf16[512,3072]{1,0:T(8,128)(2,1)}, u32[]{:S(2)}, u32[]{:S(2)}) collective-permute-start(bf16[512,3072]{1,0:T(8,128)(2,1)S(1)} %bitcast.48), channel_id=1, source_target_pairs={{0,1},{1,0},{2,3},{3,2},{4,5},{5,4},{6,7},{7,6},{8,9},{9,8},{10,11... | collective-permute-start | bytes 9437192 | tf_op jit(solution)/shard_map/ppermute | solution.py:496
  89.2 28.8 %collective-permute-start.3 = (bf16[512,3072]{1,0:T(8,128)(2,1)}, bf16[512,3072]{1,0:T(8,128)(2,1)}, u32[]{:S(2)}, u32[]{:S(2)}) collective-permute-start(bf16[512,3072]{1,0:T(8,128)(2,1)} %collective-permute-done.refs_0_), channel_id=1, source_target_pairs={{0,1},{1,0},{2,3},{3,2},{4,5},{5,4},{6,7},{7,6},{8,9},{9,8},{10,11... | collective-permute-start | bytes 9437192 | tf_op jit(solution)/shard_map/ppermute | solution.py:496
  89.2 28.8 %collective-permute-start.4 = (bf16[512,3072]{1,0:T(8,128)(2,1)}, bf16[512,3072]{1,0:T(8,128)(2,1)}, u32[]{:S(2)}, u32[]{:S(2)}) collective-permute-start(bf16[512,3072]{1,0:T(8,128)(2,1)} %collective-permute-done.1.refs_2_), channel_id=1, source_target_pairs={{0,1},{1,0},{2,3},{3,2},{4,5},{5,4},{6,7},{7,6},{8,9},{9,8},{10,11... | collective-permute-start | bytes 9437192 | tf_op jit(solution)/shard_map/ppermute | solution.py:496
  95.7 66.4 %collective-permute-start.9 = (bf16[256,3072]{1,0:T(8,128)(2,1)}, bf16[256,3072]{1,0:T(8,128)(2,1)}, u32[]{:S(2)}, u32[]{:S(2)}) collective-permute-start(bf16[256,3072]{1,0:T(8,128)(2,1)} %slice.13), channel_id=1, source_target_pairs={{0,2},{1,3},{2,0},{3,1},{4,6},{5,7},{6,4},{7,5},{8,10},{9,11},{10,... | collective-permute-start | bytes 4718600 | tf_op jit(solution)/shard_map/ppermute | solution.py:509
  97.2 64.9 %collective-permute-start.8 = (bf16[256,3072]{1,0:T(8,128)(2,1)}, bf16[256,3072]{1,0:T(8,128)(2,1)}, u32[]{:S(2)}, u32[]{:S(2)}) collective-permute-start(bf16[256,3072]{1,0:T(8,128)(2,1)} %slice.12), channel_id=1, source_target_pairs={{0,4},{1,5},{2,6},{3,7},{4,0},{5,1},{6,2},{7,3},{8,12},{9,13},{10,... | collective-permute-start | bytes 4718600 | tf_op jit(solution)/shard_map/ppermute | solution.py:509
  118.0 44.7 %copy-start.1 = (bf16[4,128,3072]{2,1,0:T(8,128)(2,1)S(1)}, bf16[4,128,3072]{2,1,0:T(8,128)(2,1)}, u32[]{:S(2)}) copy-start(bf16[4,128,3072]{2,1,0:T(8,128)(2,1)} %refs_6_.1) | copy-start | bytes 9437188
  162.1 3.8 collective-permute-start.10
  162.1 6.0 collective-permute-start.11
  162.6 70.2 %collective-permute-start.7 = (bf16[512,3072]{1,0:T(8,128)(2,1)S(1)}, bf16[512,3072]{1,0:T(8,128)(2,1)}, u32[]{:S(2)}, u32[]{:S(2)}) collective-permute-start(bf16[512,3072]{1,0:T(8,128)(2,1)S(1)} %bitcast.49), channel_id=1, source_target_pairs={{0,4},{1,5},{2,6},{3,7},{4,0},{5,1},{6,2},{7,3},{8,12},{9,13},{10,... | collective-permute-start | bytes 9437192 | tf_op jit(solution)/shard_map/ppermute | solution.py:509
  164.2 69.9 %collective-permute-start.6 = (bf16[512,3072]{1,0:T(8,128)(2,1)S(1)}, bf16[512,3072]{1,0:T(8,128)(2,1)}, u32[]{:S(2)}, u32[]{:S(2)}) collective-permute-start(bf16[512,3072]{1,0:T(8,128)(2,1)S(1)} %bitcast.50), channel_id=1, source_target_pairs={{0,2},{1,3},{2,0},{3,1},{4,6},{5,7},{6,4},{7,5},{8,10},{9,11},{10,... | collective-permute-start | bytes 9437192 | tf_op jit(solution)/shard_map/ppermute | solution.py:509
  234.1 68.9 %collective-permute-start.14 = (bf16[512,3072]{1,0:T(8,128)(2,1)}, bf16[512,3072]{1,0:T(8,128)(2,1)}, u32[]{:S(2)}, u32[]{:S(2)}) collective-permute-start(bf16[512,3072]{1,0:T(8,128)(2,1)} %collective-permute-done.6.refs_0_), channel_id=1, source_target_pairs={{0,1},{1,0},{2,3},{3,2},{4,5},{5,4},{6,7},{7,6},{8,9},{9,8},{10,11... | collective-permute-start | bytes 9437192 | tf_op jit(solution)/shard_map/ppermute | solution.py:496
  234.1 68.9 %collective-permute-start.15 = (bf16[512,3072]{1,0:T(8,128)(2,1)}, bf16[512,3072]{1,0:T(8,128)(2,1)}, u32[]{:S(2)}, u32[]{:S(2)}) collective-permute-start(bf16[512,3072]{1,0:T(8,128)(2,1)} %collective-permute-done.7.refs_2_), channel_id=1, source_target_pairs={{0,1},{1,0},{2,3},{3,2},{4,5},{5,4},{6,7},{7,6},{8,9},{9,8},{10,11... | collective-permute-start | bytes 9437192 | tf_op jit(solution)/shard_map/ppermute | solution.py:496
  262.7 4.5 collective-permute-start.16
  265.8 36.9 %collective-permute-start.13 = (bf16[256,3072]{1,0:T(8,128)(2,1)S(1)}, bf16[256,3072]{1,0:T(8,128)(2,1)}, u32[]{:S(2)}, u32[]{:S(2)}) collective-permute-start(bf16[256,3072]{1,0:T(8,128)(2,1)S(1)} %slice.15), channel_id=1, source_target_pairs={{0,2},{1,3},{2,0},{3,1},{4,6},{5,7},{6,4},{7,5},{8,10},{9,11},{10,... | collective-permute-start | bytes 4718600 | tf_op jit(solution)/shard_map/ppermute | solution.py:509
  266.3 36.6 %collective-permute-start.12 = (bf16[256,3072]{1,0:T(8,128)(2,1)S(1)}, bf16[256,3072]{1,0:T(8,128)(2,1)}, u32[]{:S(2)}, u32[]{:S(2)}) collective-permute-start(bf16[256,3072]{1,0:T(8,128)(2,1)S(1)} %slice.14), channel_id=1, source_target_pairs={{0,4},{1,5},{2,6},{3,7},{4,0},{5,1},{6,2},{7,3},{8,12},{9,13},{10,... | collective-permute-start | bytes 4718600 | tf_op jit(solution)/shard_map/ppermute | solution.py:509
  303.0 32.0 %collective-permute-start.17 = (bf16[256,3072]{1,0:T(8,128)(2,1)}, bf16[256,3072]{1,0:T(8,128)(2,1)S(1)}, u32[]{:S(2)}, u32[]{:S(2)}) collective-permute-start(bf16[256,3072]{1,0:T(8,128)(2,1)} %collective-permute-done.12.refs_0_), channel_id=1, source_target_pairs={{0,1},{1,0},{2,3},{3,2},{4,5},{5,4},{6,7},{7,6},{8,9},{9,8},{10,11... | collective-permute-start | bytes 4718600 | tf_op jit(solution)/shard_map/ppermute | solution.py:496
  303.0 32.0 %collective-permute-start.18 = (bf16[256,3072]{1,0:T(8,128)(2,1)}, bf16[256,3072]{1,0:T(8,128)(2,1)S(1)}, u32[]{:S(2)}, u32[]{:S(2)}) collective-permute-start(bf16[256,3072]{1,0:T(8,128)(2,1)} %collective-permute-done.13.refs_1_), channel_id=1, source_target_pairs={{0,1},{1,0},{2,3},{3,2},{4,5},{5,4},{6,7},{7,6},{8,9},{9,8},{10,11... | collective-permute-start | bytes 4718600 | tf_op jit(solution)/shard_map/ppermute | solution.py:496
  334.9 1.1 copy-start.2
  334.9 1.7 copy-start.3
  445.8 44.5 %collective-permute-start.19 = (bf16[8,4,128,1920]{3,2,1,0:T(8,128)(2,1)}, bf16[8,4,128,1920]{3,2,1,0:T(8,128)(2,1)}, u32[]{:S(2)}, u32[]{:S(2)}) collective-permute-start(bf16[8,4,128,1920]{3,2,1,0:T(8,128)(2,1)} %attn_bwd.2.refs_0_), channel_id=1, source_target_pairs={{0,1},{1,0},{2,3},{3,2},{4,5},{5,4},{6,7},{7,6},{8,9},{9,8},{10,11... | collective-permute-start | bytes 47185928 | tf_op jit(solution)/shard_map/ppermute | solution.py:496
  472.5 17.8 %collective-permute-start.20 = (bf16[8,4,128,640]{3,2,1,0:T(8,128)(2,1)}, bf16[8,4,128,640]{3,2,1,0:T(8,128)(2,1)}, u32[]{:S(2)}, u32[]{:S(2)}) collective-permute-start(bf16[8,4,128,640]{3,2,1,0:T(8,128)(2,1)} %attn_bwd.3.refs_2_), channel_id=1, source_target_pairs={{0,1},{1,0},{2,3},{3,2},{4,5},{5,4},{6,7},{7,6},{8,9},{9,8},{10,11... | collective-permute-start | bytes 15728648 | tf_op jit(solution)/shard_map/ppermute | solution.py:496
  543.8 45.5 %copy-start.4 = (bf16[3072]{0:T(1024)(128)(2,1)S(1)}, bf16[3072]{0:T(1024)(128)(2,1)}, u32[]{:S(2)}) copy-start(bf16[3072]{0:T(1024)(128)(2,1)} %param.9) | copy-start | bytes 18436
  543.9 85.1 %collective-permute-start.21 = (f32[1536,24,128]{2,1,0:T(8,128)}, f32[1536,24,128]{2,1,0:T(8,128)}, u32[]{:S(2)}, u32[]{:S(2)}) collective-permute-start(f32[1536,24,128]{2,1,0:T(8,128)} %get-tuple-element.122), channel_id=1, source_target_pairs={{0,1},{1,0},{2,3},{3,2},{4,5},{5,4},{6,7},{7,6},{8,9},{9,8},{10,11... | collective-permute-start | bytes 56623112 | tf_op jit(solution)/shard_map/ppermute | solution.py:496
  588.8 40.1 %collective-permute-start.22 = (f32[1536,8,128]{2,1,0:T(8,128)}, f32[1536,8,128]{2,1,0:T(8,128)}, u32[]{:S(2)}, u32[]{:S(2)}) collective-permute-start(f32[1536,8,128]{2,1,0:T(8,128)} %get-tuple-element.126), channel_id=1, source_target_pairs={{0,1},{1,0},{2,3},{3,2},{4,5},{5,4},{6,7},{7,6},{8,9},{9,8},{10,11... | collective-permute-start | bytes 18874376 | tf_op jit(solution)/shard_map/ppermute | solution.py:496
  589.0 40.0 %collective-permute-start.23 = (f32[1536,8,128]{2,1,0:T(8,128)}, f32[1536,8,128]{2,1,0:T(8,128)}, u32[]{:S(2)}, u32[]{:S(2)}) collective-permute-start(f32[1536,8,128]{2,1,0:T(8,128)} %get-tuple-element.127), channel_id=1, source_target_pairs={{0,1},{1,0},{2,3},{3,2},{4,5},{5,4},{6,7},{7,6},{8,9},{9,8},{10,11... | collective-permute-start | bytes 18874376 | tf_op jit(solution)/shard_map/ppermute | solution.py:496
  618.8 1.4 collective-permute-start.24
  620.9 3.7 collective-permute-start.25
  624.6 3.7 collective-permute-start.26
Sparse Core Ops, SparseCore 0:
  373.4 178.4 all-gather.1

commit v4 on v2

--- a/solution.py
+++ b/solution.py
@@ -323,12 +323,12 @@
 
 
 def merge_kernel(core_ref, *refs):
-    n = (len(refs) - 2) // 3
-    for i in range(n + 1):
-        refs[2 * n + 1 + i][...] = refs[n + i][...]
-
-
-def merge(fulls, recvs, gathered, core):
+    n = len(refs) // 3
+    for i in range(n):
+        refs[2 * n + i][...] = refs[n + i][...]
+
+
+def merge(fulls, recvs, core):
     steps = 12
     n = len(fulls)
 
@@ -343,85 +343,82 @@
         merge_kernel,
         grid_spec=pltpu.PrefetchScalarGridSpec(
             num_scalar_prefetch=1, grid=(steps,),
-            in_specs=[pl.BlockSpec(memory_space=pl.ANY)] * n + [spec(r, True) for r in recvs] + [spec(gathered, True)],
-            out_specs=[spec(r, False) for r in recvs] + [spec(gathered, True)]),
-        out_shape=[jax.ShapeDtypeStruct(f.shape, f.dtype) for f in fulls] + [jax.ShapeDtypeStruct(gathered.shape, gathered.dtype)],
+            in_specs=[pl.BlockSpec(memory_space=pl.ANY)] * n + [spec(r, True) for r in recvs],
+            out_specs=[spec(r, False) for r in recvs]),
+        out_shape=[jax.ShapeDtypeStruct(f.shape, f.dtype) for f in fulls],
         input_output_aliases={1 + i: i for i in range(n)},
-        compiler_params=BIG, cost_estimate=cost(1e10, 10 ** 8), name='merge')(core, *fulls, *recvs, gathered)
-
-
-def y_kernel(idx_ref, loc_ref, rem_ref, w_ref, x_ref, y_ref, acc):
-    k = pl.program_id(0)
-    per = pl.num_programs(0) // 2
-    nb, s, dm = x_ref.shape
-    tok = nb * s
-    mine = k // per == idx_ref[0]
-    part = dot(jnp.where(mine, loc_ref[...].reshape(tok, -1), rem_ref[...].reshape(tok, -1)), w_ref[...], 1, 0)
-
-    @pl.when(k == 0)
+        cost_estimate=cost(1e10, 10 ** 8), name='merge')(core, *fulls, *recvs)
+
+
+def y_kernel(idx_ref, loc_ref, rem_ref, w_ref, x_ref, y_ref, lhs):
+    nb, s, _ = x_ref.shape
+    half = loc_ref.shape[3]
+
+    @pl.when(pl.program_id(0) == 0)
     def _():
-        acc[...] = part
-
-    @pl.when(k > 0)
-    def _():
-        acc[...] += part
-
-    @pl.when(k == 2 * per - 1)
-    def _():
-        for b in range(nb):
-            y_ref[b] = (x_ref[b].astype(jnp.float32) + acc[b * s:(b + 1) * s]).astype(jnp.bfloat16)
+        first = idx_ref[0] == 0
+        loc = loc_ref[...].reshape(nb * s, half)
+        rem = rem_ref[...].reshape(nb * s, half)
+        lhs[:, :half] = jnp.where(first, loc, rem)
+        lhs[:, half:] = jnp.where(first, rem, loc)
+
+    acc = dot(lhs[...], w_ref[...], 1, 0)
+    for b in range(nb):
+        y_ref[b] = (x_ref[b].astype(jnp.float32) + acc[b * s:(b + 1) * s]).astype(jnp.bfloat16)
 
 
 def out_proj(idx, o, o_rem, wo, x):
     nb, s, dm = x.shape
-    wide = 768
-    per = o.shape[3] // wide
-    whole = pl.BlockSpec((nb, s, dm), lambda k, i: (0, 0, 0))
+    half = o.shape[3]
+    wide = 512
+    cols = pl.BlockSpec((nb, s, wide), lambda k, i: (0, 0, k))
     return pl.pallas_call(
         y_kernel,
         grid_spec=pltpu.PrefetchScalarGridSpec(
-            num_scalar_prefetch=1, grid=(2 * per,),
-            in_specs=[pl.BlockSpec((1, nb, s, wide), lambda k, i: (i[1], 0, 0, lax.rem(k, per))),
-                      pl.BlockSpec((nb, s, wide), lambda k, i: (0, 0, lax.rem(k, per))),
-                      pl.BlockSpec((wide, dm), lambda k, i: (k, 0)), whole],
-            out_specs=whole, scratch_shapes=[pltpu.VMEM((nb * s, dm), jnp.float32)]),
+            num_scalar_prefetch=1, grid=(dm // wide,),
+            in_specs=[pl.BlockSpec((1, nb, s, half), lambda k, i: (i[1], 0, 0, 0)),
+                      pl.BlockSpec((nb, s, half), lambda k, i: (0, 0, 0)),
+                      pl.BlockSpec((2 * half, wide), lambda k, i: (0, k)), cols],
+            out_specs=cols, scratch_shapes=[pltpu.VMEM((nb * s, 2 * half), jnp.bfloat16)]),
         out_shape=jax.ShapeDtypeStruct(x.shape, jnp.bfloat16),
         compiler_params=BIG, cost_estimate=cost(2 * nb * s * dm * dm, 2 * dm * dm), name='out_proj')(idx, o, o_rem, wo, x)
 
 
-def dx_kernel(plan, n_src, idx_ref, *refs):
+def dx_kernel(spans, n_src, idx_ref, *refs):
     srcs = refs[:2 * n_src]
-    w_ref, x_ref, dy_ref, g_ref, dx_ref, dg_ref, acc = refs[2 * n_src:]
-    k = pl.program_id(0)
-    nb, s, dm = x_ref.shape
-    for pos, pieces in enumerate(plan):
-        @pl.when(k == pos)
-        def _(pos=pos, pieces=pieces):
-            cols = []
-            for half, which, lo, hi in pieces:
-                loc, rem = srcs[2 * which], srcs[2 * which + 1]
-                cols.append(jnp.where(idx_ref[0] == half, loc[0, :, :, lo:hi].reshape(nb * s, hi - lo),
-                                      rem[0, :, :, lo:hi].reshape(nb * s, hi - lo)))
-            part = dot(jnp.concatenate(cols, axis=1), w_ref[...], 1, 1)
-            if pos == 0:
-                acc[...] = part
-            else:
-                acc[...] += part
-
-    @pl.when(k == len(plan) - 1)
+    w_ref, x_ref, dy_ref, g_ref, from_ref, dx_ref, dg_ref, to_ref, lhs, acc = refs[2 * n_src:]
+    n = pl.program_id(0)
+    wide = w_ref.shape[0]
+    steps = acc.shape[1] // wide
+    tok, s = acc.shape[0], x_ref.shape[1]
+
+    @pl.when(n == 0)
     def _():
+        at = 0
+        for half, which, lo, hi in spans:
+            loc, rem = srcs[2 * which], srcs[2 * which + 1]
+            lhs[:, at:at + hi - lo] = jnp.where(idx_ref[0] == half, loc[0, :, :, lo:hi].reshape(tok, hi - lo),
+                                                rem[0, :, :, lo:hi].reshape(tok, hi - lo))
+            at += hi - lo
+
+    @pl.when(n < steps)
+    def _():
+        acc[:, pl.ds(pl.multiple_of(n * wide, wide), wide)] = dot(lhs[...], w_ref[...], 1, 1)
+        to_ref[...] = from_ref[...]
+
+    @pl.when(n >= steps)
+    def _():
+        b = n - steps
         gain = g_ref[...].astype(jnp.float32)
-        total = jnp.zeros((1, dm), jnp.float32)
-        for b in range(nb):
-            x32 = x_ref[b].astype(jnp.float32)
-            inv = lax.rsqrt(jnp.mean(x32 * x32, axis=-1, keepdims=True) + EPS)
-            unit = x32 * inv
-            d_norm = acc[b * s:(b + 1) * s]
-            total = total + jnp.sum(d_norm * unit, axis=0, keepdims=True)
-            e = d_norm * gain
-            d_x = inv * (e - unit * jnp.mean(e * unit, axis=-1, keepdims=True))
-            dx_ref[b] = (dy_ref[b].astype(jnp.float32) + d_x).astype(jnp.bfloat16)
-        dg_ref[...] = total
+        x32 = x_ref[0].astype(jnp.float32)
+        inv = lax.rsqrt(jnp.mean(x32 * x32, axis=-1, keepdims=True) + EPS)
+        unit = x32 * inv
+        d_norm = acc[pl.ds(pl.multiple_of(b * s, s), s), :]
+        part = jnp.sum(d_norm * unit, axis=0, keepdims=True)
+        dg_ref[...] = jnp.where(b == 0, part, dg_ref[...] + part)
+        e = d_norm * gain
+        d_x = inv * (e - unit * jnp.mean(e * unit, axis=-1, keepdims=True))
+        dx_ref[0] = (dy_ref[0].astype(jnp.float32) + d_x).astype(jnp.bfloat16)
 
 
 def cut(spans, wide):
@@ -438,21 +435,28 @@
     return plan
 
 
-def grad_x(idx, srcs, plan, wide, wcat, x, dy, gain):
+def grad_x(idx, srcs, spans, wcat, x, dy, gain, gathered):
     nb, s, dm = x.shape
+    cols = wcat.shape[1]
+    wide = 256
+    steps = dm // wide
+    rows = gathered.shape[0] // steps
     flat = [a for pair in srcs for a in pair]
-    whole = pl.BlockSpec((nb, s, dm), lambda k, i: (0, 0, 0))
+    seq = pl.BlockSpec((1, s, dm), lambda k, i: (jnp.maximum(k - steps, 0), 0, 0))
     line = pl.BlockSpec((1, dm), lambda k, i: (0, 0))
-    return pl.pallas_call(
-        functools.partial(dx_kernel, plan, len(srcs)),
-        grid_spec=pltpu.PrefetchScalarGridSpec(
-            num_scalar_prefetch=1, grid=(len(plan),),
+    share = pl.BlockSpec((rows, gathered.shape[1]), lambda k, i: (jnp.minimum(k, steps - 1), 0))
+    return pl.pallas_call(
+        functools.partial(dx_kernel, spans, len(srcs)),
+        grid_spec=pltpu.PrefetchScalarGridSpec(
+            num_scalar_prefetch=1, grid=(steps + nb,),
             in_specs=[pl.BlockSpec((1, nb, s, a.shape[3]), lambda k, i: (i[1], 0, 0, 0)) for a in flat]
-            + [pl.BlockSpec((dm, wide), lambda k, i: (0, k)), whole, whole, line],
-            out_specs=[whole, line], scratch_shapes=[pltpu.VMEM((nb * s, dm), jnp.float32)]),
-        out_shape=[jax.ShapeDtypeStruct(x.shape, jnp.bfloat16), jax.ShapeDtypeStruct((1, dm), jnp.float32)],
-        compiler_params=BIG, cost_estimate=cost(2 * nb * s * dm * wide * len(plan), 2 * dm * dm),
-        name='grad_x')(idx, *flat, wcat, x, dy, gain)
+            + [pl.BlockSpec((wide, cols), lambda k, i: (jnp.minimum(k, steps - 1), 0)), seq, seq, line, share],
+            out_specs=[seq, line, share],
+            scratch_shapes=[pltpu.VMEM((nb * s, cols), jnp.bfloat16), pltpu.VMEM((nb * s, dm), jnp.float32)]),
+        out_shape=[jax.ShapeDtypeStruct(x.shape, jnp.bfloat16), jax.ShapeDtypeStruct((1, dm), jnp.float32),
+                   jax.ShapeDtypeStruct(gathered.shape, gathered.dtype)],
+        compiler_params=BIG, cost_estimate=cost(2 * nb * s * dm * cols, 2 * dm * cols),
+        name='grad_x')(idx, *flat, wcat, x, dy, gain, gathered)
 
 
 def solution(mesh):
@@ -527,15 +531,15 @@
             xg, flat, cut(by_k + by_v, wide), (kv_heads, kv_heads), core_arr, 'grad_wkv')
         wk_send, wv_send, x_late = lax.optimization_barrier((wk_send, wv_send, x_in))
         wk_recv, wv_recv = swap(wk_send), swap(wv_send)
-        dx_out, d_gain = grad_x(idx, pairs, cut(by_q + by_k + by_v, wide), wide, wcat, x_late, dy_in, norm_gain[None])
+        dx_out, d_gain, d_wo = grad_x(idx, pairs, by_q + by_k + by_v, wcat, x_late, dy_in, norm_gain[None], d_wo)
         d_gain = d_gain[0]
 
         def add_from(bit, a):
             return a + lax.ppermute(a, 'cp', [(d, d ^ bit) for d in range(n_dev)])
 
         d_gain = add_from(2, add_from(1, d_gain))
-        wq_recv, wk_recv, wv_recv, d_wo, dx_out = lax.optimization_barrier((wq_recv, wk_recv, wv_recv, d_wo, dx_out))
-        d_wq, d_wk, d_wv, d_wo = merge((wq_full, wk_full, wv_full), (wq_recv, wk_recv, wv_recv), d_wo, core_arr)
+        wq_recv, wk_recv, wv_recv, dx_out = lax.optimization_barrier((wq_recv, wk_recv, wv_recv, dx_out))
+        d_wq, d_wk, d_wv = merge((wq_full, wk_full, wv_full), (wq_recv, wk_recv, wv_recv), core_arr)
         d_gain = add_from(4, d_gain)
         d_wo = d_wo.reshape(n_heads, HD, dm)
         return y_out, dx_out, d_gain, d_wq, d_wk, d_wv, d_wo

time: 625 us -> 620 us (level)
    pallas_call x1, Pallas kernels: 28.7 us -> 50.9 us  [grad_x(): pl.pallas_call(functools.partial(dx_kernel, spans, len(srcs)), grid_spec=...]
    pallas_call x1, Pallas kernels: 44.1 us -> 23.8 us  [merge(): pl.pallas_call(merge_kernel, grid_spec=pltpu.PrefetchScalarGridSpec(num_s...]
  transfers between devices with their start and end apart: 14 -> 14, of which waited for: 6 -> 5; matrix products, arithmetic and copies ran while one was open for 1% -> 1% of each run, Pallas kernels for 74% -> 82%
where the time goes in v4:
time: 620 us; the launch traced here: 617 us
  Pallas kernels  520 us (84%)
  waiting for transfers between devices  63.2 us (10%)
  between operations  14 us (2%)
  other arithmetic  10.7 us (2%)
    pallas_call x2, Pallas kernels, attn_bwd(): pl.pallas_call(functools.partial(bwd_kernel, 256), grid=(nb, count), in_s...  98.3 us
    pallas_call x2, Pallas kernels, grad_wx(): pl.pallas_call(functools.partial(grad_wx_kernel, plan, len(srcs), len(hea...  97.4 us
    pallas_call x2, Pallas kernels, proj_far(): pl.pallas_call(functools.partial(far_kernel, cb), grid_spec=pltpu.Prefetc...  95.2 us
    pallas_call x1, Pallas kernels, grad_x(): pl.pallas_call(functools.partial(dx_kernel, spans, len(srcs)), grid_spec=...  50.9 us
    pallas_call x1, Pallas kernels, attn_fwd(): pl.pallas_call(functools.partial(fwd_kernel, 128), grid=(nb, kvh), in_spe...  49 us
    all_gather x1, waiting for transfers between devices, device_fn(): xg = lax.all_gather(xn, 'cp', tiled=True)  48.5 us
    pallas_call x2, Pallas kernels, proj_near(): pl.pallas_call(functools.partial(near_kernel, cb), grid_spec=pltpu.Prefet...  40.2 us
    pallas_call x1, Pallas kernels, relayout(): pl.pallas_call(relayout_kernel, grid_spec=pltpu.PrefetchScalarGridSpec(nu...  32.9 us
  transfers between devices with their start and end apart: 14, of which 5 were waited for; matrix products, arithmetic and copies ran while one was open for 1% of the time, Pallas kernels for 82%

profile of v4, /device:TPU:0, one launch (start us, length us, event | category | flops | bytes accessed | tf_op | source)
XLA Modules:
  0.0 617.1 jit_solution(5111307459795335165)
XLA Ops:
  7.2 0.0 all-gather.6.cloned.1.call-start
  7.2 2.6 fusion
  9.8 0.7 convert_element_type.10
  10.5 0.0 copy-start
  10.5 4.9 fusion.2
  15.4 0.0 all-gather.6.cloned.1.call-update
  15.4 0.0 all-gather.4.cloned.1.call-start
  15.5 0.7 all-gather.4.cloned.1.call-update
  16.2 0.0 all-gather.8.cloned.1.call-start
  16.2 0.0 copy-done
  16.2 0.8 collective-permute-start.1
  17.0 0.1 collective-permute-start
  17.1 0.6 stack.46.tbl_ref
  17.7 0.6 pad_add_fusion.tbl_ref
  18.3 32.9 %relayout.1 = (bf16[3072,5120]{1,0:T(8,128)(2,1)}, bf16[3072,2560]{1,0:T(8,128)(2,1)}) custom-call(s32[1]{0:T(128)} %bitcast.7.core_ref, bf16[3072,24,128]{2,1,0:T(8,128)(2,1)} %wq_ref.1, bf16[3072,8,128]{2,1,0:T(8,128)(2,1)} %wk_ref.1, bf16[3072,8,128]{2,1,0:T(8,128)(2,1)} %wv_ref.1), custom_call_target="tpu_custom_call" | custom-call | flops 10000000000 | bytes 62914560 | tf_op jit(solution)/shard_map/relayout/pallas_call | solution.py:47
  51.2 0.0 collective-permute-done.1.b_ref
  51.2 16.5 %near_do.1.old_ref = bf16[4096,1536]{1,0:T(8,128)(2,1)} custom-call(s32[3]{0:T(128)} %pad_add_fusion.tbl_ref, bf16[512,3072]{1,0:T(8,128)(2,1)} %bitcast.40, bf16[512,3072]{1,0:T(8,128)(2,1)} %collective-permute-done.1.b_ref, bf16[3072,3072]{1,0:T(8,128)(2,1)} %bitcast.34), custom_call_target="tpu_custom_call" | custom-call | flops 9663676416 | bytes 9437184 | tf_op jit(solution)/shard_map/near_do/pallas_call | solution.py:79
  67.6 0.0 collective-permute-done.b_ref
  67.6 23.7 %near_qkv.1.old_ref = bf16[4096,2560]{1,0:T(8,128)(2,1)} custom-call(s32[3]{0:T(128)} %pad_add_fusion.tbl_ref, bf16[512,3072]{1,0:T(8,128)(2,1)} %bitcast.48, bf16[512,3072]{1,0:T(8,128)(2,1)} %collective-permute-done.b_ref, bf16[3072,2560]{1,0:T(8,128)(2,1)} %get-tuple-element.41.w_ref), custom_call_target="tpu_custom_call" | custom-call | flops 16106127360 | bytes 15728640 | tf_op jit(solution)/shard_map/near_qkv/pallas_call | solution.py:79
  91.4 48.5 %all-gather.6.cloned.1.call-done.a_ref = bf16[4096,3072]{1,0:T(8,128)(2,1)} async-done(((bf16[512,3072]{1,0:T(8,128)(2,1)}), bf16[4096,3072]{1,0:T(8,128)(2,1)}) %all-gather.6.cloned.1.call-update) | async-done | bytes 25165840 | tf_op jit(solution)/shard_map/all_gather | solution.py:490
  139.9 57.3 %far_qkv.1 = bf16[4096,2560]{1,0:T(8,128)(2,1)} custom-call(s32[7]{0:T(128)} %stack.46.tbl_ref, bf16[4096,3072]{1,0:T(8,128)(2,1)} %all-gather.6.cloned.1.call-done.a_ref, bf16[3072,2560]{1,0:T(8,128)(2,1)} %get-tuple-element.41.w_ref, bf16[4096,2560]{1,0:T(8,128)(2,1)} %near_qkv.1.old_ref), custom_call_target="tpu_custom_call", output_to_operand_aliasing={{}: (3, {})} | custom-call | flops 48318382080 | bytes 25165824 | tf_op jit(solution)/shard_map/far_qkv/pallas_call | solution.py:93
  197.2 49.0 %attn_fwd.1 = (bf16[8,4,128,1536]{3,2,1,0:T(8,128)(2,1)}, f32[4,12,1,1024]{3,2,1,0:T(1,128)}) custom-call(bf16[8,4,128,2560]{3,2,1,0:T(8,128)(2,1)} %bitcast.24, bf16[8,4,128,2560]{3,2,1,0:T(8,128)(2,1)} %bitcast.25, bf16[8,4,128,2560]{3,2,1,0:T(8,128)(2,1)} %bitcast.26), custom_call_target="tpu_custom_call" | custom-call | flops 25769803776 | bytes 10000000 | tf_op jit(solution)/shard_map/attn_fwd/pallas_call | solution.py:153
  246.3 1.5 dynamic-slice_bitcast_fusion
  247.8 0.3 collective-permute-start.2
  248.1 0.6 pad_add_fusion.1.idx_ref
  248.6 2.6 collective-permute-done.2.rem_ref
  251.2 0.0 copy-start.1
  251.2 1.1 copy-done.1
  252.4 16.5 %out_proj.1 = bf16[4,128,3072]{2,1,0:T(8,128)(2,1)} custom-call(s32[2]{0:T(128)} %pad_add_fusion.1.idx_ref, bf16[8,4,128,1536]{3,2,1,0:T(8,128)(2,1)} %get-tuple-element.46.loc_ref.o_ref, bf16[4,128,1536]{2,1,0:T(8,128)(2,1)} %copy-done.1, bf16[3072,3072]{1,0:T(8,128)(2,1)} %bitcast.35, bf16[4,128,3072]{2,1,0:T(8,128)(2,1)} %refs_5_), custom_call_target="tpu_custom_call" | custom-call | flops 9663676416 | bytes 18874368 | tf_op jit(solution)/shard_map/out_proj/pallas_call | solution.py:375
  268.9 0.0 all-gather.4.cloned.1.call-done.a_ref.b_ref
  268.9 16.3 %grad_wo.1 = f32[384,3072]{1,0:T(8,128)} custom-call(s32[1]{0:T(128)} %bitcast.19.chip_ref, bf16[4096,1536]{1,0:T(8,128)(2,1)} %bitcast.33, bf16[4096,3072]{1,0:T(8,128)(2,1)} %all-gather.4.cloned.1.call-done.a_ref.b_ref), custom_call_target="tpu_custom_call" | custom-call | flops 9663676416 | bytes 25165824 | tf_op jit(solution)/shard_map/grad_wo/pallas_call | solution.py:245
  285.2 0.0 all-gather.8.cloned.1.call-update
  285.2 37.8 %far_do.1 = bf16[4096,1536]{1,0:T(8,128)(2,1)} custom-call(s32[7]{0:T(128)} %stack.46.tbl_ref, bf16[4096,3072]{1,0:T(8,128)(2,1)} %all-gather.4.cloned.1.call-done.a_ref.b_ref, bf16[3072,3072]{1,0:T(8,128)(2,1)} %bitcast.36, bf16[4096,1536]{1,0:T(8,128)(2,1)} %near_do.1.old_ref), custom_call_target="tpu_custom_call", output_to_operand_aliasing={{}: (3, {})} | custom-call | flops 28991029248 | bytes 25165824 | tf_op jit(solution)/shard_map/far_do/pallas_call | solution.py:93
  323.0 72.1 %attn_bwd.2.refs_0_ = bf16[8,4,128,1920]{3,2,1,0:T(8,128)(2,1)} custom-call(bf16[8,4,128,2560]{3,2,1,0:T(8,128)(2,1)} %bitcast.27, bf16[8,4,128,2560]{3,2,1,0:T(8,128)(2,1)} %bitcast.28, bf16[8,4,128,2560]{3,2,1,0:T(8,128)(2,1)} %bitcast.29, bf16[8,4,128,1536]{3,2,1,0:T(8,128)(2,1)} %get-tuple-element.46.loc_ref.o_ref, bf16[8,4,128,1536]{3,2,1,0:T(8,128)(2,1)} %bitcast.37, ...), custom_call_target="tpu_custom_call" | custom-call | flops 48318382080 | bytes 10000000 | tf_op jit(solution)/shard_map/attn_bwd/pallas_call | solution.py:223
  395.2 0.2 collective-permute-start.3
  395.4 26.2 %attn_bwd.3.refs_2_ = bf16[8,4,128,640]{3,2,1,0:T(8,128)(2,1)} custom-call(bf16[8,4,128,2560]{3,2,1,0:T(8,128)(2,1)} %bitcast.30, bf16[8,4,128,2560]{3,2,1,0:T(8,128)(2,1)} %bitcast.31, bf16[8,4,128,2560]{3,2,1,0:T(8,128)(2,1)} %bitcast.32, bf16[8,4,128,1536]{3,2,1,0:T(8,128)(2,1)} %get-tuple-element.46.loc_ref.o_ref, bf16[8,4,128,1536]{3,2,1,0:T(8,128)(2,1)} %bitcast.38, ...), custom_call_target="tpu_custom_call" | custom-call | flops 16106127360 | bytes 10000000 | tf_op jit(solution)/shard_map/attn_bwd/pallas_call | solution.py:223
  421.5 0.3 collective-permute-start.4
  421.8 8.3 %collective-permute-done.4.refs_3_ = bf16[8,4,128,640]{3,2,1,0:T(8,128)(2,1)} collective-permute-done((bf16[8,4,128,640]{3,2,1,0:T(8,128)(2,1)}, bf16[8,4,128,640]{3,2,1,0:T(8,128)(2,1)}, u32[]{:S(2)}, u32[]{:S(2)}) %collective-permute-start.4) | collective-permute-done | bytes 5242912 | tf_op jit(solution)/shard_map/ppermute | solution.py:482
  430.1 0.0 collective-permute-done.3.refs_1_
  430.1 53.4 %grad_wq.1 = (f32[3072,24,128]{2,1,0:T(8,128)}, f32[1536,24,128]{2,1,0:T(8,128)}) custom-call(s32[1]{0:T(128)} %bitcast.7.core_ref, bf16[4096,3072]{1,0:T(8,128)(2,1)} %all-gather.6.cloned.1.call-done.a_ref, bf16[4096,1920]{1,0:T(8,128)(2,1)} %bitcast.44, bf16[4096,1920]{1,0:T(8,128)(2,1)} %bitcast.16.refs_1_, bf16[4096,640]{1,0:T(8,128)(2,1)} %bitcast.42, ...), custom_call_target="tpu_custom_call" | custom-call | flops 38654705664 | bytes 25165824 | tf_op jit(solution)/shard_map/grad_wq/pallas_call | solution.py:311
  483.5 0.0 copy-start.2
  483.5 0.4 collective-permute-start.5
  483.9 44.0 %grad_wkv.1 = (f32[3072,8,128]{2,1,0:T(8,128)}, f32[3072,8,128]{2,1,0:T(8,128)}, f32[1536,8,128]{2,1,0:T(8,128)}, f32[1536,8,128]{2,1,0:T(8,128)}) custom-call(s32[1]{0:T(128)} %bitcast.7.core_ref, bf16[4096,3072]{1,0:T(8,128)(2,1)} %all-gather.6.cloned.1.call-done.a_ref, bf16[4096,1920]{1,0:T(8,128)(2,1)} %bitcast.45, bf16[4096,1920]{1,0:T(8,128)(2,1)} %bitcast.16.refs_1_, ...), custom_call_target="tpu_custom_call" | custom-call | flops 25769803776 | bytes 25165824 | tf_op jit(solution)/shard_map/grad_wkv/pallas_call | solution.py:311
  527.9 0.2 collective-permute-start.6
  528.1 0.3 collective-permute-start.7
  528.5 0.0 copy-done.2
  528.5 0.6 broadcast_in_dim.4.refs_7_
  529.1 0.0 all-gather.8.cloned.1.call-done.refs_8_
  529.1 50.9 %grad_x.1 = (bf16[4,128,3072]{2,1,0:T(8,128)(2,1)}, f32[1,3072]{1,0:T(1,128)}, f32[3072,3072]{1,0:T(8,128)}) custom-call(s32[2]{0:T(128)} %pad_add_fusion.1.idx_ref, bf16[8,4,128,1920]{3,2,1,0:T(8,128)(2,1)} %attn_bwd.2.refs_0_, bf16[8,4,128,1920]{3,2,1,0:T(8,128)(2,1)} %collective-permute-done.3.refs_1_, bf16[8,4,128,640]{3,2,1,0:T(8,128)(2,1)} %attn_bwd.3.refs_2_, ...), custom_call_target="tpu_custom_call" | custom-call | flops 16106127360 | bytes 31457280 | tf_op jit(solution)/shard_map/grad_x/pallas_call | solution.py:448
  580.0 0.2 collective-permute-start.8
  580.1 1.0 collective-permute-done.8
  581.1 0.7 add.68
  581.8 1.6 collective-permute-start.9
  583.4 0.0 collective-permute-done.6.refs_4_
  583.4 0.0 collective-permute-done.7.refs_5_
  583.4 0.0 collective-permute-done.5.refs_3_
  583.5 2.1 collective-permute-done.9
  585.5 0.5 collective-permute-start.10
  586.0 23.8 %merge.1 = (f32[3072,24,128]{2,1,0:T(8,128)}, f32[3072,8,128]{2,1,0:T(8,128)}, f32[3072,8,128]{2,1,0:T(8,128)}) custom-call(s32[1]{0:T(128)} %bitcast.7.core_ref, f32[3072,24,128]{2,1,0:T(8,128)} %get-tuple-element.65.refs_0_, f32[3072,8,128]{2,1,0:T(8,128)} %get-tuple-element.66.refs_1_, ...), custom_call_target="tpu_custom_call", output_to_operand_aliasing={{0}: (1, {}), {1}: (2, {}), {2}: (3, {})} | custom-call | flops 10000000000 | bytes 100000000 | tf_op jit(solution)/shard_map/merge/pallas_call | solution.py:342
  609.8 0.0 collective-permute-done.10
  609.8 0.6 add.70
  (2 shorter events, 0.0 us)
Async XLA Ops:
  7.2 132.7 %all-gather.6.cloned.1.call-start = ((), (), s32[]{:S(2)}) async-start(), calls=%async_computation.1 | async-start | bytes 28311552 | tf_op jit(solution)/shard_map/all_gather | solution.py:490
  10.5 5.7 copy-start
  15.4 253.5 %all-gather.4.cloned.1.call-start = ((), (), s32[]{:S(2)}) async-start(), calls=%async_computation | async-start | bytes 28311552 | tf_op jit(solution)/shard_map/all_gather | solution.py:491
  16.2 512.9 %all-gather.8.cloned.1.call-start = ((), (), s32[]{:S(2)}) async-start(), calls=%async_computation.2 | async-start | bytes 42467328 | tf_op jit(solution)/shard_map/all_gather | solution.py:506
  16.2 34.9 %collective-permute-start.1 = (bf16[512,3072]{1,0:T(8,128)(2,1)S(1)}, bf16[512,3072]{1,0:T(8,128)(2,1)}, u32[]{:S(2)}, u32[]{:S(2)}) collective-permute-start(bf16[512,3072]{1,0:T(8,128)(2,1)S(1)} %bitcast.41), channel_id=1, source_target_pairs={{0,1},{1,0},{2,3},{3,2},{4,5},{5,4},{6,7},{7,6},{8,9},{9,8},{10,11... | collective-permute-start | bytes 9437192 | tf_op jit(solution)/shard_map/ppermute | solution.py:482
  17.0 50.6 %collective-permute-start = (bf16[512,3072]{1,0:T(8,128)(2,1)}, bf16[512,3072]{1,0:T(8,128)(2,1)}, u32[]{:S(2)}, u32[]{:S(2)}) collective-permute-start(bf16[512,3072]{1,0:T(8,128)(2,1)} %bitcast.47), channel_id=1, source_target_pairs={{0,1},{1,0},{2,3},{3,2},{4,5},{5,4},{6,7},{7,6},{8,9},{9,8},{10,11... | collective-permute-start | bytes 9437192 | tf_op jit(solution)/shard_map/ppermute | solution.py:482
  247.8 3.4 collective-permute-start.2
  251.2 1.1 copy-start.1
  395.2 35.0 %collective-permute-start.3 = (bf16[8,4,128,1920]{3,2,1,0:T(8,128)(2,1)}, bf16[8,4,128,1920]{3,2,1,0:T(8,128)(2,1)}, u32[]{:S(2)}, u32[]{:S(2)}) collective-permute-start(bf16[8,4,128,1920]{3,2,1,0:T(8,128)(2,1)} %attn_bwd.2.refs_0_), channel_id=1, source_target_pairs={{0,1},{1,0},{2,3},{3,2},{4,5},{5,4},{6,7},{7,6},{8,9},{9,8},{10,11... | collective-permute-start | bytes 47185928 | tf_op jit(solution)/shard_map/ppermute | solution.py:482
  421.5 8.6 %collective-permute-start.4 = (bf16[8,4,128,640]{3,2,1,0:T(8,128)(2,1)}, bf16[8,4,128,640]{3,2,1,0:T(8,128)(2,1)}, u32[]{:S(2)}, u32[]{:S(2)}) collective-permute-start(bf16[8,4,128,640]{3,2,1,0:T(8,128)(2,1)} %attn_bwd.3.refs_2_), channel_id=1, source_target_pairs={{0,1},{1,0},{2,3},{3,2},{4,5},{5,4},{6,7},{7,6},{8,9},{9,8},{10,11... | collective-permute-start | bytes 15728648 | tf_op jit(solution)/shard_map/ppermute | solution.py:482
  483.5 45.0 %copy-start.2 = (bf16[3072]{0:T(1024)(128)(2,1)S(1)}, bf16[3072]{0:T(1024)(128)(2,1)}, u32[]{:S(2)}) copy-start(bf16[3072]{0:T(1024)(128)(2,1)} %param.9) | copy-start | bytes 18436
  483.5 99.9 %collective-permute-start.5 = (f32[1536,24,128]{2,1,0:T(8,128)}, f32[1536,24,128]{2,1,0:T(8,128)}, u32[]{:S(2)}, u32[]{:S(2)}) collective-permute-start(f32[1536,24,128]{2,1,0:T(8,128)} %get-tuple-element.54), channel_id=1, source_target_pairs={{0,1},{1,0},{2,3},{3,2},{4,5},{5,4},{6,7},{7,6},{8,9},{9,8},{10,11... | collective-permute-start | bytes 56623112 | tf_op jit(solution)/shard_map/ppermute | solution.py:482
  527.9 55.5 %collective-permute-start.6 = (f32[1536,8,128]{2,1,0:T(8,128)}, f32[1536,8,128]{2,1,0:T(8,128)}, u32[]{:S(2)}, u32[]{:S(2)}) collective-permute-start(f32[1536,8,128]{2,1,0:T(8,128)} %get-tuple-element.58), channel_id=1, source_target_pairs={{0,1},{1,0},{2,3},{3,2},{4,5},{5,4},{6,7},{7,6},{8,9},{9,8},{10,11... | collective-permute-start | bytes 18874376 | tf_op jit(solution)/shard_map/ppermute | solution.py:482
  528.1 55.3 %collective-permute-start.7 = (f32[1536,8,128]{2,1,0:T(8,128)}, f32[1536,8,128]{2,1,0:T(8,128)}, u32[]{:S(2)}, u32[]{:S(2)}) collective-permute-start(f32[1536,8,128]{2,1,0:T(8,128)} %get-tuple-element.59), channel_id=1, source_target_pairs={{0,1},{1,0},{2,3},{3,2},{4,5},{5,4},{6,7},{7,6},{8,9},{9,8},{10,11... | collective-permute-start | bytes 18874376 | tf_op jit(solution)/shard_map/ppermute | solution.py:482
  580.0 1.2 collective-permute-start.8
  581.8 3.7 collective-permute-start.9
  585.5 24.3 %collective-permute-start.10 = (f32[3072]{0:T(1024)S(1)}, f32[3072]{0:T(1024)S(1)}, u32[]{:S(2)}, u32[]{:S(2)}) collective-permute-start(f32[3072]{0:T(1024)S(1)} %add.69), channel_id=1, source_target_pairs={{0,4},{1,5},{2,6},{3,7},{4,0},{5,1},{6,2},{7,3},{8,12},{9,13},{10,... | collective-permute-start | bytes 36872 | tf_op jit(solution)/shard_map/ppermute | solution.py:538
Sparse Core Ops, SparseCore 0:
  15.5 124.2 all-gather.5
  141.7 121.4 all-gather.3
  285.3 175.8 all-gather.7

commit v5 on v4

--- a/solution.py
+++ b/solution.py
@@ -271,16 +271,21 @@
                         pltpu.make_async_copy(src.at[:, pl.ds(lo, w)], buf.at[slot, :, pl.ds(off, w)], sem.at[slot]).start()
                 off += hi - lo
 
+    keep = len(plan) == 2
+    slot = lax.rem(step, 2)
+
     @pl.when(step == 0)
     def _():
         fetch(n, 0)
 
-    @pl.when(step + 1 < pl.num_programs(0) * nn)
+    @pl.when(step + 1 < (nn if keep else pl.num_programs(0) * nn))
     def _():
         fetch(lax.rem(n + 1, nn), lax.rem(step + 1, 2))
 
-    slot = lax.rem(step, 2)
-    pltpu.make_async_copy(buf.at[slot], buf.at[slot], sem.at[slot]).wait()
+    @pl.when(step < (nn if keep else pl.num_programs(0) * nn))
+    def _():
+        pltpu.make_async_copy(buf.at[slot], buf.at[slot], sem.at[slot]).wait()
+
     acc = dot(a_ref[...], buf[slot], 0, 0)
     rows = acc.shape[0]
 
@@ -323,12 +328,12 @@
 
 
 def merge_kernel(core_ref, *refs):
-    n = len(refs) // 3
-    for i in range(n):
-        refs[2 * n + i][...] = refs[n + i][...]
-
-
-def merge(fulls, recvs, core):
+    n = (len(refs) - 2) // 3
+    for i in range(n + 1):
+        refs[2 * n + 1 + i][...] = refs[n + i][...]
+
+
+def merge(fulls, recvs, gathered, core):
     steps = 12
     n = len(fulls)
 
@@ -343,11 +348,11 @@
         merge_kernel,
         grid_spec=pltpu.PrefetchScalarGridSpec(
             num_scalar_prefetch=1, grid=(steps,),
-            in_specs=[pl.BlockSpec(memory_space=pl.ANY)] * n + [spec(r, True) for r in recvs],
-            out_specs=[spec(r, False) for r in recvs]),
-        out_shape=[jax.ShapeDtypeStruct(f.shape, f.dtype) for f in fulls],
+            in_specs=[pl.BlockSpec(memory_space=pl.ANY)] * n + [spec(r, True) for r in recvs] + [spec(gathered, True)],
+            out_specs=[spec(r, False) for r in recvs] + [spec(gathered, True)]),
+        out_shape=[jax.ShapeDtypeStruct(f.shape, f.dtype) for f in fulls] + [jax.ShapeDtypeStruct(gathered.shape, gathered.dtype)],
         input_output_aliases={1 + i: i for i in range(n)},
-        cost_estimate=cost(1e10, 10 ** 8), name='merge')(core, *fulls, *recvs)
+        compiler_params=BIG, cost_estimate=cost(1e10, 10 ** 8), name='merge')(core, *fulls, *recvs, gathered)
 
 
 def y_kernel(idx_ref, loc_ref, rem_ref, w_ref, x_ref, y_ref, lhs):
@@ -386,7 +391,7 @@
 
 def dx_kernel(spans, n_src, idx_ref, *refs):
     srcs = refs[:2 * n_src]
-    w_ref, x_ref, dy_ref, g_ref, from_ref, dx_ref, dg_ref, to_ref, lhs, acc = refs[2 * n_src:]
+    w_ref, x_ref, dy_ref, g_ref, dx_ref, dg_ref, lhs, acc = refs[2 * n_src:]
     n = pl.program_id(0)
     wide = w_ref.shape[0]
     steps = acc.shape[1] // wide
@@ -404,7 +409,6 @@
     @pl.when(n < steps)
     def _():
         acc[:, pl.ds(pl.multiple_of(n * wide, wide), wide)] = dot(lhs[...], w_ref[...], 1, 1)
-        to_ref[...] = from_ref[...]
 
     @pl.when(n >= steps)
     def _():
@@ -435,28 +439,25 @@
     return plan
 
 
-def grad_x(idx, srcs, spans, wcat, x, dy, gain, gathered):
+def grad_x(idx, srcs, spans, wcat, x, dy, gain):
     nb, s, dm = x.shape
     cols = wcat.shape[1]
-    wide = 256
+    wide = 512
     steps = dm // wide
-    rows = gathered.shape[0] // steps
     flat = [a for pair in srcs for a in pair]
     seq = pl.BlockSpec((1, s, dm), lambda k, i: (jnp.maximum(k - steps, 0), 0, 0))
     line = pl.BlockSpec((1, dm), lambda k, i: (0, 0))
-    share = pl.BlockSpec((rows, gathered.shape[1]), lambda k, i: (jnp.minimum(k, steps - 1), 0))
     return pl.pallas_call(
         functools.partial(dx_kernel, spans, len(srcs)),
         grid_spec=pltpu.PrefetchScalarGridSpec(
             num_scalar_prefetch=1, grid=(steps + nb,),
             in_specs=[pl.BlockSpec((1, nb, s, a.shape[3]), lambda k, i: (i[1], 0, 0, 0)) for a in flat]
-            + [pl.BlockSpec((wide, cols), lambda k, i: (jnp.minimum(k, steps - 1), 0)), seq, seq, line, share],
-            out_specs=[seq, line, share],
+            + [pl.BlockSpec((wide, cols), lambda k, i: (jnp.minimum(k, steps - 1), 0)), seq, seq, line],
+            out_specs=[seq, line],
             scratch_shapes=[pltpu.VMEM((nb * s, cols), jnp.bfloat16), pltpu.VMEM((nb * s, dm), jnp.float32)]),
-        out_shape=[jax.ShapeDtypeStruct(x.shape, jnp.bfloat16), jax.ShapeDtypeStruct((1, dm), jnp.float32),
-                   jax.ShapeDtypeStruct(gathered.shape, gathered.dtype)],
+        out_shape=[jax.ShapeDtypeStruct(x.shape, jnp.bfloat16), jax.ShapeDtypeStruct((1, dm), jnp.float32)],
         compiler_params=BIG, cost_estimate=cost(2 * nb * s * dm * cols, 2 * dm * cols),
-        name='grad_x')(idx, *flat, wcat, x, dy, gain, gathered)
+        name='grad_x')(idx, *flat, wcat, x, dy, gain)
 
 
 def solution(mesh):
@@ -531,15 +532,15 @@
             xg, flat, cut(by_k + by_v, wide), (kv_heads, kv_heads), core_arr, 'grad_wkv')
         wk_send, wv_send, x_late = lax.optimization_barrier((wk_send, wv_send, x_in))
         wk_recv, wv_recv = swap(wk_send), swap(wv_send)
-        dx_out, d_gain, d_wo = grad_x(idx, pairs, by_q + by_k + by_v, wcat, x_late, dy_in, norm_gain[None], d_wo)
+        dx_out, d_gain = grad_x(idx, pairs, by_q + by_k + by_v, wcat, x_late, dy_in, norm_gain[None])
         d_gain = d_gain[0]
 
         def add_from(bit, a):
             return a + lax.ppermute(a, 'cp', [(d, d ^ bit) for d in range(n_dev)])
 
         d_gain = add_from(2, add_from(1, d_gain))
-        wq_recv, wk_recv, wv_recv, dx_out = lax.optimization_barrier((wq_recv, wk_recv, wv_recv, dx_out))
-        d_wq, d_wk, d_wv = merge((wq_full, wk_full, wv_full), (wq_recv, wk_recv, wv_recv), core_arr)
+        wq_recv, wk_recv, wv_recv, d_wo, dx_out = lax.optimization_barrier((wq_recv, wk_recv, wv_recv, d_wo, dx_out))
+        d_wq, d_wk, d_wv, d_wo = merge((wq_full, wk_full, wv_full), (wq_recv, wk_recv, wv_recv), d_wo, core_arr)
         d_gain = add_from(4, d_gain)
         d_wo = d_wo.reshape(n_heads, HD, dm)
         return y_out, dx_out, d_gain, d_wq, d_wk, d_wv, d_wo

time: 620 us -> 624 us (level)
    pallas_call x1, Pallas kernels: 23.8 us -> 44.1 us  [merge(): pl.pallas_call(merge_kernel, grid_spec=pltpu.PrefetchScalarGridSpec(num_s...]
    pallas_call x1, Pallas kernels: 50.9 us -> 30.7 us  [grad_x(): pl.pallas_call(functools.partial(dx_kernel, spans, len(srcs)), grid_spec=...]
  transfers between devices with their start and end apart: 14 -> 14, of which waited for: 5 -> 6; matrix products, arithmetic and copies ran while one was open for 1% -> 1% of each run, Pallas kernels for 82% -> 74%
where the time goes in v5:
time: 624 us; the launch traced here: 620 us
  Pallas kernels  520 us (83%)
  waiting for transfers between devices  66.6 us (11%)
  between operations  14 us (2%)
  other arithmetic  10.7 us (2%)
    pallas_call x2, Pallas kernels, attn_bwd(): pl.pallas_call(functools.partial(bwd_kernel, 256), grid=(nb, count), in_s...  98.2 us
    pallas_call x2, Pallas kernels, grad_wx(): pl.pallas_call(functools.partial(grad_wx_kernel, plan, len(srcs), len(hea...  97.3 us
    pallas_call x2, Pallas kernels, proj_far(): pl.pallas_call(functools.partial(far_kernel, cb), grid_spec=pltpu.Prefetc...  95.2 us
    pallas_call x1, Pallas kernels, attn_fwd(): pl.pallas_call(functools.partial(fwd_kernel, 128), grid=(nb, kvh), in_spe...  49 us
    all_gather x1, waiting for transfers between devices, device_fn(): xg = lax.all_gather(xn, 'cp', tiled=True)  48.5 us
    pallas_call x1, Pallas kernels, merge(): pl.pallas_call(merge_kernel, grid_spec=pltpu.PrefetchScalarGridSpec(num_s...  44.1 us
    pallas_call x2, Pallas kernels, proj_near(): pl.pallas_call(functools.partial(near_kernel, cb), grid_spec=pltpu.Prefet...  40.2 us
    pallas_call x1, Pallas kernels, relayout(): pl.pallas_call(relayout_kernel, grid_spec=pltpu.PrefetchScalarGridSpec(nu...  32.9 us
  transfers between devices with their start and end apart: 14, of which 6 were waited for; matrix products, arithmetic and copies ran while one was open for 1% of the time, Pallas kernels for 74%

profile of v5, /device:TPU:0, one launch (start us, length us, event | category | flops | bytes accessed | tf_op | source)
XLA Modules:
  0.0 620.4 jit_solution(3605056424213074189)
XLA Ops:
  7.2 0.0 all-gather.6.cloned.1.call-start
  7.2 2.6 fusion
  9.8 0.7 convert_element_type.10
  10.5 0.0 copy-start
  10.5 4.9 fusion.2
  15.4 0.0 all-gather.6.cloned.1.call-update
  15.4 0.0 all-gather.4.cloned.1.call-start
  15.5 0.7 all-gather.4.cloned.1.call-update
  16.2 0.0 all-gather.8.cloned.1.call-start
  16.2 0.0 copy-done
  16.2 0.8 collective-permute-start.1
  17.0 0.1 collective-permute-start
  17.1 0.6 stack.46.tbl_ref
  17.7 0.6 pad_add_fusion.tbl_ref
  18.3 32.9 %relayout.1 = (bf16[3072,5120]{1,0:T(8,128)(2,1)}, bf16[3072,2560]{1,0:T(8,128)(2,1)}) custom-call(s32[1]{0:T(128)} %bitcast.7.core_ref, bf16[3072,24,128]{2,1,0:T(8,128)(2,1)} %wq_ref.1, bf16[3072,8,128]{2,1,0:T(8,128)(2,1)} %wk_ref.1, bf16[3072,8,128]{2,1,0:T(8,128)(2,1)} %wv_ref.1), custom_call_target="tpu_custom_call" | custom-call | flops 10000000000 | bytes 62914560 | tf_op jit(solution)/shard_map/relayout/pallas_call | solution.py:47
  51.2 0.0 collective-permute-done.1.b_ref
  51.2 16.4 %near_do.1.old_ref = bf16[4096,1536]{1,0:T(8,128)(2,1)} custom-call(s32[3]{0:T(128)} %pad_add_fusion.tbl_ref, bf16[512,3072]{1,0:T(8,128)(2,1)} %bitcast.40, bf16[512,3072]{1,0:T(8,128)(2,1)} %collective-permute-done.1.b_ref, bf16[3072,3072]{1,0:T(8,128)(2,1)} %bitcast.34), custom_call_target="tpu_custom_call" | custom-call | flops 9663676416 | bytes 9437184 | tf_op jit(solution)/shard_map/near_do/pallas_call | solution.py:79
  67.7 0.0 collective-permute-done.b_ref
  67.7 23.7 %near_qkv.1.old_ref = bf16[4096,2560]{1,0:T(8,128)(2,1)} custom-call(s32[3]{0:T(128)} %pad_add_fusion.tbl_ref, bf16[512,3072]{1,0:T(8,128)(2,1)} %bitcast.48, bf16[512,3072]{1,0:T(8,128)(2,1)} %collective-permute-done.b_ref, bf16[3072,2560]{1,0:T(8,128)(2,1)} %get-tuple-element.42.w_ref), custom_call_target="tpu_custom_call" | custom-call | flops 16106127360 | bytes 15728640 | tf_op jit(solution)/shard_map/near_qkv/pallas_call | solution.py:79
  91.4 48.5 %all-gather.6.cloned.1.call-done.a_ref = bf16[4096,3072]{1,0:T(8,128)(2,1)} async-done(((bf16[512,3072]{1,0:T(8,128)(2,1)}), bf16[4096,3072]{1,0:T(8,128)(2,1)}) %all-gather.6.cloned.1.call-update) | async-done | bytes 25165840 | tf_op jit(solution)/shard_map/all_gather | solution.py:491
  139.9 57.3 %far_qkv.1 = bf16[4096,2560]{1,0:T(8,128)(2,1)} custom-call(s32[7]{0:T(128)} %stack.46.tbl_ref, bf16[4096,3072]{1,0:T(8,128)(2,1)} %all-gather.6.cloned.1.call-done.a_ref, bf16[3072,2560]{1,0:T(8,128)(2,1)} %get-tuple-element.42.w_ref, bf16[4096,2560]{1,0:T(8,128)(2,1)} %near_qkv.1.old_ref), custom_call_target="tpu_custom_call", output_to_operand_aliasing={{}: (3, {})} | custom-call | flops 48318382080 | bytes 25165824 | tf_op jit(solution)/shard_map/far_qkv/pallas_call | solution.py:93
  197.2 49.0 %attn_fwd.1 = (bf16[8,4,128,1536]{3,2,1,0:T(8,128)(2,1)}, f32[4,12,1,1024]{3,2,1,0:T(1,128)}) custom-call(bf16[8,4,128,2560]{3,2,1,0:T(8,128)(2,1)} %bitcast.24, bf16[8,4,128,2560]{3,2,1,0:T(8,128)(2,1)} %bitcast.25, bf16[8,4,128,2560]{3,2,1,0:T(8,128)(2,1)} %bitcast.26), custom_call_target="tpu_custom_call" | custom-call | flops 25769803776 | bytes 10000000 | tf_op jit(solution)/shard_map/attn_fwd/pallas_call | solution.py:153
  246.3 1.5 dynamic-slice_bitcast_fusion
  247.8 0.3 collective-permute-start.2
  248.1 0.6 pad_add_fusion.1.idx_ref
  248.7 2.5 collective-permute-done.2.rem_ref
  251.2 0.0 copy-start.1
  251.2 1.1 copy-done.1
  252.4 16.5 %out_proj.1 = bf16[4,128,3072]{2,1,0:T(8,128)(2,1)} custom-call(s32[2]{0:T(128)} %pad_add_fusion.1.idx_ref, bf16[8,4,128,1536]{3,2,1,0:T(8,128)(2,1)} %get-tuple-element.47.loc_ref.o_ref, bf16[4,128,1536]{2,1,0:T(8,128)(2,1)} %copy-done.1, bf16[3072,3072]{1,0:T(8,128)(2,1)} %bitcast.35, bf16[4,128,3072]{2,1,0:T(8,128)(2,1)} %refs_5_), custom_call_target="tpu_custom_call" | custom-call | flops 9663676416 | bytes 18874368 | tf_op jit(solution)/shard_map/out_proj/pallas_call | solution.py:380
  268.9 0.0 all-gather.4.cloned.1.call-done.a_ref.b_ref
  268.9 16.4 %grad_wo.1 = f32[384,3072]{1,0:T(8,128)} custom-call(s32[1]{0:T(128)} %bitcast.19.chip_ref, bf16[4096,1536]{1,0:T(8,128)(2,1)} %bitcast.33, bf16[4096,3072]{1,0:T(8,128)(2,1)} %all-gather.4.cloned.1.call-done.a_ref.b_ref), custom_call_target="tpu_custom_call" | custom-call | flops 9663676416 | bytes 25165824 | tf_op jit(solution)/shard_map/grad_wo/pallas_call | solution.py:245
  285.2 0.0 all-gather.8.cloned.1.call-update
  285.3 37.8 %far_do.1 = bf16[4096,1536]{1,0:T(8,128)(2,1)} custom-call(s32[7]{0:T(128)} %stack.46.tbl_ref, bf16[4096,3072]{1,0:T(8,128)(2,1)} %all-gather.4.cloned.1.call-done.a_ref.b_ref, bf16[3072,3072]{1,0:T(8,128)(2,1)} %bitcast.36, bf16[4096,1536]{1,0:T(8,128)(2,1)} %near_do.1.old_ref), custom_call_target="tpu_custom_call", output_to_operand_aliasing={{}: (3, {})} | custom-call | flops 28991029248 | bytes 25165824 | tf_op jit(solution)/shard_map/far_do/pallas_call | solution.py:93
  323.1 72.1 %attn_bwd.2.refs_0_ = bf16[8,4,128,1920]{3,2,1,0:T(8,128)(2,1)} custom-call(bf16[8,4,128,2560]{3,2,1,0:T(8,128)(2,1)} %bitcast.27, bf16[8,4,128,2560]{3,2,1,0:T(8,128)(2,1)} %bitcast.28, bf16[8,4,128,2560]{3,2,1,0:T(8,128)(2,1)} %bitcast.29, bf16[8,4,128,1536]{3,2,1,0:T(8,128)(2,1)} %get-tuple-element.47.loc_ref.o_ref, bf16[8,4,128,1536]{3,2,1,0:T(8,128)(2,1)} %bitcast.37, ...), custom_call_target="tpu_custom_call" | custom-call | flops 48318382080 | bytes 10000000 | tf_op jit(solution)/shard_map/attn_bwd/pallas_call | solution.py:223
  395.1 0.2 collective-permute-start.3
  395.4 26.2 %attn_bwd.3.refs_2_ = bf16[8,4,128,640]{3,2,1,0:T(8,128)(2,1)} custom-call(bf16[8,4,128,2560]{3,2,1,0:T(8,128)(2,1)} %bitcast.30, bf16[8,4,128,2560]{3,2,1,0:T(8,128)(2,1)} %bitcast.31, bf16[8,4,128,2560]{3,2,1,0:T(8,128)(2,1)} %bitcast.32, bf16[8,4,128,1536]{3,2,1,0:T(8,128)(2,1)} %get-tuple-element.47.loc_ref.o_ref, bf16[8,4,128,1536]{3,2,1,0:T(8,128)(2,1)} %bitcast.38, ...), custom_call_target="tpu_custom_call" | custom-call | flops 16106127360 | bytes 10000000 | tf_op jit(solution)/shard_map/attn_bwd/pallas_call | solution.py:223
  421.6 0.3 collective-permute-start.4
  421.8 8.3 %collective-permute-done.4.refs_3_ = bf16[8,4,128,640]{3,2,1,0:T(8,128)(2,1)} collective-permute-done((bf16[8,4,128,640]{3,2,1,0:T(8,128)(2,1)}, bf16[8,4,128,640]{3,2,1,0:T(8,128)(2,1)}, u32[]{:S(2)}, u32[]{:S(2)}) %collective-permute-start.4) | collective-permute-done | bytes 5242912 | tf_op jit(solution)/shard_map/ppermute | solution.py:483
  430.2 0.0 collective-permute-done.3.refs_1_
  430.2 53.4 %grad_wq.1 = (f32[3072,24,128]{2,1,0:T(8,128)}, f32[1536,24,128]{2,1,0:T(8,128)}) custom-call(s32[1]{0:T(128)} %bitcast.7.core_ref, bf16[4096,3072]{1,0:T(8,128)(2,1)} %all-gather.6.cloned.1.call-done.a_ref, bf16[4096,1920]{1,0:T(8,128)(2,1)} %bitcast.44, bf16[4096,1920]{1,0:T(8,128)(2,1)} %bitcast.16.refs_1_, bf16[4096,640]{1,0:T(8,128)(2,1)} %bitcast.42, ...), custom_call_target="tpu_custom_call" | custom-call | flops 38654705664 | bytes 25165824 | tf_op jit(solution)/shard_map/grad_wq/pallas_call | solution.py:316
  483.6 0.0 copy-start.2
  483.6 0.3 collective-permute-start.5
  483.9 43.9 %grad_wkv.1 = (f32[3072,8,128]{2,1,0:T(8,128)}, f32[3072,8,128]{2,1,0:T(8,128)}, f32[1536,8,128]{2,1,0:T(8,128)}, f32[1536,8,128]{2,1,0:T(8,128)}) custom-call(s32[1]{0:T(128)} %bitcast.7.core_ref, bf16[4096,3072]{1,0:T(8,128)(2,1)} %all-gather.6.cloned.1.call-done.a_ref, bf16[4096,1920]{1,0:T(8,128)(2,1)} %bitcast.45, bf16[4096,1920]{1,0:T(8,128)(2,1)} %bitcast.16.refs_1_, ...), custom_call_target="tpu_custom_call" | custom-call | flops 25769803776 | bytes 25165824 | tf_op jit(solution)/shard_map/grad_wkv/pallas_call | solution.py:316
  527.8 0.3 collective-permute-start.6
  528.1 0.3 collective-permute-start.7
  528.4 0.0 copy-done.2
  528.4 0.6 broadcast_in_dim.10.refs_7_
  529.0 30.7 %grad_x.1 = (bf16[4,128,3072]{2,1,0:T(8,128)(2,1)}, f32[1,3072]{1,0:T(1,128)}) custom-call(s32[2]{0:T(128)} %pad_add_fusion.1.idx_ref, bf16[8,4,128,1920]{3,2,1,0:T(8,128)(2,1)} %attn_bwd.2.refs_0_, bf16[8,4,128,1920]{3,2,1,0:T(8,128)(2,1)} %collective-permute-done.3.refs_1_, bf16[8,4,128,640]{3,2,1,0:T(8,128)(2,1)} %attn_bwd.3.refs_2_, ...), custom_call_target="tpu_custom_call" | custom-call | flops 16106127360 | bytes 31457280 | tf_op jit(solution)/shard_map/grad_x/pallas_call | solution.py:450
  559.6 0.2 collective-permute-start.8
  559.9 1.0 collective-permute-done.8
  560.8 0.7 add.68
  561.5 1.5 collective-permute-start.9
  563.0 2.2 collective-permute-done.9
  565.2 0.4 collective-permute-start.10
  565.6 3.3 collective-permute-done.10
  568.9 0.6 add.70
  569.5 0.0 collective-permute-done.6.refs_4_
  569.5 0.0 collective-permute-done.7.refs_5_
  569.5 0.0 collective-permute-done.5.refs_3_
  569.5 0.0 all-gather.8.cloned.1.call-done.refs_6_
  569.6 44.1 %merge.1 = (f32[3072,24,128]{2,1,0:T(8,128)}, f32[3072,8,128]{2,1,0:T(8,128)}, f32[3072,8,128]{2,1,0:T(8,128)}, f32[3072,3072]{1,0:T(8,128)}) custom-call(s32[1]{0:T(128)} %bitcast.7.core_ref, f32[3072,24,128]{2,1,0:T(8,128)} %get-tuple-element.66.refs_0_, ...), custom_call_target="tpu_custom_call", output_to_operand_aliasing={{0}: (1, {}), {1}: (2, {}), {2}: (3, {})} | custom-call | flops 10000000000 | bytes 100000000 | tf_op jit(solution)/shard_map/merge/pallas_call | solution.py:347
  (2 shorter events, 0.0 us)
Async XLA Ops:
  7.2 132.7 %all-gather.6.cloned.1.call-start = ((), (), s32[]{:S(2)}) async-start(), calls=%async_computation.1 | async-start | bytes 28311552 | tf_op jit(solution)/shard_map/all_gather | solution.py:491
  10.5 5.7 copy-start
  15.4 253.4 %all-gather.4.cloned.1.call-start = ((), (), s32[]{:S(2)}) async-start(), calls=%async_computation | async-start | bytes 28311552 | tf_op jit(solution)/shard_map/all_gather | solution.py:492
  16.2 553.4 %all-gather.8.cloned.1.call-start = ((), (), s32[]{:S(2)}) async-start(), calls=%async_computation.2 | async-start | bytes 42467328 | tf_op jit(solution)/shard_map/all_gather | solution.py:507
  16.2 35.0 %collective-permute-start.1 = (bf16[512,3072]{1,0:T(8,128)(2,1)S(1)}, bf16[512,3072]{1,0:T(8,128)(2,1)}, u32[]{:S(2)}, u32[]{:S(2)}) collective-permute-start(bf16[512,3072]{1,0:T(8,128)(2,1)S(1)} %bitcast.41), channel_id=1, source_target_pairs={{0,1},{1,0},{2,3},{3,2},{4,5},{5,4},{6,7},{7,6},{8,9},{9,8},{10,11... | collective-permute-start | bytes 9437192 | tf_op jit(solution)/shard_map/ppermute | solution.py:483
  17.0 50.6 %collective-permute-start = (bf16[512,3072]{1,0:T(8,128)(2,1)}, bf16[512,3072]{1,0:T(8,128)(2,1)}, u32[]{:S(2)}, u32[]{:S(2)}) collective-permute-start(bf16[512,3072]{1,0:T(8,128)(2,1)} %bitcast.47), channel_id=1, source_target_pairs={{0,1},{1,0},{2,3},{3,2},{4,5},{5,4},{6,7},{7,6},{8,9},{9,8},{10,11... | collective-permute-start | bytes 9437192 | tf_op jit(solution)/shard_map/ppermute | solution.py:483
  247.8 3.4 collective-permute-start.2
  251.2 1.1 copy-start.1
  395.1 35.0 %collective-permute-start.3 = (bf16[8,4,128,1920]{3,2,1,0:T(8,128)(2,1)}, bf16[8,4,128,1920]{3,2,1,0:T(8,128)(2,1)}, u32[]{:S(2)}, u32[]{:S(2)}) collective-permute-start(bf16[8,4,128,1920]{3,2,1,0:T(8,128)(2,1)} %attn_bwd.2.refs_0_), channel_id=1, source_target_pairs={{0,1},{1,0},{2,3},{3,2},{4,5},{5,4},{6,7},{7,6},{8,9},{9,8},{10,11... | collective-permute-start | bytes 47185928 | tf_op jit(solution)/shard_map/ppermute | solution.py:483
  421.6 8.6 %collective-permute-start.4 = (bf16[8,4,128,640]{3,2,1,0:T(8,128)(2,1)}, bf16[8,4,128,640]{3,2,1,0:T(8,128)(2,1)}, u32[]{:S(2)}, u32[]{:S(2)}) collective-permute-start(bf16[8,4,128,640]{3,2,1,0:T(8,128)(2,1)} %attn_bwd.3.refs_2_), channel_id=1, source_target_pairs={{0,1},{1,0},{2,3},{3,2},{4,5},{5,4},{6,7},{7,6},{8,9},{9,8},{10,11... | collective-permute-start | bytes 15728648 | tf_op jit(solution)/shard_map/ppermute | solution.py:483
  483.6 44.8 %copy-start.2 = (bf16[3072]{0:T(1024)(128)(2,1)S(1)}, bf16[3072]{0:T(1024)(128)(2,1)}, u32[]{:S(2)}) copy-start(bf16[3072]{0:T(1024)(128)(2,1)} %param.9) | copy-start | bytes 18436
  483.6 86.0 %collective-permute-start.5 = (f32[1536,24,128]{2,1,0:T(8,128)}, f32[1536,24,128]{2,1,0:T(8,128)}, u32[]{:S(2)}, u32[]{:S(2)}) collective-permute-start(f32[1536,24,128]{2,1,0:T(8,128)} %get-tuple-element.55), channel_id=1, source_target_pairs={{0,1},{1,0},{2,3},{3,2},{4,5},{5,4},{6,7},{7,6},{8,9},{9,8},{10,11... | collective-permute-start | bytes 56623112 | tf_op jit(solution)/shard_map/ppermute | solution.py:483
  527.8 41.7 %collective-permute-start.6 = (f32[1536,8,128]{2,1,0:T(8,128)}, f32[1536,8,128]{2,1,0:T(8,128)}, u32[]{:S(2)}, u32[]{:S(2)}) collective-permute-start(f32[1536,8,128]{2,1,0:T(8,128)} %get-tuple-element.59), channel_id=1, source_target_pairs={{0,1},{1,0},{2,3},{3,2},{4,5},{5,4},{6,7},{7,6},{8,9},{9,8},{10,11... | collective-permute-start | bytes 18874376 | tf_op jit(solution)/shard_map/ppermute | solution.py:483
  528.1 41.4 %collective-permute-start.7 = (f32[1536,8,128]{2,1,0:T(8,128)}, f32[1536,8,128]{2,1,0:T(8,128)}, u32[]{:S(2)}, u32[]{:S(2)}) collective-permute-start(f32[1536,8,128]{2,1,0:T(8,128)} %get-tuple-element.60), channel_id=1, source_target_pairs={{0,1},{1,0},{2,3},{3,2},{4,5},{5,4},{6,7},{7,6},{8,9},{9,8},{10,11... | collective-permute-start | bytes 18874376 | tf_op jit(solution)/shard_map/ppermute | solution.py:483
  559.6 1.2 collective-permute-start.8
  561.5 3.7 collective-permute-start.9
  565.2 3.7 collective-permute-start.10
Sparse Core Ops, SparseCore 0:
  15.5 124.2 all-gather.5
  141.7 121.4 all-gather.3
  285.4 175.8 all-gather.7
